TPU v7x, 1024 devices: a whole 8x8x8 slice. The times are simulated.
1024 devices in a mesh: gx: 4 (over x_lo), gy: 8 (over y), gz: 32 (over z, x_hi, core).
Axes of the slice: x: 8 (x_hi: 2, x_lo: 4; x = x_hi * 4 + x_lo), y: 8, z: 8, core: 2. Of those that a mesh axis runs over, the one named last changes fastest.
Arguments:
- velocity_rhs: float32 [3, 256, 128, 512], P(None, 'gz', 'gy', 'gx'), may hold values from -48 to 48
- pressure_rhs: float32 [128, 64, 256], P('gz', 'gy', 'gx'), may hold values from -6 to 6
- viscosity: float32 [256, 128, 512], P('gz', 'gy', 'gx'), may hold values from 0.6 to 1.4
- velocity_mass: float32 [256, 128, 512], P('gz', 'gy', 'gx'), may hold values from 0.5 to 4
- pressure_scale: float32 [128, 64, 256], P('gz', 'gy', 'gx'), may hold values from 0.6 to 1.5
- velocity_bounds: float32 [2], replicated, may hold values from 4 to 72, as said below
- pressure_bounds: float32 [2], replicated, may hold values from 0.08 to 2.8, as said below
Outputs:
- velocity: float32 [3, 256, 128, 512], P(None, 'gz', 'gy', 'gx')
- pressure: float32 [128, 64, 256], P('gz', 'gy', 'gx')
Inputs may be any that keep to these rules, and one draw needn't show every extreme that they name: velocity_bounds[0] is the lower bound and velocity_bounds[1] the upper one; the upper one exceeds the largest eigenvalue of A. pressure_bounds[0] is the lower bound and pressure_bounds[1] the upper one; the upper one exceeds the largest eigenvalue of M.
All inputs are finite; a program needn't handle non-finite values.
Results may differ from a plain program's by a relative error of at most 0.00002.
Values sent between devices are 32-bit elements; how exact they have to be, the bound alone decides.
No kernel may reach another device: no remote copies, remote signals or barrier semaphores. Data moves between devices by JAX's collectives and lax.ppermute only.
A program may use at most 32 MiB of HBM per device.

v0:
```python
import jax
import jax.numpy as jnp
from jax import lax
from jax.sharding import PartitionSpec as P

SWEEPS = 2
PITERS = 2


def with_halo(value, sides, width):
    for axis, dim in sides:
        size, length = (lax.axis_size(axis), value.shape[dim])
        up = [(i, (i + 1) % size) for i in range(size - 1)]
        down = [(j, i) for i, j in up]
        last = lax.slice_in_dim(value, length - width, length, axis=dim)
        leading = lax.slice_in_dim(value, 0, width, axis=dim)
        before = lax.ppermute(last, axis, up)
        after = lax.ppermute(leading, axis, down)
        value = jnp.concatenate([before, value, after], axis=dim)
    return value


def pad_cells(field, width):
    return jnp.pad(field, [(0, 0)] * (field.ndim - 3) + [(width, width)] * 3)


def smooth_three(padded, outer_weight, centre):
    result = padded
    base = padded.ndim - 3
    for offset in range(3):
        dimension = base + offset
        length = result.shape[dimension] - 2
        result = (
            outer_weight * lax.slice_in_dim(result, 0, length, axis=dimension)
            + centre * lax.slice_in_dim(result, 1, length + 1, axis=dimension)
            + outer_weight * lax.slice_in_dim(result, 2, length + 2, axis=dimension)
        )
    return result


def chebyshev(source, operator, bounds, count):
    low_end = bounds[0]
    high_end = bounds[1]
    centre_value = (high_end + low_end) / 2.0
    spread = (high_end - low_end) / 2.0
    sigma_ratio = centre_value / spread
    factor = 1.0 / sigma_ratio
    direction = source / centre_value
    iterate = direction
    residual = source
    for repeat in range(count):
        residual = residual - operator(direction)
        factor_next = 1.0 / (2.0 * sigma_ratio - factor)
        direction = factor_next * factor * direction + 2.0 * factor_next / spread * residual
        iterate = iterate + direction
        factor = factor_next
    return iterate


def restrict_one(field, dimension):
    count = (field.shape[dimension] - 2) // 2
    return (
        0.25 * lax.slice_in_dim(field, 0, 2 * count, stride=2, axis=dimension)
        + 0.5 * lax.slice_in_dim(field, 1, 2 * count + 1, stride=2, axis=dimension)
        + 0.25 * lax.slice_in_dim(field, 2, 2 * count + 2, stride=2, axis=dimension)
    )


def divergence_restricted(padded):
    along_x = 0.5 * (padded[0, 1:-1, 1:-1, 2:] - padded[0, 1:-1, 1:-1, :-2])
    along_y = 0.5 * (padded[1, 1:-1, 2:, 1:-1] - padded[1, 1:-1, :-2, 1:-1])
    along_z = 0.5 * (padded[2, 2:, 1:-1, 1:-1] - padded[2, :-2, 1:-1, 1:-1])
    diverge = along_x + along_y + along_z
    for dimension in range(3):
        diverge = restrict_one(diverge, dimension)
    return diverge


def crop_cells(field, width):
    return field[..., width:-width, width:-width, width:-width]


def per_device(
    velocity_rhs,
    pressure_rhs,
    viscosity,
    velocity_mass,
    pressure_scale,
    velocity_bounds,
    pressure_bounds,
):
    stacked = jnp.concatenate([velocity_rhs, viscosity[None], velocity_mass[None]], axis=0)
    extended = with_halo(stacked, (("gx", 3), ("gy", 2), ("gz", 1)), SWEEPS + 2)
    source_wide = extended[:3]
    scale_wide = extended[3]
    mass_wide = extended[4]

    def apply_wide(direction):
        weighted = scale_wide * direction
        laplace = 16.0 * weighted - 2.0 * smooth_three(pad_cells(weighted, 1), 0.5, 1.0)
        return scale_wide * laplace + mass_wide * direction

    velocity_wide = chebyshev(source_wide, apply_wide, velocity_bounds, SWEEPS)
    velocity_padded = crop_cells(velocity_wide, SWEEPS)
    velocity = crop_cells(velocity_padded, 2)
    coupled = pressure_rhs - divergence_restricted(velocity_padded)
    paired = jnp.stack([coupled, pressure_scale], axis=0)
    extended = with_halo(paired, (("gx", 3), ("gy", 2), ("gz", 1)), PITERS)
    coupled_wide = extended[0]
    scale_wide = extended[1]

    def apply_pressure_wide(direction):
        weighted = scale_wide * direction
        return scale_wide * smooth_three(pad_cells(weighted, 1), 1.0 / 6.0, 2.0 / 3.0)

    pressure = crop_cells(
        chebyshev(coupled_wide, apply_pressure_wide, pressure_bounds, PITERS), PITERS
    )
    return (velocity, pressure)


def solution(mesh):
    in_specs = (
        P(None, "gz", "gy", "gx"),
        P("gz", "gy", "gx"),
        P("gz", "gy", "gx"),
        P("gz", "gy", "gx"),
        P("gz", "gy", "gx"),
        P(),
        P(),
    )
    out_specs = (P(None, "gz", "gy", "gx"), P("gz", "gy", "gx"))
    return jax.shard_map(
        per_device, mesh=mesh, in_specs=in_specs, out_specs=out_specs, check_vma=False
    )
```

profile of v0, /device:TPU:427, one launch (start us, length us, event | category | flops | bytes accessed | tf_op | source)
XLA Modules:
  0.0 109.1 jit_solution(4897271104836966971)
XLA Ops:
  0.7 1.1 pad_maximum_fusion.2
  1.9 2.2 %collective-permute-start = (f32[5,8,16,4]{3,2,1,0:T(8,128)S(1)}, f32[5,8,16,4]{3,2,1,0:T(8,128)S(1)}, u32[]{:S(2)}, u32[]{:S(2)}) collective-permute-start(f32[5,8,16,4]{3,2,1,0:T(8,128)S(1)} %get-tuple-element.13), channel_id=1, source_target_pairs={{0,256},{256,512},{512,768},{1,257},{257,513},{513,769},{2,258},{2... | collective-permute-start | bytes 30728 | tf_op jit(solution)/shard_map/ppermute | solution.py:17
  4.1 3.1 %collective-permute-start.1 = (f32[5,8,16,4]{3,2,1,0:T(8,128)S(1)}, f32[5,8,16,4]{3,2,1,0:T(8,128)S(1)}, u32[]{:S(2)}, u32[]{:S(2)}) collective-permute-start(f32[5,8,16,4]{3,2,1,0:T(8,128)S(1)} %get-tuple-element.14), channel_id=1, source_target_pairs={{256,0},{512,256},{768,512},{257,1},{513,257},{769,513},{258,2},{5... | collective-permute-start | bytes 30728 | tf_op jit(solution)/shard_map/ppermute | solution.py:18
  7.2 5.2 %collective-permute-done = f32[5,8,16,4]{3,2,1,0:T(8,128)S(1)} collective-permute-done((f32[5,8,16,4]{3,2,1,0:T(8,128)S(1)}, f32[5,8,16,4]{3,2,1,0:T(8,128)S(1)}, u32[]{:S(2)}, u32[]{:S(2)}) %collective-permute-start) | collective-permute-done | bytes 10272 | tf_op jit(solution)/shard_map/ppermute | solution.py:17
  12.4 1.9 %collective-permute-done.1 = f32[5,8,16,4]{3,2,1,0:T(8,128)S(1)} collective-permute-done((f32[5,8,16,4]{3,2,1,0:T(8,128)S(1)}, f32[5,8,16,4]{3,2,1,0:T(8,128)S(1)}, u32[]{:S(2)}, u32[]{:S(2)}) %collective-permute-start.1) | collective-permute-done | bytes 10272 | tf_op jit(solution)/shard_map/ppermute | solution.py:18
  14.7 3.3 %collective-permute-start.2 = (f32[5,8,4,136]{3,2,1,0:T(4,128)S(1)}, f32[5,8,4,136]{3,2,1,0:T(4,128)S(1)}, u32[]{:S(2)}, u32[]{:S(2)}) collective-permute-start(f32[5,8,4,136]{3,2,1,0:T(4,128)S(1)} %get-tuple-element.11), channel_id=1, source_target_pairs={{0,32},{32,64},{64,96},{96,128},{128,160},{160,192},{192,224},{1,3... | collective-permute-start | bytes 261128 | tf_op jit(solution)/shard_map/ppermute | solution.py:17
  18.0 2.0 %collective-permute-start.3 = (f32[5,8,4,136]{3,2,1,0:T(4,128)S(1)}, f32[5,8,4,136]{3,2,1,0:T(4,128)S(1)}, u32[]{:S(2)}, u32[]{:S(2)}) collective-permute-start(f32[5,8,4,136]{3,2,1,0:T(4,128)S(1)} %get-tuple-element.12), channel_id=1, source_target_pairs={{32,0},{64,32},{96,64},{128,96},{160,128},{192,160},{224,192},{33,... | collective-permute-start | bytes 261128 | tf_op jit(solution)/shard_map/ppermute | solution.py:18
  20.0 0.8 collective-permute-done.2
  20.7 4.5 %collective-permute-done.3 = f32[5,8,4,136]{3,2,1,0:T(4,128)S(1)} collective-permute-done((f32[5,8,4,136]{3,2,1,0:T(4,128)S(1)}, f32[5,8,4,136]{3,2,1,0:T(4,128)S(1)}, u32[]{:S(2)}, u32[]{:S(2)}) %collective-permute-start.3) | collective-permute-done | bytes 87072 | tf_op jit(solution)/shard_map/ppermute | solution.py:18
  25.2 0.5 pad_maximum_fusion.1
  25.8 10.7 %collective-permute-start.4 = (f32[5,4,24,136]{3,2,1,0:T(8,128)S(1)}, f32[5,4,24,136]{3,2,1,0:T(8,128)S(1)}, u32[]{:S(2)}, u32[]{:S(2)}) collective-permute-start(f32[5,4,24,136]{3,2,1,0:T(8,128)S(1)} %get-tuple-element.9), channel_id=1, source_target_pairs={{0,1},{1,2},{2,3},{3,4},{4,5},{5,6},{6,7},{7,8},{8,9},{9,10},{10,1... | collective-permute-start | bytes 783368 | tf_op jit(solution)/shard_map/ppermute | solution.py:17
  36.4 1.9 %collective-permute-start.5 = (f32[5,4,24,136]{3,2,1,0:T(8,128)S(1)}, f32[5,4,24,136]{3,2,1,0:T(8,128)S(1)}, u32[]{:S(2)}, u32[]{:S(2)}) collective-permute-start(f32[5,4,24,136]{3,2,1,0:T(8,128)S(1)} %get-tuple-element.10), channel_id=1, source_target_pairs={{1,0},{2,1},{3,2},{4,3},{5,4},{6,5},{7,6},{8,7},{9,8},{10,9},{11,1... | collective-permute-start | bytes 783368 | tf_op jit(solution)/shard_map/ppermute | solution.py:18
  38.4 0.6 fusion.61
  41.8 14.5 %collective-permute-done.4 = f32[5,4,24,136]{3,2,1,0:T(8,128)S(1)} collective-permute-done((f32[5,4,24,136]{3,2,1,0:T(8,128)S(1)}, f32[5,4,24,136]{3,2,1,0:T(8,128)S(1)}, u32[]{:S(2)}, u32[]{:S(2)}) %collective-permute-start.4) | collective-permute-done | bytes 261152 | tf_op jit(solution)/shard_map/ppermute | solution.py:17
  56.2 4.6 %collective-permute-done.5 = f32[5,4,24,136]{3,2,1,0:T(8,128)S(1)} collective-permute-done((f32[5,4,24,136]{3,2,1,0:T(8,128)S(1)}, f32[5,4,24,136]{3,2,1,0:T(8,128)S(1)}, u32[]{:S(2)}, u32[]{:S(2)}) %collective-permute-start.5) | collective-permute-done | bytes 261152 | tf_op jit(solution)/shard_map/ppermute | solution.py:18
  60.9 0.5 pad_maximum_fusion
  61.5 1.2 %fusion.2 = f32[3,16,26,138]{3,2,1,0:T(8,128)S(1)} fusion(f32[3,16,24,136]{3,2,1,0:T(8,128)S(1)} %broadcast_multiply_fusion), kind=kLoop, calls=%fused_computation.9 | loop fusion | flops 688896 | bytes 1315584 | tf_op jit(solution)/shard_map/add | solution.py:34
  63.1 0.9 fusion.25
  64.0 1.2 %fusion.6 = f32[3,16,26,138]{3,2,1,0:T(8,128)S(1)} fusion(f32[3,16,24,136]{3,2,1,0:T(8,128)S(1)} %fusion.25), kind=kLoop, calls=%fused_computation.13 | loop fusion | flops 688896 | bytes 1315584 | tf_op jit(solution)/shard_map/add | solution.py:34
  65.5 1.7 %fusion.16 = f32[3,16,24,136]{3,2,1,0:T(8,128)S(1)} fusion(f32[3,16,24,138]{3,2,1,0:T(8,128)S(1)} %fusion.17, f32[]{:T(128)S(6)} %div.79, f32[]{:T(128)S(6)} %mul.301, f32[16,24,136]{2,1,0:T(8,128)S(1)} %get-tuple-element.7, f32[16,24,136]{2,1,0:T(8,128)S(1)} %get-tuple-element.8, f32[]{:T(128)S(6)} %div.77, f32[]{:T(128)S(6)} %mul.280, ...), kind=kLoop, calls=%fused_computation.24 | loop fusion | flops 5170176 | bytes 5431316 | tf_op jit(solution)/shard_map/add | solution.py:55
  69.0 3.2 %collective-permute-start.6 = (f32[2,4,8,2]{3,2,1,0:T(8,128)S(1)}, f32[2,4,8,2]{3,2,1,0:T(8,128)S(1)}, u32[]{:S(2)}, u32[]{:S(2)}) collective-permute-start(f32[2,4,8,2]{3,2,1,0:T(8,128)S(1)} %get-tuple-element.21), channel_id=1, source_target_pairs={{0,256},{256,512},{512,768},{1,257},{257,513},{513,769},{2,258},{2... | collective-permute-start | bytes 1544 | tf_op jit(solution)/shard_map/ppermute | solution.py:17
  72.2 2.1 %collective-permute-start.7 = (f32[2,4,8,2]{3,2,1,0:T(8,128)S(1)}, f32[2,4,8,2]{3,2,1,0:T(8,128)S(1)}, u32[]{:S(2)}, u32[]{:S(2)}) collective-permute-start(f32[2,4,8,2]{3,2,1,0:T(8,128)S(1)} %get-tuple-element.22), channel_id=1, source_target_pairs={{256,0},{512,256},{768,512},{257,1},{513,257},{769,513},{258,2},{5... | collective-permute-start | bytes 1544 | tf_op jit(solution)/shard_map/ppermute | solution.py:18
  74.3 2.5 %collective-permute-done.7 = f32[2,4,8,2]{3,2,1,0:T(8,128)S(1)} collective-permute-done((f32[2,4,8,2]{3,2,1,0:T(8,128)S(1)}, f32[2,4,8,2]{3,2,1,0:T(8,128)S(1)}, u32[]{:S(2)}, u32[]{:S(2)}) %collective-permute-start.7) | collective-permute-done | bytes 544 | tf_op jit(solution)/shard_map/ppermute | solution.py:18
  77.0 4.9 %collective-permute-start.8 = (f32[2,4,2,68]{3,2,1,0:T(2,128)S(1)}, f32[2,4,2,68]{3,2,1,0:T(2,128)S(1)}, u32[]{:S(2)}, u32[]{:S(2)}) collective-permute-start(f32[2,4,2,68]{3,2,1,0:T(2,128)S(1)} %get-tuple-element.15), channel_id=1, source_target_pairs={{0,32},{32,64},{64,96},{96,128},{128,160},{160,192},{192,224},{1,3... | collective-permute-start | bytes 13064 | tf_op jit(solution)/shard_map/ppermute | solution.py:17
  81.8 1.9 %collective-permute-start.9 = (f32[2,4,2,68]{3,2,1,0:T(2,128)S(1)}, f32[2,4,2,68]{3,2,1,0:T(2,128)S(1)}, u32[]{:S(2)}, u32[]{:S(2)}) collective-permute-start(f32[2,4,2,68]{3,2,1,0:T(2,128)S(1)} %get-tuple-element.16), channel_id=1, source_target_pairs={{32,0},{64,32},{96,64},{128,96},{160,128},{192,160},{224,192},{33,... | collective-permute-start | bytes 13064 | tf_op jit(solution)/shard_map/ppermute | solution.py:18
  83.8 2.5 %collective-permute-done.9 = f32[2,4,2,68]{3,2,1,0:T(2,128)S(1)} collective-permute-done((f32[2,4,2,68]{3,2,1,0:T(2,128)S(1)}, f32[2,4,2,68]{3,2,1,0:T(2,128)S(1)}, u32[]{:S(2)}, u32[]{:S(2)}) %collective-permute-start.9) | collective-permute-done | bytes 4384 | tf_op jit(solution)/shard_map/ppermute | solution.py:18
  86.3 10.1 %collective-permute-start.10 = (f32[2,2,12,68]{3,2,1,0:T(8,128)S(1)}, f32[2,2,12,68]{3,2,1,0:T(8,128)S(1)}, u32[]{:S(2)}, u32[]{:S(2)}) collective-permute-start(f32[2,2,12,68]{3,2,1,0:T(8,128)S(1)} %get-tuple-element.19), channel_id=1, source_target_pairs={{0,1},{1,2},{2,3},{3,4},{4,5},{5,6},{6,7},{7,8},{8,9},{9,10},{10,1... | collective-permute-start | bytes 39176 | tf_op jit(solution)/shard_map/ppermute | solution.py:17
  96.4 1.9 %collective-permute-start.11 = (f32[2,2,12,68]{3,2,1,0:T(8,128)S(1)}, f32[2,2,12,68]{3,2,1,0:T(8,128)S(1)}, u32[]{:S(2)}, u32[]{:S(2)}) collective-permute-start(f32[2,2,12,68]{3,2,1,0:T(8,128)S(1)} %get-tuple-element.20), channel_id=1, source_target_pairs={{1,0},{2,1},{3,2},{4,3},{5,4},{6,5},{7,6},{8,7},{9,8},{10,9},{11,1... | collective-permute-start | bytes 39176 | tf_op jit(solution)/shard_map/ppermute | solution.py:18
  98.4 0.6 fusion.60
  101.8 0.8 slice.323
  102.6 5.1 %collective-permute-done.11 = f32[2,2,12,68]{3,2,1,0:T(8,128)S(1)} collective-permute-done((f32[2,2,12,68]{3,2,1,0:T(8,128)S(1)}, f32[2,2,12,68]{3,2,1,0:T(8,128)S(1)}, u32[]{:S(2)}, u32[]{:S(2)}) %collective-permute-start.11) | collective-permute-done | bytes 13088 | tf_op jit(solution)/shard_map/ppermute | solution.py:18
  108.4 0.7 fusion.50
  (47 shorter events, 3.9 us)
Async XLA Ops:
  0.6 13.7 %copy-start.2 = (f32[8,16,128]{2,1,0:T(8,128)S(1)}, f32[8,16,128]{2,1,0:T(8,128)}, u32[]{:S(2)}) copy-start(f32[8,16,128]{2,1,0:T(8,128)} %param.9) | copy-start | bytes 196612
  0.6 13.7 %copy-start.1 = (f32[8,16,128]{2,1,0:T(8,128)S(1)}, f32[8,16,128]{2,1,0:T(8,128)}, u32[]{:S(2)}) copy-start(f32[8,16,128]{2,1,0:T(8,128)} %param.10) | copy-start | bytes 196612
  0.7 13.7 %copy-start = (f32[3,8,16,128]{3,2,1,0:T(8,128)S(1)}, f32[3,8,16,128]{3,2,1,0:T(8,128)}, u32[]{:S(2)}) copy-start(f32[3,8,16,128]{3,2,1,0:T(8,128)} %param.7) | copy-start | bytes 589828
  1.9 10.5 %collective-permute-start = (f32[5,8,16,4]{3,2,1,0:T(8,128)S(1)}, f32[5,8,16,4]{3,2,1,0:T(8,128)S(1)}, u32[]{:S(2)}, u32[]{:S(2)}) collective-permute-start(f32[5,8,16,4]{3,2,1,0:T(8,128)S(1)} %get-tuple-element.13), channel_id=1, source_target_pairs={{0,256},{256,512},{512,768},{1,257},{257,513},{513,769},{2,258},{2... | collective-permute-start | bytes 30728 | tf_op jit(solution)/shard_map/ppermute | solution.py:17
  4.1 10.2 %collective-permute-start.1 = (f32[5,8,16,4]{3,2,1,0:T(8,128)S(1)}, f32[5,8,16,4]{3,2,1,0:T(8,128)S(1)}, u32[]{:S(2)}, u32[]{:S(2)}) collective-permute-start(f32[5,8,16,4]{3,2,1,0:T(8,128)S(1)} %get-tuple-element.14), channel_id=1, source_target_pairs={{256,0},{512,256},{768,512},{257,1},{513,257},{769,513},{258,2},{5... | collective-permute-start | bytes 30728 | tf_op jit(solution)/shard_map/ppermute | solution.py:18
  14.7 6.1 %collective-permute-start.2 = (f32[5,8,4,136]{3,2,1,0:T(4,128)S(1)}, f32[5,8,4,136]{3,2,1,0:T(4,128)S(1)}, u32[]{:S(2)}, u32[]{:S(2)}) collective-permute-start(f32[5,8,4,136]{3,2,1,0:T(4,128)S(1)} %get-tuple-element.11), channel_id=1, source_target_pairs={{0,32},{32,64},{64,96},{96,128},{128,160},{160,192},{192,224},{1,3... | collective-permute-start | bytes 261128 | tf_op jit(solution)/shard_map/ppermute | solution.py:17
  18.0 7.2 %collective-permute-start.3 = (f32[5,8,4,136]{3,2,1,0:T(4,128)S(1)}, f32[5,8,4,136]{3,2,1,0:T(4,128)S(1)}, u32[]{:S(2)}, u32[]{:S(2)}) collective-permute-start(f32[5,8,4,136]{3,2,1,0:T(4,128)S(1)} %get-tuple-element.12), channel_id=1, source_target_pairs={{32,0},{64,32},{96,64},{128,96},{160,128},{192,160},{224,192},{33,... | collective-permute-start | bytes 261128 | tf_op jit(solution)/shard_map/ppermute | solution.py:18
  25.7 12.7 %copy-start.5 = (f32[2]{0:T(128)S(1)}, f32[2]{0:T(128)}, u32[]{:S(2)}) copy-start(f32[2]{0:T(128)} %param.12) | copy-start | bytes 28
  25.8 30.5 %collective-permute-start.4 = (f32[5,4,24,136]{3,2,1,0:T(8,128)S(1)}, f32[5,4,24,136]{3,2,1,0:T(8,128)S(1)}, u32[]{:S(2)}, u32[]{:S(2)}) collective-permute-start(f32[5,4,24,136]{3,2,1,0:T(8,128)S(1)} %get-tuple-element.9), channel_id=1, source_target_pairs={{0,1},{1,2},{2,3},{3,4},{4,5},{5,6},{6,7},{7,8},{8,9},{9,10},{10,1... | collective-permute-start | bytes 783368 | tf_op jit(solution)/shard_map/ppermute | solution.py:17
  36.4 24.4 %collective-permute-start.5 = (f32[5,4,24,136]{3,2,1,0:T(8,128)S(1)}, f32[5,4,24,136]{3,2,1,0:T(8,128)S(1)}, u32[]{:S(2)}, u32[]{:S(2)}) collective-permute-start(f32[5,4,24,136]{3,2,1,0:T(8,128)S(1)} %get-tuple-element.10), channel_id=1, source_target_pairs={{1,0},{2,1},{3,2},{4,3},{5,4},{6,5},{7,6},{8,7},{9,8},{10,9},{11,1... | collective-permute-start | bytes 783368 | tf_op jit(solution)/shard_map/ppermute | solution.py:18
  67.3 1.6 %copy-start.4 = (f32[4,8,64]{2,1,0:T(8,128)S(1)}, f32[4,8,64]{2,1,0:T(8,128)}, u32[]{:S(2)}) copy-start(f32[4,8,64]{2,1,0:T(8,128)} %param.8) | copy-start | bytes 24580
  67.3 1.7 %copy-start.3 = (f32[4,8,64]{2,1,0:T(8,128)S(1)}, f32[4,8,64]{2,1,0:T(8,128)}, u32[]{:S(2)}) copy-start(f32[4,8,64]{2,1,0:T(8,128)} %param.11) | copy-start | bytes 24580
  67.3 31.1 %copy-start.6 = (f32[2]{0:T(128)S(1)}, f32[2]{0:T(128)}, u32[]{:S(2)}) copy-start(f32[2]{0:T(128)} %param.13) | copy-start | bytes 28
  69.0 5.3 %collective-permute-start.6 = (f32[2,4,8,2]{3,2,1,0:T(8,128)S(1)}, f32[2,4,8,2]{3,2,1,0:T(8,128)S(1)}, u32[]{:S(2)}, u32[]{:S(2)}) collective-permute-start(f32[2,4,8,2]{3,2,1,0:T(8,128)S(1)} %get-tuple-element.21), channel_id=1, source_target_pairs={{0,256},{256,512},{512,768},{1,257},{257,513},{513,769},{2,258},{2... | collective-permute-start | bytes 1544 | tf_op jit(solution)/shard_map/ppermute | solution.py:17
  72.2 4.7 %collective-permute-start.7 = (f32[2,4,8,2]{3,2,1,0:T(8,128)S(1)}, f32[2,4,8,2]{3,2,1,0:T(8,128)S(1)}, u32[]{:S(2)}, u32[]{:S(2)}) collective-permute-start(f32[2,4,8,2]{3,2,1,0:T(8,128)S(1)} %get-tuple-element.22), channel_id=1, source_target_pairs={{256,0},{512,256},{768,512},{257,1},{513,257},{769,513},{258,2},{5... | collective-permute-start | bytes 1544 | tf_op jit(solution)/shard_map/ppermute | solution.py:18
  77.0 6.8 %collective-permute-start.8 = (f32[2,4,2,68]{3,2,1,0:T(2,128)S(1)}, f32[2,4,2,68]{3,2,1,0:T(2,128)S(1)}, u32[]{:S(2)}, u32[]{:S(2)}) collective-permute-start(f32[2,4,2,68]{3,2,1,0:T(2,128)S(1)} %get-tuple-element.15), channel_id=1, source_target_pairs={{0,32},{32,64},{64,96},{96,128},{128,160},{160,192},{192,224},{1,3... | collective-permute-start | bytes 13064 | tf_op jit(solution)/shard_map/ppermute | solution.py:17
  81.8 4.4 %collective-permute-start.9 = (f32[2,4,2,68]{3,2,1,0:T(2,128)S(1)}, f32[2,4,2,68]{3,2,1,0:T(2,128)S(1)}, u32[]{:S(2)}, u32[]{:S(2)}) collective-permute-start(f32[2,4,2,68]{3,2,1,0:T(2,128)S(1)} %get-tuple-element.16), channel_id=1, source_target_pairs={{32,0},{64,32},{96,64},{128,96},{160,128},{192,160},{224,192},{33,... | collective-permute-start | bytes 13064 | tf_op jit(solution)/shard_map/ppermute | solution.py:18
  86.3 16.2 %collective-permute-start.10 = (f32[2,2,12,68]{3,2,1,0:T(8,128)S(1)}, f32[2,2,12,68]{3,2,1,0:T(8,128)S(1)}, u32[]{:S(2)}, u32[]{:S(2)}) collective-permute-start(f32[2,2,12,68]{3,2,1,0:T(8,128)S(1)} %get-tuple-element.19), channel_id=1, source_target_pairs={{0,1},{1,2},{2,3},{3,4},{4,5},{5,6},{6,7},{7,8},{8,9},{9,10},{10,1... | collective-permute-start | bytes 39176 | tf_op jit(solution)/shard_map/ppermute | solution.py:17
  96.4 11.3 %collective-permute-start.11 = (f32[2,2,12,68]{3,2,1,0:T(8,128)S(1)}, f32[2,2,12,68]{3,2,1,0:T(8,128)S(1)}, u32[]{:S(2)}, u32[]{:S(2)}) collective-permute-start(f32[2,2,12,68]{3,2,1,0:T(8,128)S(1)} %get-tuple-element.20), channel_id=1, source_target_pairs={{1,0},{2,1},{3,2},{4,3},{5,4},{6,5},{7,6},{8,7},{9,8},{10,9},{11,1... | collective-permute-start | bytes 39176 | tf_op jit(solution)/shard_map/ppermute | solution.py:18
where the time goes:
time: 110 us; the launch traced here: 109 us
  starting transfers between devices  47.2 us (43%)
  waiting for transfers between devices  41.5 us (38%)
  other arithmetic  10.2 us (9%)
  between operations  6.75 us (6%)
  local copies, waits for them, and re-layouts  3.38 us (3%)
    ppermute x6, starting transfers between devices, with_halo(): before = lax.ppermute(last, axis, up)  34.3 us
    ppermute x6, waiting for transfers between devices, with_halo(): after = lax.ppermute(leading, axis, down)  21.1 us
    ppermute x6, waiting for transfers between devices, with_halo(): before = lax.ppermute(last, axis, up)  20.4 us
    ppermute x6, starting transfers between devices, with_halo(): after = lax.ppermute(leading, axis, down)  12.9 us
    add x9, other arithmetic, smooth_three(): outer_weight * lax.slice_in_dim(result, 0, length, axis=dimension)  3.46 us
    add x2, other arithmetic, chebyshev(): iterate = iterate + direction  2.45 us
  transfers between devices with their start and end apart: 12, of which 9 were waited for; matrix products, arithmetic and copies ran while one was open for 2% of the time, Pallas kernels for 0%

commit v1 on v0

v1 whole, which is shorter than its diff:
```python
import jax
import jax.numpy as jnp
import ml_dtypes
import numpy as np
from jax import lax
from jax.experimental import pallas as pl
from jax.experimental.pallas import tpu as pltpu
from jax.sharding import PartitionSpec as P

Z, Y, X = 8, 16, 128
PZ, PY, PX = 4, 8, 64
F32 = jnp.float32

ZW = Z + 4
PLANES = 4 * ZW + Z + 2
S0, M0 = 3 * ZW, 4 * ZW
VT = 4 * PLANES
TILES = VT + 24
PACKED = TILES // 16


def parity(axis):
    return lax.rem(lax.axis_index(axis), 2)


def swap_neighbours(axis, first, second):
    size = lax.axis_size(axis)
    even = [(i, i ^ 1) for i in range(size)]
    odd = [(i, ((i + 1) ^ 1) - 1) for i in range(1, size - 1)]
    return lax.ppermute(first, axis, even), lax.ppermute(second, axis, odd)


def both_neighbours(axis, to_above, to_below):
    size = lax.axis_size(axis)
    up = [(i, i + 1) for i in range(size - 1)]
    down = [(i + 1, i) for i in range(size - 1)]
    return lax.ppermute(to_above, axis, up), lax.ppermute(to_below, axis, down)


def call(body, outs, scratch=(), smem=()):
    def run(*args):
        specs = [
            pl.BlockSpec(memory_space=pltpu.SMEM if i in smem else pltpu.VMEM)
            for i in range(len(args))
        ]
        return pl.pallas_call(
            body,
            in_specs=specs,
            out_specs=[pl.BlockSpec(memory_space=pltpu.VMEM) for _ in outs],
            out_shape=[jax.ShapeDtypeStruct(o, F32) for o in outs],
            scratch_shapes=list(scratch),
            name=body.__name__,
        )(*args)

    return run


def pack_z(rhs, visc, mass, msg_even, msg_odd):
    par = parity("gz")
    for out, up in ((msg_even, 1 - par), (msg_odd, par)):
        z0 = 6 * up
        for c in range(3):
            for j in range(2):
                out[2 * c + j] = rhs[c, z0 + j]
        for j in range(2):
            out[6 + j] = visc[z0 + j]
        out[8] = mass[7 * up]


def pack_y(rhs, visc, mass, got_even, got_odd, pscale, prhs, own, up, down, pt):
    even = parity("gz") == 0

    def put(plane, value):
        own[plane] = value
        down[plane] = value[:8]
        up[plane] = value[8:]

    def halo(i):
        a, b = got_even[i], got_odd[i]
        return jnp.where(even, b, a), jnp.where(even, a, b)

    for c in range(3):
        for j in range(2):
            below, above = halo(2 * c + j)
            put(c * ZW + j, below)
            put(c * ZW + 10 + j, above)
        for z in range(Z):
            put(c * ZW + 2 + z, rhs[c, z])
    for j in range(2):
        below, above = halo(6 + j)
        put(S0 + j, below)
        put(S0 + 10 + j, above)
    below, above = halo(8)
    put(M0, below)
    put(M0 + 9, above)
    for z in range(Z):
        put(S0 + 2 + z, visc[z])
        put(M0 + 1 + z, mass[z])
    for k in range(PZ):
        tile = jnp.concatenate([pscale[k], prhs[k]], axis=1)
        pt[k] = tile
        up[PLANES + k] = tile
        down[PLANES + k] = tile


def lanes():
    return lax.broadcasted_iota(jnp.int32, (8, X), 1)


def pack_x(own, below, above, pt, main, up, down):
    lane = lanes()
    for p in range(PLANES):
        main[4 * p] = below[p]
        main[4 * p + 1] = own[p, :8]
        main[4 * p + 2] = own[p, 8:]
        main[4 * p + 3] = above[p]
    for k in range(PZ):
        for t, src in enumerate((below[PLANES + k], pt[k], above[PLANES + k])):
            turned = pltpu.roll(src, 64, axis=1)
            main[VT + 3 * k + t] = jnp.where(lane < 64, src, turned)
            main[VT + 12 + 3 * k + t] = jnp.where(lane < 64, turned, src)
    low = (lane & 15) < 8

    def group(j):
        acc = pltpu.roll(main[8 * j], 8, axis=1)
        for k in range(1, 8):
            acc = jnp.where(lane >= 16 * k, pltpu.roll(main[8 * j + k], (8 + 16 * k) % X, axis=1), acc)
        return acc

    for i in range(PACKED):
        a, b = group(2 * i), group(2 * i + 1)
        up[i] = jnp.where(low, a, pltpu.roll(b, 8, axis=1))
        down[i] = jnp.where(low, pltpu.roll(a, 120, axis=1), b)


def coefficients(bounds):
    low = jnp.full((8, X), bounds[0], F32)
    high = jnp.full((8, X), bounds[1], F32)
    centre = (high + low) / 2.0
    spread = (high - low) / 2.0
    sigma = centre / spread
    rho0 = 1.0 / sigma
    rho1 = 1.0 / (2.0 * sigma - rho0)
    rho2 = 1.0 / (2.0 * sigma - rho1)
    return 1.0 / centre, rho1 * rho0, 2.0 * rho1 / spread, rho2 * rho1, 2.0 * rho2 / spread


def tall(coef, rows):
    return jnp.concatenate([coef] * (rows // 8), axis=0)


def restriction():
    table = np.zeros((4, X, X), np.float32)
    for half in range(2):
        for l in range(X):
            x = l if half == 0 else (X + l if l < 8 else l - X)
            if half and 8 <= l < 120:
                continue
            for node in range(-2, PX + 2):
                o = x - 2 * node
                table[half, l, node + 2] = {-1: 0.25, 0: 0.5, 1: 0.25}.get(o, 0.0)
                table[2 + half, l, node + 2] = {-2: -0.125, -1: -0.25, 1: 0.25, 2: 0.125}.get(o, 0.0)
    return table.reshape(4 * X, X).astype(ml_dtypes.bfloat16)


SMOOTH_Z = {-1: (), 0: ((0, 0.5), (1, 0.25)), 4: ((7, 0.25),)}
DERIVE_Z = {
    -1: ((0, 0.125),),
    0: ((1, 0.25), (2, 0.125)),
    1: ((0, -0.125), (1, -0.25), (3, 0.25), (4, 0.125)),
    2: ((2, -0.125), (3, -0.25), (5, 0.25), (6, 0.125)),
    3: ((4, -0.125), (5, -0.25), (7, 0.25)),
    4: ((6, -0.125), (7, -0.25)),
}
for _k in (1, 2, 3):
    SMOOTH_Z[_k] = ((2 * _k - 1, 0.25), (2 * _k, 0.5), (2 * _k + 1, 0.25))


def velocity_step(
    main, from_below, from_above, table, bounds, vel, coupled, pscale, msg_even, msg_odd,
    halo, w, d, r, u, t, g, q, ptmp,
):
    lane = lanes()
    low = (lane & 15) < 8
    edge = (lane < 8) | (lane >= 120)
    for i in range(PACKED):
        a, b = from_below[i], from_above[i]
        pair = (
            jnp.where(low, a, pltpu.roll(b, 8, axis=1)),
            jnp.where(low, pltpu.roll(a, 120, axis=1), b),
        )
        for e in range(2):
            for k in range(8):
                halo[16 * i + 8 * e + k] = jnp.where(
                    edge, pltpu.roll(pair[e], (120 - 16 * k) % X, axis=1), 0.0
                )

    inv, a1, g1, a2, g2 = (tall(v, 32) for v in coefficients(bounds))
    lane32 = lax.broadcasted_iota(jnp.int32, (32, X), 1)
    first, last = lane32 == 0, lane32 == X - 1
    t[...] = jnp.zeros_like(t)

    def planes(ref, p):
        return ref[pl.ds(4 * p, 4)].reshape(32, X)

    def smooth(src, z):
        out = []
        for h in range(2):
            v = src[h, z] + 0.5 * (src[h, z - 1] + src[h, z + 1])
            t[h, 8:40] = v
            out.append(v + 0.5 * (t[h, 7:39] + t[h, 9:41]))
        m, s = out
        ml, sl = pltpu.roll(m, 1, axis=1), pltpu.roll(s, 1, axis=1)
        mr, sr = pltpu.roll(m, X - 1, axis=1), pltpu.roll(s, X - 1, axis=1)
        return (
            m + 0.5 * (jnp.where(first, sl, ml) + jnp.where(last, sr, mr)),
            s + 0.5 * (jnp.where(first, ml, sl) + jnp.where(last, mr, sr)),
        )

    def component(c, _):
        base = c * ZW

        def weight(z, _):
            for h, src in enumerate((main, halo)):
                w[0, h, z] = planes(src, S0 + z) * (planes(src, base + z) * inv)
            return 0

        lax.fori_loop(0, ZW, weight, 0)

        def sweep1(z, _):
            s = smooth(w.at[0], z)
            for h, src in enumerate((main, halo)):
                b = planes(src, base + z)
                visc = planes(src, S0 + z)
                d0 = b * inv
                res = b - (visc * (16.0 * w[0, h, z] - 2.0 * s[h]) + planes(src, M0 + z - 1) * d0)
                d1 = a1 * d0 + g1 * res
                r[h, z] = res
                d[h, z] = d1
                w[1, h, z] = visc * d1
            return 0

        lax.fori_loop(1, ZW - 1, sweep1, 0)

        def sweep2(z, _):
            s = smooth(w.at[1], z)
            for h, src in enumerate((main, halo)):
                d1 = d[h, z]
                res = r[h, z] - (
                    planes(src, S0 + z) * (16.0 * w[1, h, z] - 2.0 * s[h]) + planes(src, M0 + z - 1) * d1
                )
                total = planes(src, base + z) * inv + d1 + (a2 * d1 + g2 * res)
                u[c, h, z - 2] = total
                if h == 0:
                    vel[c, z - 2] = total[8:24]
            return 0

        lax.fori_loop(2, ZW - 2, sweep2, 0)
        return 0

    lax.fori_loop(0, 3, component, 0)

    q[...] = jnp.zeros_like(q)
    for node in range(-1, 5):
        rows = slice(16 * (node + 1), 16 * (node + 1) + 12)

        def along_z(c, h, weights):
            acc = None
            for z, f in weights:
                term = f * u[c, h, z]
                acc = term if acc is None else acc + term
            return acc

        def at(k, start):
            return g[k, pl.ds(start, 12, stride=2), :]

        for h in range(2):
            cols = slice(X * h, X * (h + 1))
            g[2] = along_z(2, h, DERIVE_Z[node])
            total = 0.25 * (at(2, 3) + at(2, 5)) + 0.5 * at(2, 4)
            if SMOOTH_Z[node]:
                g[0] = along_z(0, h, SMOOTH_Z[node])
                g[1] = along_z(1, h, SMOOTH_Z[node])
                total = total + 0.25 * (at(1, 5) - at(1, 3)) + 0.125 * (at(1, 6) - at(1, 2))
                q[rows, 2 * X + X * h : 3 * X + X * h] = 0.25 * (at(0, 3) + at(0, 5)) + 0.5 * at(0, 4)
            q[rows, cols] = total

    full = q[...]
    hi = full.astype(jnp.bfloat16)
    rest = full - hi.astype(F32)
    mid = rest.astype(jnp.bfloat16)
    lo = (rest - mid.astype(F32)).astype(jnp.bfloat16)
    weights = table[...]
    div = sum(
        lax.dot_general(v, weights, (((1,), (0,)), ((), ())), preferred_element_type=F32)
        for v in (lo, mid, hi)
    )

    def nodes(base, k):
        for i in range(3):
            own = pltpu.roll(main[base + 3 * k + i], 2, axis=1)
            side = halo[base + 3 * k + i]
            left = pltpu.roll(side, 2, axis=1)
            right = pltpu.roll(side, 66, axis=1)
            value = jnp.where(lane < 66, own, jnp.where(lane < 68, right, 0.0))
            ptmp[8 * i : 8 * i + 8] = jnp.where(lane < 2, left, value)
        return ptmp[6:18]

    coupled[...] = -div.reshape(6, 16, X)
    pscale[...] = jnp.zeros_like(pscale)
    for k in range(PZ):
        pscale[k, :12] = nodes(VT, k)
        coupled[k + 1, :12] = nodes(VT + 12, k) - div[16 * (k + 1) : 16 * (k + 1) + 12]
    par = parity("gz")
    for out, up in ((msg_even, 1 - par), (msg_odd, par)):
        for j in range(3):
            out[j] = coupled[3 * up + j]
        for j in range(2):
            out[3 + j] = pscale[2 * up + j]


def pressure_step(coupled, pscale, got_even, got_odd, bounds, out):
    even = parity("gz") == 0
    below, above = [], []
    for i in range(5):
        a, b = got_even[i], got_odd[i]
        below.append(jnp.where(even, b, a))
        above.append(jnp.where(even, a, b))
    b = [
        below[0], below[1] + coupled[0], below[2] + coupled[1], coupled[2], coupled[3],
        coupled[4] + above[0], coupled[5] + above[1], above[2],
    ]
    s = [below[3], below[4], pscale[0], pscale[1], pscale[2], pscale[3], above[3], above[4]]
    inv, a1, g1, a2, g2 = (tall(v, 16) for v in coefficients(bounds))

    def operator(w, z):
        v = (1.0 / 6.0) * (w[z - 1] + w[z + 1]) + (2.0 / 3.0) * w[z]
        v = (1.0 / 6.0) * (pltpu.roll(v, 1, axis=0) + pltpu.roll(v, 15, axis=0)) + (2.0 / 3.0) * v
        v = (1.0 / 6.0) * (pltpu.roll(v, 1, axis=1) + pltpu.roll(v, X - 1, axis=1)) + (2.0 / 3.0) * v
        return s[z] * v

    d0 = [v * inv for v in b]
    w = [x * y for x, y in zip(s, d0)]
    r1, d1, w1 = [None] * 8, [None] * 8, [None] * 8
    for z in range(1, 7):
        r1[z] = b[z] - operator(w, z)
        d1[z] = a1 * d0[z] + g1 * r1[z]
        w1[z] = s[z] * d1[z]
    for z in range(2, 6):
        res = r1[z] - operator(w1, z)
        total = d0[z] + d1[z] + (a2 * d1[z] + g2 * res)
        total = pltpu.roll(pltpu.roll(total, 14, axis=0), X - 2, axis=1)
        out[z - 2] = total[:PY, :PX]


def per_device(rhs, prhs, visc, mass, pscale, vbounds, pbounds):
    plane = (Y, X)
    msg_even, msg_odd = call(pack_z, [(9, *plane)] * 2)(rhs, visc, mass)
    got_even, got_odd = swap_neighbours("gz", msg_even, msg_odd)
    own, up, down, pt = call(
        pack_y, [(PLANES, *plane), (PLANES + PZ, 8, X), (PLANES + PZ, 8, X), (PZ, 8, X)]
    )(rhs, visc, mass, got_even, got_odd, pscale, prhs)
    below, above = both_neighbours("gy", up, down)
    main, up, down = call(pack_x, [(TILES, 8, X), (PACKED, 8, X), (PACKED, 8, X)])(
        own, below, above, pt
    )
    below, above = both_neighbours("gx", up, down)
    vel, coupled, scale, msg_even, msg_odd = call(
        velocity_step,
        [(3, Z, Y, X), (6, *plane), (PZ, *plane), (5, *plane), (5, *plane)],
        scratch=[
            pltpu.VMEM((TILES, 8, X), F32),
            pltpu.VMEM((2, 2, ZW, 32, X), F32),
            pltpu.VMEM((2, ZW, 32, X), F32),
            pltpu.VMEM((2, ZW, 32, X), F32),
            pltpu.VMEM((3, 2, Z, 32, X), F32),
            pltpu.VMEM((2, 48, X), F32),
            pltpu.VMEM((3, 32, X), F32),
            pltpu.VMEM((96, 4 * X), F32),
            pltpu.VMEM((24, X), F32),
        ],
        smem=(4,),
    )(main, below, above, jnp.asarray(restriction()), vbounds)
    got_even, got_odd = swap_neighbours("gz", msg_even, msg_odd)
    (pressure,) = call(pressure_step, [(PZ, PY, PX)], smem=(4,))(
        coupled, scale, got_even, got_odd, pbounds
    )
    return vel, pressure


def solution(mesh):
    block = P("gz", "gy", "gx")
    field = P(None, "gz", "gy", "gx")
    return jax.shard_map(
        per_device,
        mesh=mesh,
        in_specs=(field, block, block, block, block, P(), P()),
        out_specs=(field, block),
        check_vma=False,
    )
```

time: 110 us -> 75.1 us (0.68)
  the two profiles are of different devices: /device:TPU:427 before, /device:TPU:562 now
where the time goes in v1:
time: 75.1 us; the launch traced here: 74.7 us
  waiting for transfers between devices  27.7 us (37%)
  starting transfers between devices  25.3 us (34%)
  Pallas kernels  18.4 us (25%)
  local copies, waits for them, and re-layouts  2.58 us (3%)
    pallas_call x5, Pallas kernels, run(): pl.pallas_call(body, in_specs=specs, out_specs=[pl.BlockSpec(memory_space...  18.4 us
    ppermute x4, waiting for transfers between devices, swap_neighbours(): return (lax.ppermute(first, axis, even), lax.ppermute(second, axis, odd))  15.6 us
    ppermute x4, starting transfers between devices, swap_neighbours(): return (lax.ppermute(first, axis, even), lax.ppermute(second, axis, odd))  11.7 us
    ppermute x2, starting transfers between devices, both_neighbours(): lax.ppermute(to_above, axis, up)  9.83 us
    ppermute x2, waiting for transfers between devices, both_neighbours(): lax.ppermute(to_below, axis, down)  9.53 us
    ppermute x2, starting transfers between devices, both_neighbours(): lax.ppermute(to_below, axis, down)  3.84 us
    ppermute x2, waiting for transfers between devices, both_neighbours(): lax.ppermute(to_above, axis, up)  2.58 us
    unnamed x16, local copies, waits for them, and re-layouts  2.58 us
  transfers between devices with their start and end apart: 8, of which 6 were waited for; matrix products, arithmetic and copies ran while one was open for 0% of the time, Pallas kernels for 0%

profile of v1, /device:TPU:562, one launch (start us, length us, event | category | flops | bytes accessed | tf_op | source)
XLA Modules:
  0.0 74.7 jit_solution(3637519230725496742)
XLA Ops:
  0.6 1.6 %pack_z.1 = (f32[9,16,128]{2,1,0:T(8,128)}, f32[9,16,128]{2,1,0:T(8,128)}) custom-call(f32[3,8,16,128]{3,2,1,0:T(8,128)} %rhs.3, f32[8,16,128]{2,1,0:T(8,128)} %visc.3, f32[8,16,128]{2,1,0:T(8,128)} %mass.3), custom_call_target="tpu_custom_call" | custom-call | tf_op jit(solution)/shard_map/pack_z/pallas_call | solution.py:46
  2.3 1.9 %collective-permute-start = (f32[9,16,128]{2,1,0:T(8,128)}, f32[9,16,128]{2,1,0:T(8,128)S(1)}, u32[]{:S(2)}, u32[]{:S(2)}) collective-permute-start(f32[9,16,128]{2,1,0:T(8,128)} %get-tuple-element.16), channel_id=1, source_target_pairs={{0,1},{1,0},{2,3},{3,2},{4,5},{5,4},{6,7},{7,6},{8,9},{9,8},{10,11... | collective-permute-start | bytes 221192 | tf_op jit(solution)/shard_map/ppermute | solution.py:30
  4.2 4.8 %collective-permute-start.1 = (f32[9,16,128]{2,1,0:T(8,128)}, f32[9,16,128]{2,1,0:T(8,128)S(1)}, u32[]{:S(2)}, u32[]{:S(2)}) collective-permute-start(f32[9,16,128]{2,1,0:T(8,128)} %get-tuple-element.17), channel_id=1, source_target_pairs={{1,2},{2,1},{3,4},{4,3},{5,6},{6,5},{7,8},{8,7},{9,10},{10,9},{11,... | collective-permute-start | bytes 221192 | tf_op jit(solution)/shard_map/ppermute | solution.py:30
  9.0 0.0 collective-permute-done.got_even
  9.0 0.0 copy-start.2
  9.0 7.1 %collective-permute-done.1.got_odd = f32[9,16,128]{2,1,0:T(8,128)S(1)} collective-permute-done((f32[9,16,128]{2,1,0:T(8,128)}, f32[9,16,128]{2,1,0:T(8,128)S(1)}, u32[]{:S(2)}, u32[]{:S(2)}) %collective-permute-start.1) | collective-permute-done | bytes 73760 | tf_op jit(solution)/shard_map/ppermute | solution.py:30
  16.1 0.0 copy-done.2
  16.1 0.0 copy-start.3
  16.1 0.6 copy-done.3
  16.7 2.1 %pack_y.1 = (f32[58,16,128]{2,1,0:T(8,128)}, f32[62,8,128]{2,1,0:T(8,128)}, f32[62,8,128]{2,1,0:T(8,128)}, f32[4,8,128]{2,1,0:T(8,128)}) custom-call(f32[3,8,16,128]{3,2,1,0:T(8,128)} %rhs.3, f32[8,16,128]{2,1,0:T(8,128)} %visc.3, f32[8,16,128]{2,1,0:T(8,128)} %mass.3, f32[9,16,128]{2,1,0:T(8,128)} %copy-done.2, f32[9,16,128]{2,1,0:T(8,128)} %copy-done.3, ...), custom_call_target="tpu_custom_call" | custom-call | tf_op jit(solution)/shard_map/pack_y/pallas_call | solution.py:46
  18.8 4.8 %collective-permute-start.2 = (f32[62,8,128]{2,1,0:T(8,128)}, f32[62,8,128]{2,1,0:T(8,128)S(1)}, u32[]{:S(2)}, u32[]{:S(2)}) collective-permute-start(f32[62,8,128]{2,1,0:T(8,128)} %get-tuple-element.19), channel_id=1, source_target_pairs={{0,32},{32,64},{64,96},{96,128},{128,160},{160,192},{192,224},{1,3... | collective-permute-start | bytes 761864 | tf_op jit(solution)/shard_map/ppermute | solution.py:37
  23.6 1.9 %collective-permute-start.3 = (f32[62,8,128]{2,1,0:T(8,128)}, f32[62,8,128]{2,1,0:T(8,128)S(1)}, u32[]{:S(2)}, u32[]{:S(2)}) collective-permute-start(f32[62,8,128]{2,1,0:T(8,128)} %get-tuple-element.20), channel_id=1, source_target_pairs={{32,0},{64,32},{96,64},{128,96},{160,128},{192,160},{224,192},{33,... | collective-permute-start | bytes 761864 | tf_op jit(solution)/shard_map/ppermute | solution.py:37
  25.5 2.3 %collective-permute-done.2.below = f32[62,8,128]{2,1,0:T(8,128)S(1)} collective-permute-done((f32[62,8,128]{2,1,0:T(8,128)}, f32[62,8,128]{2,1,0:T(8,128)S(1)}, u32[]{:S(2)}, u32[]{:S(2)}) %collective-permute-start.2) | collective-permute-done | bytes 253984 | tf_op jit(solution)/shard_map/ppermute | solution.py:37
  27.9 5.4 %collective-permute-done.3.above = f32[62,8,128]{2,1,0:T(8,128)S(1)} collective-permute-done((f32[62,8,128]{2,1,0:T(8,128)}, f32[62,8,128]{2,1,0:T(8,128)S(1)}, u32[]{:S(2)}, u32[]{:S(2)}) %collective-permute-start.3) | collective-permute-done | bytes 253984 | tf_op jit(solution)/shard_map/ppermute | solution.py:37
  33.2 0.0 copy-done
  33.2 0.7 copy-done.1
  33.9 3.1 %pack_x.1 = (f32[256,8,128]{2,1,0:T(8,128)}, f32[16,8,128]{2,1,0:T(8,128)}, f32[16,8,128]{2,1,0:T(8,128)}) custom-call(f32[58,16,128]{2,1,0:T(8,128)} %get-tuple-element.18.own, f32[62,8,128]{2,1,0:T(8,128)} %copy-done, f32[62,8,128]{2,1,0:T(8,128)} %copy-done.1, f32[4,8,128]{2,1,0:T(8,128)} %get-tuple-element.21.pt), custom_call_target="tpu_custom_call" | custom-call | tf_op jit(solution)/shard_map/pack_x/pallas_call | solution.py:46
  37.0 5.0 %collective-permute-start.4 = (f32[16,8,128]{2,1,0:T(8,128)}, f32[16,8,128]{2,1,0:T(8,128)S(1)}, u32[]{:S(2)}, u32[]{:S(2)}) collective-permute-start(f32[16,8,128]{2,1,0:T(8,128)} %get-tuple-element.23), channel_id=1, source_target_pairs={{0,256},{256,512},{512,768},{1,257},{257,513},{513,769},{2,258},{2... | collective-permute-start | bytes 196616 | tf_op jit(solution)/shard_map/ppermute | solution.py:37
  42.1 1.9 %collective-permute-start.5 = (f32[16,8,128]{2,1,0:T(8,128)}, f32[16,8,128]{2,1,0:T(8,128)S(1)}, u32[]{:S(2)}, u32[]{:S(2)}) collective-permute-start(f32[16,8,128]{2,1,0:T(8,128)} %get-tuple-element.24), channel_id=1, source_target_pairs={{256,0},{512,256},{768,512},{257,1},{513,257},{769,513},{258,2},{5... | collective-permute-start | bytes 196616 | tf_op jit(solution)/shard_map/ppermute | solution.py:37
  44.0 0.3 collective-permute-done.4.from_below
  44.3 4.2 %collective-permute-done.5.from_above = f32[16,8,128]{2,1,0:T(8,128)S(1)} collective-permute-done((f32[16,8,128]{2,1,0:T(8,128)}, f32[16,8,128]{2,1,0:T(8,128)S(1)}, u32[]{:S(2)}, u32[]{:S(2)}) %collective-permute-start.5) | collective-permute-done | bytes 65568 | tf_op jit(solution)/shard_map/ppermute | solution.py:37
  48.4 0.0 copy-done.4
  48.4 0.6 copy-done.5
  49.1 9.8 %velocity_step.1 = (f32[3,8,16,128]{3,2,1,0:T(8,128)}, f32[6,16,128]{2,1,0:T(8,128)}, f32[4,16,128]{2,1,0:T(8,128)}, f32[5,16,128]{2,1,0:T(8,128)}, f32[5,16,128]{2,1,0:T(8,128)}) custom-call(f32[256,8,128]{2,1,0:T(8,128)} %get-tuple-element.22.main, f32[16,8,128]{2,1,0:T(8,128)} %copy-done.4, f32[16,8,128]{2,1,0:T(8,128)} %copy-done.5, ...), custom_call_target="tpu_custom_call" | custom-call | tf_op jit(solution)/shard_map/velocity_step/pallas_call | solution.py:46
  58.9 1.9 %collective-permute-start.6 = (f32[5,16,128]{2,1,0:T(8,128)}, f32[5,16,128]{2,1,0:T(8,128)S(1)}, u32[]{:S(2)}, u32[]{:S(2)}) collective-permute-start(f32[5,16,128]{2,1,0:T(8,128)} %get-tuple-element.28), channel_id=1, source_target_pairs={{0,1},{1,0},{2,3},{3,2},{4,5},{5,4},{6,7},{7,6},{8,9},{9,8},{10,11... | collective-permute-start | bytes 122888 | tf_op jit(solution)/shard_map/ppermute | solution.py:30
  60.8 3.1 %collective-permute-start.7 = (f32[5,16,128]{2,1,0:T(8,128)}, f32[5,16,128]{2,1,0:T(8,128)S(1)}, u32[]{:S(2)}, u32[]{:S(2)}) collective-permute-start(f32[5,16,128]{2,1,0:T(8,128)} %get-tuple-element.29), channel_id=1, source_target_pairs={{1,2},{2,1},{3,4},{4,3},{5,6},{6,5},{7,8},{8,7},{9,10},{10,9},{11,... | collective-permute-start | bytes 122888 | tf_op jit(solution)/shard_map/ppermute | solution.py:30
  63.9 0.0 collective-permute-done.6.got_even
  63.9 0.0 copy-start.6
  63.9 8.5 %collective-permute-done.7.got_odd = f32[5,16,128]{2,1,0:T(8,128)S(1)} collective-permute-done((f32[5,16,128]{2,1,0:T(8,128)}, f32[5,16,128]{2,1,0:T(8,128)S(1)}, u32[]{:S(2)}, u32[]{:S(2)}) %collective-permute-start.7) | collective-permute-done | bytes 40992 | tf_op jit(solution)/shard_map/ppermute | solution.py:30
  72.4 0.0 copy-done.6
  72.4 0.6 copy-done.7
  73.0 1.7 %pressure_step.1 = f32[4,8,64]{2,1,0:T(8,128)} custom-call(f32[6,16,128]{2,1,0:T(8,128)} %get-tuple-element.26.coupled, f32[4,16,128]{2,1,0:T(8,128)} %get-tuple-element.27.pscale, f32[5,16,128]{2,1,0:T(8,128)} %copy-done.6, f32[5,16,128]{2,1,0:T(8,128)} %copy-done.7, f32[2]{0:T(128)} %bounds.3), custom_call_target="tpu_custom_call" | custom-call | tf_op jit(solution)/shard_map/pressure_step/pallas_call | solution.py:46
  (5 shorter events, 0.0 us)
Async XLA Ops:
  2.3 6.7 %collective-permute-start = (f32[9,16,128]{2,1,0:T(8,128)}, f32[9,16,128]{2,1,0:T(8,128)S(1)}, u32[]{:S(2)}, u32[]{:S(2)}) collective-permute-start(f32[9,16,128]{2,1,0:T(8,128)} %get-tuple-element.16), channel_id=1, source_target_pairs={{0,1},{1,0},{2,3},{3,2},{4,5},{5,4},{6,7},{7,6},{8,9},{9,8},{10,11... | collective-permute-start | bytes 221192 | tf_op jit(solution)/shard_map/ppermute | solution.py:30
  4.2 11.9 %collective-permute-start.1 = (f32[9,16,128]{2,1,0:T(8,128)}, f32[9,16,128]{2,1,0:T(8,128)S(1)}, u32[]{:S(2)}, u32[]{:S(2)}) collective-permute-start(f32[9,16,128]{2,1,0:T(8,128)} %get-tuple-element.17), channel_id=1, source_target_pairs={{1,2},{2,1},{3,4},{4,3},{5,6},{6,5},{7,8},{8,7},{9,10},{10,9},{11,... | collective-permute-start | bytes 221192 | tf_op jit(solution)/shard_map/ppermute | solution.py:30
  9.0 7.1 %copy-start.2 = (f32[9,16,128]{2,1,0:T(8,128)}, f32[9,16,128]{2,1,0:T(8,128)S(1)}, u32[]{:S(2)}) copy-start(f32[9,16,128]{2,1,0:T(8,128)S(1)} %collective-permute-done.got_even) | copy-start | bytes 221188
  16.1 0.6 copy-start.3
  18.8 9.0 %collective-permute-start.2 = (f32[62,8,128]{2,1,0:T(8,128)}, f32[62,8,128]{2,1,0:T(8,128)S(1)}, u32[]{:S(2)}, u32[]{:S(2)}) collective-permute-start(f32[62,8,128]{2,1,0:T(8,128)} %get-tuple-element.19), channel_id=1, source_target_pairs={{0,32},{32,64},{64,96},{96,128},{128,160},{160,192},{192,224},{1,3... | collective-permute-start | bytes 761864 | tf_op jit(solution)/shard_map/ppermute | solution.py:37
  23.6 9.6 %collective-permute-start.3 = (f32[62,8,128]{2,1,0:T(8,128)}, f32[62,8,128]{2,1,0:T(8,128)S(1)}, u32[]{:S(2)}, u32[]{:S(2)}) collective-permute-start(f32[62,8,128]{2,1,0:T(8,128)} %get-tuple-element.20), channel_id=1, source_target_pairs={{32,0},{64,32},{96,64},{128,96},{160,128},{192,160},{224,192},{33,... | collective-permute-start | bytes 761864 | tf_op jit(solution)/shard_map/ppermute | solution.py:37
  27.9 5.4 %copy-start = (f32[62,8,128]{2,1,0:T(8,128)}, f32[62,8,128]{2,1,0:T(8,128)S(1)}, u32[]{:S(2)}) copy-start(f32[62,8,128]{2,1,0:T(8,128)S(1)} %collective-permute-done.2.below) | copy-start | bytes 761860
  33.2 0.7 copy-start.1
  37.0 7.2 %collective-permute-start.4 = (f32[16,8,128]{2,1,0:T(8,128)}, f32[16,8,128]{2,1,0:T(8,128)S(1)}, u32[]{:S(2)}, u32[]{:S(2)}) collective-permute-start(f32[16,8,128]{2,1,0:T(8,128)} %get-tuple-element.23), channel_id=1, source_target_pairs={{0,256},{256,512},{512,768},{1,257},{257,513},{513,769},{2,258},{2... | collective-permute-start | bytes 196616 | tf_op jit(solution)/shard_map/ppermute | solution.py:37
  42.1 6.4 %collective-permute-start.5 = (f32[16,8,128]{2,1,0:T(8,128)}, f32[16,8,128]{2,1,0:T(8,128)S(1)}, u32[]{:S(2)}, u32[]{:S(2)}) collective-permute-start(f32[16,8,128]{2,1,0:T(8,128)} %get-tuple-element.24), channel_id=1, source_target_pairs={{256,0},{512,256},{768,512},{257,1},{513,257},{769,513},{258,2},{5... | collective-permute-start | bytes 196616 | tf_op jit(solution)/shard_map/ppermute | solution.py:37
  44.3 4.2 %copy-start.4 = (f32[16,8,128]{2,1,0:T(8,128)}, f32[16,8,128]{2,1,0:T(8,128)S(1)}, u32[]{:S(2)}) copy-start(f32[16,8,128]{2,1,0:T(8,128)S(1)} %collective-permute-done.4.from_below) | copy-start | bytes 196612
  48.4 0.6 copy-start.5
  58.9 5.0 %collective-permute-start.6 = (f32[5,16,128]{2,1,0:T(8,128)}, f32[5,16,128]{2,1,0:T(8,128)S(1)}, u32[]{:S(2)}, u32[]{:S(2)}) collective-permute-start(f32[5,16,128]{2,1,0:T(8,128)} %get-tuple-element.28), channel_id=1, source_target_pairs={{0,1},{1,0},{2,3},{3,2},{4,5},{5,4},{6,7},{7,6},{8,9},{9,8},{10,11... | collective-permute-start | bytes 122888 | tf_op jit(solution)/shard_map/ppermute | solution.py:30
  60.8 11.5 %collective-permute-start.7 = (f32[5,16,128]{2,1,0:T(8,128)}, f32[5,16,128]{2,1,0:T(8,128)S(1)}, u32[]{:S(2)}, u32[]{:S(2)}) collective-permute-start(f32[5,16,128]{2,1,0:T(8,128)} %get-tuple-element.29), channel_id=1, source_target_pairs={{1,2},{2,1},{3,4},{4,3},{5,6},{6,5},{7,8},{8,7},{9,10},{10,9},{11,... | collective-permute-start | bytes 122888 | tf_op jit(solution)/shard_map/ppermute | solution.py:30
  63.9 8.5 %copy-start.6 = (f32[5,16,128]{2,1,0:T(8,128)}, f32[5,16,128]{2,1,0:T(8,128)S(1)}, u32[]{:S(2)}) copy-start(f32[5,16,128]{2,1,0:T(8,128)S(1)} %collective-permute-done.6.got_even) | copy-start | bytes 122884
  72.4 0.6 copy-start.7

commit v2 on v1

--- a/solution.py
+++ b/solution.py
@@ -10,6 +10,7 @@
 Z, Y, X = 8, 16, 128
 PZ, PY, PX = 4, 8, 64
 F32 = jnp.float32
+VMEM_LIMIT = 16 * 2**20
 
 ZW = Z + 4
 PLANES = 4 * ZW + Z + 2
@@ -50,6 +51,7 @@
             out_shape=[jax.ShapeDtypeStruct(o, F32) for o in outs],
             scratch_shapes=list(scratch),
             name=body.__name__,
+            compiler_params=pltpu.CompilerParams(vmem_limit_bytes=VMEM_LIMIT),
         )(*args)
 
     return run

time: 75.1 us -> 68.3 us (0.909)
  Pallas kernels: 18.4 us -> 11.5 us
  waiting for transfers between devices: 27.7 us -> 26.8 us
    pallas_call x5, Pallas kernels: 18.4 us -> 11.5 us  [run(): pl.pallas_call(body, in_specs=specs, out_specs=[pl.BlockSpec(memory_space...]
  transfers between devices with their start and end apart: 8 -> 8, of which waited for: 6 -> 5; matrix products, arithmetic and copies ran while one was open for 0% -> 0% of each run, Pallas kernels for 0% -> 0%
where the time goes in v2:
time: 68.3 us; the launch traced here: 67.9 us
  waiting for transfers between devices  26.8 us (39%)
  starting transfers between devices  25.5 us (37%)
  Pallas kernels  11.5 us (17%)
  local copies, waits for them, and re-layouts  3.27 us (5%)
  between operations  0.76 us (1%)
    ppermute x4, waiting for transfers between devices, swap_neighbours(): return (lax.ppermute(first, axis, even), lax.ppermute(second, axis, odd))  15.2 us
    ppermute x4, starting transfers between devices, swap_neighbours(): return (lax.ppermute(first, axis, even), lax.ppermute(second, axis, odd))  11.8 us
    pallas_call x5, Pallas kernels, run(): pl.pallas_call(body, in_specs=specs, out_specs=[pl.BlockSpec(memory_space...  11.5 us
    ppermute x2, starting transfers between devices, both_neighbours(): lax.ppermute(to_above, axis, up)  9.86 us
    ppermute x2, waiting for transfers between devices, both_neighbours(): lax.ppermute(to_below, axis, down)  9.69 us
    ppermute x2, starting transfers between devices, both_neighbours(): lax.ppermute(to_below, axis, down)  3.84 us
    unnamed x16, local copies, waits for them, and re-layouts  3.27 us
    ppermute x2, waiting for transfers between devices, both_neighbours(): lax.ppermute(to_above, axis, up)  1.99 us
  transfers between devices with their start and end apart: 8, of which 5 were waited for; matrix products, arithmetic and copies ran while one was open for 0% of the time, Pallas kernels for 0%

profile of v2, /device:TPU:562, one launch (start us, length us, event | category | flops | bytes accessed | tf_op | source)
XLA Modules:
  0.0 67.9 jit_solution(4781727753656042027)
XLA Ops:
  0.6 0.0 copy-start
  0.6 0.9 %copy-done = f32[3,8,16,128]{3,2,1,0:T(8,128)S(1)} copy-done((f32[3,8,16,128]{3,2,1,0:T(8,128)S(1)}, f32[3,8,16,128]{3,2,1,0:T(8,128)}, u32[]{:S(2)}) %copy-start) | copy-done | bytes 196632
  1.6 0.0 copy-start.1
  1.6 0.8 %copy-done.1 = f32[8,16,128]{2,1,0:T(8,128)S(1)} copy-done((f32[8,16,128]{2,1,0:T(8,128)S(1)}, f32[8,16,128]{2,1,0:T(8,128)}, u32[]{:S(2)}) %copy-start.1) | copy-done | bytes 65560
  2.4 0.0 copy-start.2
  2.4 0.8 %copy-done.2 = f32[8,16,128]{2,1,0:T(8,128)S(1)} copy-done((f32[8,16,128]{2,1,0:T(8,128)S(1)}, f32[8,16,128]{2,1,0:T(8,128)}, u32[]{:S(2)}) %copy-start.2) | copy-done | bytes 65560
  3.3 2.1 %collective-permute-start = (f32[9,16,128]{2,1,0:T(8,128)S(1)}, f32[9,16,128]{2,1,0:T(8,128)S(1)}, u32[]{:S(2)}, u32[]{:S(2)}) collective-permute-start(f32[9,16,128]{2,1,0:T(8,128)S(1)} %get-tuple-element.16), channel_id=1, source_target_pairs={{0,1},{1,0},{2,3},{3,2},{4,5},{5,4},{6,7},{7,6},{8,9},{9,8},{10,11... | collective-permute-start | bytes 221192 | tf_op jit(solution)/shard_map/ppermute | solution.py:31
  5.3 4.8 %collective-permute-start.1 = (f32[9,16,128]{2,1,0:T(8,128)S(1)}, f32[9,16,128]{2,1,0:T(8,128)S(1)}, u32[]{:S(2)}, u32[]{:S(2)}) collective-permute-start(f32[9,16,128]{2,1,0:T(8,128)S(1)} %get-tuple-element.17), channel_id=1, source_target_pairs={{1,2},{2,1},{3,4},{4,3},{5,6},{6,5},{7,8},{8,7},{9,10},{10,9},{11,... | collective-permute-start | bytes 221192 | tf_op jit(solution)/shard_map/ppermute | solution.py:31
  10.1 0.0 collective-permute-done.got_even
  10.1 6.9 %collective-permute-done.1.got_odd = f32[9,16,128]{2,1,0:T(8,128)S(1)} collective-permute-done((f32[9,16,128]{2,1,0:T(8,128)S(1)}, f32[9,16,128]{2,1,0:T(8,128)S(1)}, u32[]{:S(2)}, u32[]{:S(2)}) %collective-permute-start.1) | collective-permute-done | bytes 73760 | tf_op jit(solution)/shard_map/ppermute | solution.py:31
  17.0 0.0 copy-done.4
  17.0 0.0 copy-done.5
  17.0 0.1 pack_y.1
  17.1 4.8 %collective-permute-start.2 = (f32[62,8,128]{2,1,0:T(8,128)S(1)}, f32[62,8,128]{2,1,0:T(8,128)S(1)}, u32[]{:S(2)}, u32[]{:S(2)}) collective-permute-start(f32[62,8,128]{2,1,0:T(8,128)S(1)} %get-tuple-element.19), channel_id=1, source_target_pairs={{0,32},{32,64},{64,96},{96,128},{128,160},{160,192},{192,224},{1,3... | collective-permute-start | bytes 761864 | tf_op jit(solution)/shard_map/ppermute | solution.py:38
  21.9 1.9 %collective-permute-start.3 = (f32[62,8,128]{2,1,0:T(8,128)S(1)}, f32[62,8,128]{2,1,0:T(8,128)S(1)}, u32[]{:S(2)}, u32[]{:S(2)}) collective-permute-start(f32[62,8,128]{2,1,0:T(8,128)S(1)} %get-tuple-element.20), channel_id=1, source_target_pairs={{32,0},{64,32},{96,64},{128,96},{160,128},{192,160},{224,192},{33,... | collective-permute-start | bytes 761864 | tf_op jit(solution)/shard_map/ppermute | solution.py:38
  23.8 2.0 %collective-permute-done.2.below = f32[62,8,128]{2,1,0:T(8,128)S(1)} collective-permute-done((f32[62,8,128]{2,1,0:T(8,128)S(1)}, f32[62,8,128]{2,1,0:T(8,128)S(1)}, u32[]{:S(2)}, u32[]{:S(2)}) %collective-permute-start.2) | collective-permute-done | bytes 253984 | tf_op jit(solution)/shard_map/ppermute | solution.py:38
  25.8 5.5 %collective-permute-done.3.above = f32[62,8,128]{2,1,0:T(8,128)S(1)} collective-permute-done((f32[62,8,128]{2,1,0:T(8,128)S(1)}, f32[62,8,128]{2,1,0:T(8,128)S(1)}, u32[]{:S(2)}, u32[]{:S(2)}) %collective-permute-start.3) | collective-permute-done | bytes 253984 | tf_op jit(solution)/shard_map/ppermute | solution.py:38
  31.3 1.1 %pack_x.1 = (f32[256,8,128]{2,1,0:T(8,128)S(1)}, f32[16,8,128]{2,1,0:T(8,128)S(1)}, f32[16,8,128]{2,1,0:T(8,128)S(1)}) custom-call(f32[58,16,128]{2,1,0:T(8,128)S(1)} %get-tuple-element.18.own, f32[62,8,128]{2,1,0:T(8,128)S(1)} %collective-permute-done.2.below, f32[62,8,128]{2,1,0:T(8,128)S(1)} %collective-permute-done.3.above, ...), custom_call_target="tpu_custom_call" | custom-call | tf_op jit(solution)/shard_map/pack_x/pallas_call | solution.py:47
  32.4 5.0 %collective-permute-start.4 = (f32[16,8,128]{2,1,0:T(8,128)S(1)}, f32[16,8,128]{2,1,0:T(8,128)S(1)}, u32[]{:S(2)}, u32[]{:S(2)}) collective-permute-start(f32[16,8,128]{2,1,0:T(8,128)S(1)} %get-tuple-element.23), channel_id=1, source_target_pairs={{0,256},{256,512},{512,768},{1,257},{257,513},{513,769},{2,258},{2... | collective-permute-start | bytes 196616 | tf_op jit(solution)/shard_map/ppermute | solution.py:38
  37.4 0.0 copy-start.6
  37.5 1.9 %collective-permute-start.5 = (f32[16,8,128]{2,1,0:T(8,128)S(1)}, f32[16,8,128]{2,1,0:T(8,128)S(1)}, u32[]{:S(2)}, u32[]{:S(2)}) collective-permute-start(f32[16,8,128]{2,1,0:T(8,128)S(1)} %get-tuple-element.24), channel_id=1, source_target_pairs={{256,0},{512,256},{768,512},{257,1},{513,257},{769,513},{258,2},{5... | collective-permute-start | bytes 196616 | tf_op jit(solution)/shard_map/ppermute | solution.py:38
  39.4 0.0 collective-permute-done.4.from_below
  39.4 4.2 %collective-permute-done.5.from_above = f32[16,8,128]{2,1,0:T(8,128)S(1)} collective-permute-done((f32[16,8,128]{2,1,0:T(8,128)S(1)}, f32[16,8,128]{2,1,0:T(8,128)S(1)}, u32[]{:S(2)}, u32[]{:S(2)}) %collective-permute-start.5) | collective-permute-done | bytes 65568 | tf_op jit(solution)/shard_map/ppermute | solution.py:38
  43.6 0.0 copy-done.3
  43.6 0.0 copy-done.6
  43.6 8.9 %velocity_step.1 = (f32[3,8,16,128]{3,2,1,0:T(8,128)}, f32[6,16,128]{2,1,0:T(8,128)S(1)}, f32[4,16,128]{2,1,0:T(8,128)S(1)}, f32[5,16,128]{2,1,0:T(8,128)S(1)}, f32[5,16,128]{2,1,0:T(8,128)S(1)}) custom-call(f32[256,8,128]{2,1,0:T(8,128)S(1)} %get-tuple-element.22.main, f32[16,8,128]{2,1,0:T(8,128)S(1)} %collective-permute-done.4.from_below, ...), custom_call_target="tpu_custom_call" | custom-call | tf_op jit(solution)/shard_map/velocity_step/pallas_call | solution.py:47
  52.5 1.9 %collective-permute-start.6 = (f32[5,16,128]{2,1,0:T(8,128)S(1)}, f32[5,16,128]{2,1,0:T(8,128)S(1)}, u32[]{:S(2)}, u32[]{:S(2)}) collective-permute-start(f32[5,16,128]{2,1,0:T(8,128)S(1)} %get-tuple-element.28), channel_id=1, source_target_pairs={{0,1},{1,0},{2,3},{3,2},{4,5},{5,4},{6,7},{7,6},{8,9},{9,8},{10,11... | collective-permute-start | bytes 122888 | tf_op jit(solution)/shard_map/ppermute | solution.py:31
  54.5 3.1 %collective-permute-start.7 = (f32[5,16,128]{2,1,0:T(8,128)S(1)}, f32[5,16,128]{2,1,0:T(8,128)S(1)}, u32[]{:S(2)}, u32[]{:S(2)}) collective-permute-start(f32[5,16,128]{2,1,0:T(8,128)S(1)} %get-tuple-element.29), channel_id=1, source_target_pairs={{1,2},{2,1},{3,4},{4,3},{5,6},{6,5},{7,8},{8,7},{9,10},{10,9},{11,... | collective-permute-start | bytes 122888 | tf_op jit(solution)/shard_map/ppermute | solution.py:31
  57.5 0.0 collective-permute-done.6.got_even
  57.5 8.3 %collective-permute-done.7.got_odd = f32[5,16,128]{2,1,0:T(8,128)S(1)} collective-permute-done((f32[5,16,128]{2,1,0:T(8,128)S(1)}, f32[5,16,128]{2,1,0:T(8,128)S(1)}, u32[]{:S(2)}, u32[]{:S(2)}) %collective-permute-start.7) | collective-permute-done | bytes 40992 | tf_op jit(solution)/shard_map/ppermute | solution.py:31
  65.8 0.7 copy-done.7
  66.5 1.4 %pressure_step.1 = f32[4,8,64]{2,1,0:T(8,128)} custom-call(f32[6,16,128]{2,1,0:T(8,128)S(1)} %get-tuple-element.26.coupled, f32[4,16,128]{2,1,0:T(8,128)S(1)} %get-tuple-element.27.pscale, f32[5,16,128]{2,1,0:T(8,128)S(1)} %collective-permute-done.6.got_even, f32[5,16,128]{2,1,0:T(8,128)S(1)} %collective-permute-done.7.got_odd, f32[2]{0:T(128)S(1)} %copy-done.7), custom_call_target="tpu_custom_call" | custom-call | tf_op jit(solution)/shard_map/pressure_step/pallas_call | solution.py:47
  (5 shorter events, 0.0 us)
Async XLA Ops:
  0.6 0.9 %copy-start = (f32[3,8,16,128]{3,2,1,0:T(8,128)S(1)}, f32[3,8,16,128]{3,2,1,0:T(8,128)}, u32[]{:S(2)}) copy-start(f32[3,8,16,128]{3,2,1,0:T(8,128)} %rhs.3) | copy-start | bytes 589828
  1.6 0.8 %copy-start.1 = (f32[8,16,128]{2,1,0:T(8,128)S(1)}, f32[8,16,128]{2,1,0:T(8,128)}, u32[]{:S(2)}) copy-start(f32[8,16,128]{2,1,0:T(8,128)} %visc.3) | copy-start | bytes 196612
  2.4 0.8 %copy-start.2 = (f32[8,16,128]{2,1,0:T(8,128)S(1)}, f32[8,16,128]{2,1,0:T(8,128)}, u32[]{:S(2)}) copy-start(f32[8,16,128]{2,1,0:T(8,128)} %mass.3) | copy-start | bytes 196612
  3.2 13.8 %copy-start.4 = (f32[4,8,64]{2,1,0:T(8,128)S(1)}, f32[4,8,64]{2,1,0:T(8,128)}, u32[]{:S(2)}) copy-start(f32[4,8,64]{2,1,0:T(8,128)} %pscale.1) | copy-start | bytes 24580
  3.2 13.8 %copy-start.5 = (f32[4,8,64]{2,1,0:T(8,128)S(1)}, f32[4,8,64]{2,1,0:T(8,128)}, u32[]{:S(2)}) copy-start(f32[4,8,64]{2,1,0:T(8,128)} %prhs.1) | copy-start | bytes 24580
  3.3 6.8 %collective-permute-start = (f32[9,16,128]{2,1,0:T(8,128)S(1)}, f32[9,16,128]{2,1,0:T(8,128)S(1)}, u32[]{:S(2)}, u32[]{:S(2)}) collective-permute-start(f32[9,16,128]{2,1,0:T(8,128)S(1)} %get-tuple-element.16), channel_id=1, source_target_pairs={{0,1},{1,0},{2,3},{3,2},{4,5},{5,4},{6,7},{7,6},{8,9},{9,8},{10,11... | collective-permute-start | bytes 221192 | tf_op jit(solution)/shard_map/ppermute | solution.py:31
  5.3 11.7 %collective-permute-start.1 = (f32[9,16,128]{2,1,0:T(8,128)S(1)}, f32[9,16,128]{2,1,0:T(8,128)S(1)}, u32[]{:S(2)}, u32[]{:S(2)}) collective-permute-start(f32[9,16,128]{2,1,0:T(8,128)S(1)} %get-tuple-element.17), channel_id=1, source_target_pairs={{1,2},{2,1},{3,4},{4,3},{5,6},{6,5},{7,8},{8,7},{9,10},{10,9},{11,... | collective-permute-start | bytes 221192 | tf_op jit(solution)/shard_map/ppermute | solution.py:31
  17.1 8.7 %collective-permute-start.2 = (f32[62,8,128]{2,1,0:T(8,128)S(1)}, f32[62,8,128]{2,1,0:T(8,128)S(1)}, u32[]{:S(2)}, u32[]{:S(2)}) collective-permute-start(f32[62,8,128]{2,1,0:T(8,128)S(1)} %get-tuple-element.19), channel_id=1, source_target_pairs={{0,32},{32,64},{64,96},{96,128},{128,160},{160,192},{192,224},{1,3... | collective-permute-start | bytes 761864 | tf_op jit(solution)/shard_map/ppermute | solution.py:38
  21.9 9.4 %collective-permute-start.3 = (f32[62,8,128]{2,1,0:T(8,128)S(1)}, f32[62,8,128]{2,1,0:T(8,128)S(1)}, u32[]{:S(2)}, u32[]{:S(2)}) collective-permute-start(f32[62,8,128]{2,1,0:T(8,128)S(1)} %get-tuple-element.20), channel_id=1, source_target_pairs={{32,0},{64,32},{96,64},{128,96},{160,128},{192,160},{224,192},{33,... | collective-permute-start | bytes 761864 | tf_op jit(solution)/shard_map/ppermute | solution.py:38
  31.3 12.3 %copy-start.3 = (bf16[512,128]{1,0:T(8,128)(2,1)S(1)}, bf16[512,128]{1,0:T(8,128)(2,1)}, u32[]{:S(2)}) copy-start(bf16[512,128]{1,0:T(8,128)(2,1)} %constant.2.clone.table) | copy-start | bytes 393220
  32.4 7.0 %collective-permute-start.4 = (f32[16,8,128]{2,1,0:T(8,128)S(1)}, f32[16,8,128]{2,1,0:T(8,128)S(1)}, u32[]{:S(2)}, u32[]{:S(2)}) collective-permute-start(f32[16,8,128]{2,1,0:T(8,128)S(1)} %get-tuple-element.23), channel_id=1, source_target_pairs={{0,256},{256,512},{512,768},{1,257},{257,513},{513,769},{2,258},{2... | collective-permute-start | bytes 196616 | tf_op jit(solution)/shard_map/ppermute | solution.py:38
  37.4 6.2 %copy-start.6 = (f32[2]{0:T(128)S(1)}, f32[2]{0:T(128)}, u32[]{:S(2)}) copy-start(f32[2]{0:T(128)} %bounds.2) | copy-start | bytes 28
  37.5 6.2 %collective-permute-start.5 = (f32[16,8,128]{2,1,0:T(8,128)S(1)}, f32[16,8,128]{2,1,0:T(8,128)S(1)}, u32[]{:S(2)}, u32[]{:S(2)}) collective-permute-start(f32[16,8,128]{2,1,0:T(8,128)S(1)} %get-tuple-element.24), channel_id=1, source_target_pairs={{256,0},{512,256},{768,512},{257,1},{513,257},{769,513},{258,2},{5... | collective-permute-start | bytes 196616 | tf_op jit(solution)/shard_map/ppermute | solution.py:38
  52.5 5.0 %collective-permute-start.6 = (f32[5,16,128]{2,1,0:T(8,128)S(1)}, f32[5,16,128]{2,1,0:T(8,128)S(1)}, u32[]{:S(2)}, u32[]{:S(2)}) collective-permute-start(f32[5,16,128]{2,1,0:T(8,128)S(1)} %get-tuple-element.28), channel_id=1, source_target_pairs={{0,1},{1,0},{2,3},{3,2},{4,5},{5,4},{6,7},{7,6},{8,9},{9,8},{10,11... | collective-permute-start | bytes 122888 | tf_op jit(solution)/shard_map/ppermute | solution.py:31
  54.5 11.3 %collective-permute-start.7 = (f32[5,16,128]{2,1,0:T(8,128)S(1)}, f32[5,16,128]{2,1,0:T(8,128)S(1)}, u32[]{:S(2)}, u32[]{:S(2)}) collective-permute-start(f32[5,16,128]{2,1,0:T(8,128)S(1)} %get-tuple-element.29), channel_id=1, source_target_pairs={{1,2},{2,1},{3,4},{4,3},{5,6},{6,5},{7,8},{8,7},{9,10},{10,9},{11,... | collective-permute-start | bytes 122888 | tf_op jit(solution)/shard_map/ppermute | solution.py:31
  65.8 0.7 copy-start.7

commit v3 on v2

v3 whole, which is shorter than its diff:
```python
import jax
import jax.numpy as jnp
import ml_dtypes
import numpy as np
from jax import lax
from jax.experimental import pallas as pl
from jax.experimental.pallas import tpu as pltpu
from jax.sharding import PartitionSpec as P


Z, Y, X = 8, 16, 128
PZ, PY, PX = 4, 8, 64
F32 = jnp.float32
VMEM_LIMIT = 16 * 2**20

ZW = Z + 4
PLANES = 4 * ZW + Z + 2
S0, M0 = 3 * ZW, 4 * ZW
VT = 4 * PLANES
TILES = VT + 24
PACKED = TILES // 16


def parity(axis):
    return lax.rem(lax.axis_index(axis), 2)


def swap_neighbours(axis, first, second):
    size = lax.axis_size(axis)
    even = [(i, i ^ 1) for i in range(size)]
    odd = [(i, ((i + 1) ^ 1) - 1) for i in range(1, size - 1)]
    inner = lax.ppermute(first, axis, even)
    outer = lax.ppermute(second, axis, odd)
    return inner, outer


def both_neighbours(axis, to_above, to_below):
    size = lax.axis_size(axis)
    up = [(i, i + 1) for i in range(size - 1)]
    down = [(i + 1, i) for i in range(size - 1)]
    from_below = lax.ppermute(to_above, axis, up)
    from_above = lax.ppermute(to_below, axis, down)
    return from_below, from_above


def call(body, outs, scratch=(), smem=(), hbm=()):
    def run(*args):
        space = {i: pltpu.SMEM for i in smem} | {i: pltpu.HBM for i in hbm}
        args = [
            pltpu.with_memory_space_constraint(x, pltpu.HBM) if i in hbm else x
            for i, x in enumerate(args)
        ]
        return pl.pallas_call(
            body,
            in_specs=[
                pl.BlockSpec(memory_space=space.get(i, pltpu.VMEM)) for i in range(len(args))
            ],
            out_specs=[pl.BlockSpec(memory_space=pltpu.VMEM) for _ in outs],
            out_shape=[jax.ShapeDtypeStruct(o, F32) for o in outs],
            scratch_shapes=list(scratch),
            compiler_params=pltpu.CompilerParams(vmem_limit_bytes=VMEM_LIMIT),
        )(*args)

    return run


def pack_z(rhs, visc, mass, msg_even, msg_odd, sems):
    par = parity("gz")
    copies = []
    for out, up in ((msg_even, 1 - par), (msg_odd, par)):
        z = pl.ds(6 * up, 2)
        for c in range(3):
            copies.append((rhs.at[c, z], out.at[pl.ds(2 * c, 2)]))
        copies.append((visc.at[z], out.at[pl.ds(6, 2)]))
        copies.append((mass.at[pl.ds(7 * up, 1)], out.at[pl.ds(8, 1)]))
    copies = [pltpu.make_async_copy(*c, sems.at[i]) for i, c in enumerate(copies)]
    for c in copies:
        c.start()
    for c in copies:
        c.wait()


def pack_y_own(rhs, visc, mass, pscale, prhs, vbounds, pbounds, up, down, pt, coefs):
    def put(plane, value):
        down[plane] = value[:8]
        up[plane] = value[8:]

    for z in range(Z):
        for c in range(3):
            put(c * Z + z, rhs[c, z])
        put(3 * Z + z, visc[z])
        put(4 * Z + z, mass[z])
    for k in range(PZ):
        tile = jnp.concatenate([pscale[k], prhs[k]], axis=1)
        pt[k] = tile
        up[5 * Z + k] = tile
        down[5 * Z + k] = tile
    for i, bounds in enumerate((vbounds, pbounds)):
        for j, value in enumerate(coefficients(bounds)):
            coefs[5 * i + j] = value


def z_halo(got_even, got_odd, i):
    even = parity("gz") == 0
    a, b = got_even[i], got_odd[i]
    return jnp.where(even, b, a), jnp.where(even, a, b)


def pack_y_halo(got_even, got_odd, up, down):
    for i in range(9):
        for side, value in enumerate(z_halo(got_even, got_odd, i)):
            down[9 * side + i] = value[:8]
            up[9 * side + i] = value[8:]


def pack_x(
    rhs, visc, mass, got_even, got_odd, below_own, above_own, below_halo, above_halo, pt,
    main, up, down,
):
    def put(p, value, below, above):
        main[4 * p] = below
        main[4 * p + 1] = value[:8]
        main[4 * p + 2] = value[8:]
        main[4 * p + 3] = above

    for z in range(Z):
        for c in range(3):
            i = c * Z + z
            put(c * ZW + 2 + z, rhs[c, z], below_own[i], above_own[i])
        put(S0 + 2 + z, visc[z], below_own[3 * Z + z], above_own[3 * Z + z])
        put(M0 + 1 + z, mass[z], below_own[4 * Z + z], above_own[4 * Z + z])
    for i in range(9):
        field, j = divmod(i, 2)
        places = (field * ZW + j, field * ZW + ZW - 2 + j) if i < 8 else (M0, M0 + Z + 1)
        for side, value in enumerate(z_halo(got_even, got_odd, i)):
            put(places[side], value, below_halo[9 * side + i], above_halo[9 * side + i])
    lane = lanes()
    for k in range(PZ):
        tiles = (below_own[5 * Z + k], pt[k], above_own[5 * Z + k])
        for t, src in enumerate(tiles):
            turned = pltpu.roll(src, 64, axis=1)
            main[VT + 3 * k + t] = jnp.where(lane < 64, src, turned)
            main[VT + 12 + 3 * k + t] = jnp.where(lane < 64, turned, src)
    for i in range(PACKED):
        turned = main[16 * i : 16 * i + 16].reshape(X, X).T
        down[i] = turned[:8]
        up[i] = turned[X - 8 :]


def lanes():
    return lax.broadcasted_iota(jnp.int32, (8, X), 1)


def coefficients(bounds):
    low = jnp.full((8, X), bounds[0], F32)
    high = jnp.full((8, X), bounds[1], F32)
    centre = (high + low) / 2.0
    spread = (high - low) / 2.0
    sigma = centre / spread
    rho0 = 1.0 / sigma
    rho1 = 1.0 / (2.0 * sigma - rho0)
    rho2 = 1.0 / (2.0 * sigma - rho1)
    return 1.0 / centre, rho1 * rho0, 2.0 * rho1 / spread, rho2 * rho1, 2.0 * rho2 / spread


def tall(coef, rows):
    return jnp.concatenate([coef] * (rows // 8), axis=0)


def restriction():
    table = np.zeros((4, X, X), np.float32)
    for half in range(2):
        for l in range(X):
            x = l if half == 0 else (X + l if l < 8 else l - X)
            if half and 8 <= l < 120:
                continue
            for node in range(-2, PX + 2):
                o = x - 2 * node
                table[half, l, node + 2] = {-1: 0.25, 0: 0.5, 1: 0.25}.get(o, 0.0)
                table[2 + half, l, node + 2] = {-2: -0.125, -1: -0.25, 1: 0.25, 2: 0.125}.get(o, 0.0)
    return table.reshape(4 * X, X).astype(ml_dtypes.bfloat16)


SMOOTH_Z = {-1: (), 0: ((0, 0.5), (1, 0.25)), 4: ((7, 0.25),)}
DERIVE_Z = {
    -1: ((0, 0.125),),
    0: ((1, 0.25), (2, 0.125)),
    1: ((0, -0.125), (1, -0.25), (3, 0.25), (4, 0.125)),
    2: ((2, -0.125), (3, -0.25), (5, 0.25), (6, 0.125)),
    3: ((4, -0.125), (5, -0.25), (7, 0.25)),
    4: ((6, -0.125), (7, -0.25)),
}
for _k in (1, 2, 3):
    SMOOTH_Z[_k] = ((2 * _k - 1, 0.25), (2 * _k, 0.5), (2 * _k + 1, 0.25))


def smoothing():
    ring = np.eye(2 * X, dtype=np.float32)
    ring += 0.5 * (np.roll(ring, 1, axis=0) + np.roll(ring, -1, axis=0))
    return np.concatenate([ring, ring]).astype(ml_dtypes.bfloat16)


def split(value, parts):
    out = []
    for _ in range(parts):
        out.append(value.astype(jnp.bfloat16))
        value = value - out[-1].astype(F32)
    return out


def dot(a, b):
    return lax.dot_general(a, b, (((1,), (0,)), ((), ())), preferred_element_type=F32)


def velocity_step(
    main, from_below, from_above, table, ring, coefs, vel, coupled, pscale, msg_even, msg_odd,
    halo, w, d, r, u, t, lhs, s, g, q, ptmp,
):
    lane = lanes()
    gap = jnp.zeros((X - 16, X), F32)
    for i in range(PACKED):
        strips = jnp.concatenate([from_above[i], gap, from_below[i]], axis=0)
        halo[16 * i : 16 * i + 16] = strips.T.reshape(16, 8, X)

    inv, a1, g1, a2, g2 = (tall(coefs[i], 32) for i in range(5))
    t[...] = jnp.zeros_like(t)

    def planes(ref, p):
        return ref[pl.ds(4 * p, 4)].reshape(32, X)

    def smooth(k, z0, count):
        for c in range(3):
            def rows(z, _):
                for h in range(2):
                    src = w.at[k, c, h]
                    v = src[z] + 0.5 * (src[z - 1] + src[z + 1])
                    t[h, 8:40] = v
                    v = v + 0.5 * (t[h, 7:39] + t[h, 9:41])
                    at = pl.ds((c * count + z - z0) * 32, 32)
                    for part, value in enumerate(split(v, 2)):
                        lhs[at, (2 * part + h) * X : (2 * part + h + 1) * X] = value
                return 0

            lax.fori_loop(z0, z0 + count, rows, 0)
        total = 3 * count * 32
        s[:total] = dot(lhs[:total], ring[...])

    for c in range(3):
        def weight(z, _):
            for h, src in enumerate((main, halo)):
                w[0, c, h, z] = planes(src, S0 + z) * (planes(src, c * ZW + z) * inv)
            return 0

        lax.fori_loop(0, ZW, weight, 0)

    smooth(0, 1, Z + 2)
    for c in range(3):
        def sweep1(z, _):
            at = pl.ds((c * (Z + 2) + z - 1) * 32, 32)
            for h, src in enumerate((main, halo)):
                b = planes(src, c * ZW + z)
                visc = planes(src, S0 + z)
                d0 = b * inv
                lap = 16.0 * w[0, c, h, z] - 2.0 * s[at, h * X : (h + 1) * X]
                res = b - (visc * lap + planes(src, M0 + z - 1) * d0)
                d1 = a1 * d0 + g1 * res
                r[c, h, z] = res
                d[c, h, z] = d1
                w[1, c, h, z] = visc * d1
            return 0

        lax.fori_loop(1, ZW - 1, sweep1, 0)

    smooth(1, 2, Z)
    for c in range(3):
        def sweep2(z, _):
            at = pl.ds((c * Z + z - 2) * 32, 32)
            for h, src in enumerate((main, halo)):
                d1 = d[c, h, z]
                lap = 16.0 * w[1, c, h, z] - 2.0 * s[at, h * X : (h + 1) * X]
                res = r[c, h, z] - (planes(src, S0 + z) * lap + planes(src, M0 + z - 1) * d1)
                total = planes(src, c * ZW + z) * inv + d1 + (a2 * d1 + g2 * res)
                u[c, h, z - 2] = total
                if h == 0:
                    vel[c, z - 2] = total[8:24]
            return 0

        lax.fori_loop(2, ZW - 2, sweep2, 0)

    q[...] = jnp.zeros_like(q)
    for node in range(-1, 5):
        rows = slice(16 * (node + 1), 16 * (node + 1) + 12)

        def along_z(c, h, weights):
            acc = None
            for z, f in weights:
                term = f * u[c, h, z]
                acc = term if acc is None else acc + term
            return acc

        def at(k, start):
            return g[k, pl.ds(start, 12, stride=2), :]

        for h in range(2):
            cols = slice(X * h, X * (h + 1))
            g[2] = along_z(2, h, DERIVE_Z[node])
            total = 0.25 * (at(2, 3) + at(2, 5)) + 0.5 * at(2, 4)
            if SMOOTH_Z[node]:
                g[0] = along_z(0, h, SMOOTH_Z[node])
                g[1] = along_z(1, h, SMOOTH_Z[node])
                total = total + 0.25 * (at(1, 5) - at(1, 3)) + 0.125 * (at(1, 6) - at(1, 2))
                q[rows, 2 * X + X * h : 3 * X + X * h] = 0.25 * (at(0, 3) + at(0, 5)) + 0.5 * at(0, 4)
            q[rows, cols] = total

    div = sum(dot(v, table[...]) for v in reversed(split(q[...], 3)))

    def nodes(base, k):
        for i in range(3):
            own = pltpu.roll(main[base + 3 * k + i], 2, axis=1)
            side = halo[base + 3 * k + i]
            left = pltpu.roll(side, 2, axis=1)
            right = pltpu.roll(side, 66, axis=1)
            value = jnp.where(lane < 66, own, jnp.where(lane < 68, right, 0.0))
            ptmp[8 * i : 8 * i + 8] = jnp.where(lane < 2, left, value)
        return ptmp[6:18]

    coupled[...] = -div.reshape(6, 16, X)
    pscale[...] = jnp.zeros_like(pscale)
    for k in range(PZ):
        pscale[k, :12] = nodes(VT, k)
        coupled[k + 1, :12] = nodes(VT + 12, k) - div[16 * (k + 1) : 16 * (k + 1) + 12]
    par = parity("gz")
    for out, up in ((msg_even, 1 - par), (msg_odd, par)):
        for j in range(3):
            out[j] = coupled[3 * up + j]
        for j in range(2):
            out[3 + j] = pscale[2 * up + j]


def pressure_step(coupled, pscale, got_even, got_odd, coefs, out):
    below, above = [], []
    for i in range(5):
        low, high = z_halo(got_even, got_odd, i)
        below.append(low)
        above.append(high)
    b = [
        below[0], below[1] + coupled[0], below[2] + coupled[1], coupled[2], coupled[3],
        coupled[4] + above[0], coupled[5] + above[1], above[2],
    ]
    s = [below[3], below[4], pscale[0], pscale[1], pscale[2], pscale[3], above[3], above[4]]
    inv, a1, g1, a2, g2 = (tall(coefs[5 + i], 16) for i in range(5))

    def operator(w, z):
        v = (1.0 / 6.0) * (w[z - 1] + w[z + 1]) + (2.0 / 3.0) * w[z]
        v = (1.0 / 6.0) * (pltpu.roll(v, 1, axis=0) + pltpu.roll(v, 15, axis=0)) + (2.0 / 3.0) * v
        v = (1.0 / 6.0) * (pltpu.roll(v, 1, axis=1) + pltpu.roll(v, X - 1, axis=1)) + (2.0 / 3.0) * v
        return s[z] * v

    d0 = [v * inv for v in b]
    w = [x * y for x, y in zip(s, d0)]
    r1, d1, w1 = [None] * 8, [None] * 8, [None] * 8
    for z in range(1, 7):
        r1[z] = b[z] - operator(w, z)
        d1[z] = a1 * d0[z] + g1 * r1[z]
        w1[z] = s[z] * d1[z]
    for z in range(2, 6):
        res = r1[z] - operator(w1, z)
        total = d0[z] + d1[z] + (a2 * d1[z] + g2 * res)
        total = pltpu.roll(pltpu.roll(total, 14, axis=0), X - 2, axis=1)
        out[z - 2] = total[:PY, :PX]


def per_device(rhs, prhs, visc, mass, pscale, vbounds, pbounds):
    plane, tile = (Y, X), (8, X)
    msg_even, msg_odd = call(
        pack_z, [(9, *plane)] * 2, scratch=[pltpu.SemaphoreType.DMA((10,))], hbm=(0, 1, 2)
    )(rhs, visc, mass)
    z_halos = swap_neighbours("gz", msg_even, msg_odd)
    up, down, pt, coefs = call(
        pack_y_own, [(5 * Z + PZ, *tile)] * 2 + [(PZ, *tile), (10, *tile)], smem=(5, 6)
    )(rhs, visc, mass, pscale, prhs, vbounds, pbounds)
    y_own = both_neighbours("gy", up, down)
    up, down = call(pack_y_halo, [(18, *tile)] * 2)(*z_halos)
    y_halos = both_neighbours("gy", up, down)
    main, up, down = call(pack_x, [(TILES, *tile), (PACKED, *tile), (PACKED, *tile)])(
        rhs, visc, mass, *z_halos, *y_own, *y_halos, pt
    )
    below, above = both_neighbours("gx", up, down)
    vel, coupled, scale, msg_even, msg_odd = call(
        velocity_step,
        [(3, Z, Y, X), (6, *plane), (PZ, *plane), (5, *plane), (5, *plane)],
        scratch=[
            pltpu.VMEM((TILES, 8, X), F32),
            pltpu.VMEM((2, 3, 2, ZW, 32, X), F32),
            pltpu.VMEM((3, 2, ZW, 32, X), F32),
            pltpu.VMEM((3, 2, ZW, 32, X), F32),
            pltpu.VMEM((3, 2, Z, 32, X), F32),
            pltpu.VMEM((2, 48, X), F32),
            pltpu.VMEM((3 * (Z + 2) * 32, 4 * X), jnp.bfloat16),
            pltpu.VMEM((3 * (Z + 2) * 32, 2 * X), F32),
            pltpu.VMEM((3, 32, X), F32),
            pltpu.VMEM((96, 4 * X), F32),
            pltpu.VMEM((24, X), F32),
        ],
    )(main, below, above, jnp.asarray(restriction()), jnp.asarray(smoothing()), coefs)
    z_halos = swap_neighbours("gz", msg_even, msg_odd)
    (pressure,) = call(pressure_step, [(PZ, PY, PX)])(coupled, scale, *z_halos, coefs)
    return vel, pressure


def solution(mesh):
    block = P("gz", "gy", "gx")
    field = P(None, "gz", "gy", "gx")
    return jax.shard_map(
        per_device,
        mesh=mesh,
        in_specs=(field, block, block, block, block, P(), P()),
        out_specs=(field, block),
        check_vma=False,
    )
```

time: 68.3 us -> 71.6 us (1.048)
  starting transfers between devices: 25.5 us -> 30.8 us
  Pallas kernels: 11.5 us -> 7.98 us
  local copies, waits for them, and re-layouts: 3.27 us -> 5.38 us
  waiting for transfers between devices: 26.8 us -> 25.9 us
    ppermute x8 -> x10, starting transfers between devices: 25.5 us -> 30.8 us  [the longest x3 14.1 us: both_neighbours(): from_below = lax.ppermute(to_above, axis, up)]
    pallas_call x5 -> x6, Pallas kernels: 11.5 us -> 7.98 us  [run(): pl.pallas_call(body, in_specs=[pl.BlockSpec(memory_space=space.get(i, plt...]
    unnamed x16 -> x24, local copies, waits for them, and re-layouts: 3.27 us -> 5.38 us
    ppermute x8 -> x10, waiting for transfers between devices: 26.8 us -> 25.9 us  [the longest x2 16.1 us: swap_neighbours(): outer = lax.ppermute(second, axis, odd)]
  transfers between devices with their start and end apart: 8 -> 10, of which waited for: 5 -> 5; matrix products, arithmetic and copies ran while one was open for 0% -> 0% of each run, Pallas kernels for 0% -> 1%
where the time goes in v3:
time: 71.6 us; the launch traced here: 70.9 us
  starting transfers between devices  30.8 us (43%)
  waiting for transfers between devices  25.9 us (36%)
  Pallas kernels  7.98 us (11%)
  local copies, waits for them, and re-layouts  5.38 us (8%)
  between operations  0.82 us (1%)
    ppermute x2, waiting for transfers between devices, swap_neighbours(): outer = lax.ppermute(second, axis, odd)  16.1 us
    ppermute x3, starting transfers between devices, both_neighbours(): from_below = lax.ppermute(to_above, axis, up)  14.1 us
    ppermute x3, waiting for transfers between devices, both_neighbours(): from_above = lax.ppermute(to_below, axis, down)  9.64 us
    pallas_call x6, Pallas kernels, run(): pl.pallas_call(body, in_specs=[pl.BlockSpec(memory_space=space.get(i, plt...  7.98 us
    ppermute x2, starting transfers between devices, swap_neighbours(): outer = lax.ppermute(second, axis, odd)  7 us
    ppermute x3, starting transfers between devices, both_neighbours(): from_above = lax.ppermute(to_below, axis, down)  5.89 us
    unnamed x24, local copies, waits for them, and re-layouts  5.38 us
    ppermute x2, starting transfers between devices, swap_neighbours(): inner = lax.ppermute(first, axis, even)  3.83 us
  transfers between devices with their start and end apart: 10, of which 5 were waited for; matrix products, arithmetic and copies ran while one was open for 0% of the time, Pallas kernels for 1%

profile of v3, /device:TPU:562, one launch (start us, length us, event | category | flops | bytes accessed | tf_op | source)
XLA Modules:
  0.0 70.9 jit_solution(4039683185673732184)
XLA Ops:
  0.6 0.0 copy-start
  0.6 0.9 %copy-done = f32[3,8,16,128]{3,2,1,0:T(8,128)S(1)} copy-done((f32[3,8,16,128]{3,2,1,0:T(8,128)S(1)}, f32[3,8,16,128]{3,2,1,0:T(8,128)}, u32[]{:S(2)}) %copy-start) | copy-done | bytes 196632
  1.6 0.8 %copy-done.2 = f32[8,16,128]{2,1,0:T(8,128)S(1)} copy-done((f32[8,16,128]{2,1,0:T(8,128)S(1)}, f32[8,16,128]{2,1,0:T(8,128)}, u32[]{:S(2)}) %copy-start.2) | copy-done | bytes 65560
  2.4 0.8 %copy-done.4 = f32[8,16,128]{2,1,0:T(8,128)S(1)} copy-done((f32[8,16,128]{2,1,0:T(8,128)S(1)}, f32[8,16,128]{2,1,0:T(8,128)}, u32[]{:S(2)}) %copy-start.4) | copy-done | bytes 65560
  3.2 0.7 %copy-done.8 = f32[4,8,64]{2,1,0:T(8,128)S(1)} copy-done((f32[4,8,64]{2,1,0:T(8,128)S(1)}, f32[4,8,64]{2,1,0:T(8,128)}, u32[]{:S(2)}) %copy-start.8) | copy-done | bytes 8216
  4.0 0.7 %copy-done.9 = f32[4,8,64]{2,1,0:T(8,128)S(1)} copy-done((f32[4,8,64]{2,1,0:T(8,128)S(1)}, f32[4,8,64]{2,1,0:T(8,128)}, u32[]{:S(2)}) %copy-start.9) | copy-done | bytes 8216
  4.7 0.7 copy-done.10
  5.3 0.7 copy-done.11
  6.0 0.6 shard_map.105
  6.6 4.8 %collective-permute-start.2 = (f32[44,8,128]{2,1,0:T(8,128)S(1)}, f32[44,8,128]{2,1,0:T(8,128)S(1)}, u32[]{:S(2)}, u32[]{:S(2)}) collective-permute-start(f32[44,8,128]{2,1,0:T(8,128)S(1)} %get-tuple-element.20), channel_id=1, source_target_pairs={{0,32},{32,64},{64,96},{96,128},{128,160},{160,192},{192,224},{1,3... | collective-permute-start | bytes 540680 | tf_op jit(solution)/shard_map/ppermute | solution.py:41
  11.4 2.1 %collective-permute-start.3 = (f32[44,8,128]{2,1,0:T(8,128)S(1)}, f32[44,8,128]{2,1,0:T(8,128)S(1)}, u32[]{:S(2)}, u32[]{:S(2)}) collective-permute-start(f32[44,8,128]{2,1,0:T(8,128)S(1)} %get-tuple-element.21), channel_id=1, source_target_pairs={{32,0},{64,32},{96,64},{128,96},{160,128},{192,160},{224,192},{33,... | collective-permute-start | bytes 540680 | tf_op jit(solution)/shard_map/ppermute | solution.py:42
  13.5 1.0 %shard_map.104 = (f32[9,16,128]{2,1,0:T(8,128)S(1)}, f32[9,16,128]{2,1,0:T(8,128)S(1)}) custom-call(f32[3,8,16,128]{3,2,1,0:T(8,128)} %rhs.5, f32[8,16,128]{2,1,0:T(8,128)} %visc.5, f32[8,16,128]{2,1,0:T(8,128)} %mass.5), custom_call_target="tpu_custom_call" | custom-call | tf_op jit(solution)/shard_map/pallas_call | solution.py:53
  14.4 1.9 %collective-permute-start = (f32[9,16,128]{2,1,0:T(8,128)S(1)}, f32[9,16,128]{2,1,0:T(8,128)S(1)}, u32[]{:S(2)}, u32[]{:S(2)}) collective-permute-start(f32[9,16,128]{2,1,0:T(8,128)S(1)} %get-tuple-element.18), channel_id=1, source_target_pairs={{0,1},{1,0},{2,3},{3,2},{4,5},{5,4},{6,7},{7,6},{8,9},{9,8},{10,11... | collective-permute-start | bytes 221192 | tf_op jit(solution)/shard_map/ppermute | solution.py:32
  16.4 0.0 copy-start.3
  16.4 4.9 %collective-permute-start.1 = (f32[9,16,128]{2,1,0:T(8,128)S(1)}, f32[9,16,128]{2,1,0:T(8,128)S(1)}, u32[]{:S(2)}, u32[]{:S(2)}) collective-permute-start(f32[9,16,128]{2,1,0:T(8,128)S(1)} %get-tuple-element.19), channel_id=1, source_target_pairs={{1,2},{2,1},{3,4},{4,3},{5,6},{6,5},{7,8},{8,7},{9,10},{10,9},{11,... | collective-permute-start | bytes 221192 | tf_op jit(solution)/shard_map/ppermute | solution.py:33
  21.3 6.9 %collective-permute-done.1.got_odd = f32[9,16,128]{2,1,0:T(8,128)S(1)} collective-permute-done((f32[9,16,128]{2,1,0:T(8,128)S(1)}, f32[9,16,128]{2,1,0:T(8,128)S(1)}, u32[]{:S(2)}, u32[]{:S(2)}) %collective-permute-start.1) | collective-permute-done | bytes 73760 | tf_op jit(solution)/shard_map/ppermute | solution.py:33
  28.2 5.1 %collective-permute-start.4 = (f32[18,8,128]{2,1,0:T(8,128)S(1)}, f32[18,8,128]{2,1,0:T(8,128)S(1)}, u32[]{:S(2)}, u32[]{:S(2)}) collective-permute-start(f32[18,8,128]{2,1,0:T(8,128)S(1)} %get-tuple-element.22), channel_id=1, source_target_pairs={{0,32},{32,64},{64,96},{96,128},{128,160},{160,192},{192,224},{1,3... | collective-permute-start | bytes 221192 | tf_op jit(solution)/shard_map/ppermute | solution.py:41
  33.4 1.9 %collective-permute-start.5 = (f32[18,8,128]{2,1,0:T(8,128)S(1)}, f32[18,8,128]{2,1,0:T(8,128)S(1)}, u32[]{:S(2)}, u32[]{:S(2)}) collective-permute-start(f32[18,8,128]{2,1,0:T(8,128)S(1)} %get-tuple-element.23), channel_id=1, source_target_pairs={{32,0},{64,32},{96,64},{128,96},{160,128},{192,160},{224,192},{33,... | collective-permute-start | bytes 221192 | tf_op jit(solution)/shard_map/ppermute | solution.py:42
  35.3 0.0 collective-permute-done.4.below_halo
  35.3 5.5 %collective-permute-done.5.above_halo = f32[18,8,128]{2,1,0:T(8,128)S(1)} collective-permute-done((f32[18,8,128]{2,1,0:T(8,128)S(1)}, f32[18,8,128]{2,1,0:T(8,128)S(1)}, u32[]{:S(2)}, u32[]{:S(2)}) %collective-permute-start.5) | collective-permute-done | bytes 73760 | tf_op jit(solution)/shard_map/ppermute | solution.py:42
  40.9 0.0 copy-start.6
  40.9 0.0 copy-start.7
  40.9 0.4 shard_map.107
  41.3 4.1 %collective-permute-start.6 = (f32[16,8,128]{2,1,0:T(8,128)S(1)}, f32[16,8,128]{2,1,0:T(8,128)S(1)}, u32[]{:S(2)}, u32[]{:S(2)}) collective-permute-start(f32[16,8,128]{2,1,0:T(8,128)S(1)} %get-tuple-element.26), channel_id=1, source_target_pairs={{0,256},{256,512},{512,768},{1,257},{257,513},{513,769},{2,258},{2... | collective-permute-start | bytes 196616 | tf_op jit(solution)/shard_map/ppermute | solution.py:41
  45.4 1.9 %collective-permute-start.7 = (f32[16,8,128]{2,1,0:T(8,128)S(1)}, f32[16,8,128]{2,1,0:T(8,128)S(1)}, u32[]{:S(2)}, u32[]{:S(2)}) collective-permute-start(f32[16,8,128]{2,1,0:T(8,128)S(1)} %get-tuple-element.27), channel_id=1, source_target_pairs={{256,0},{512,256},{768,512},{257,1},{513,257},{769,513},{258,2},{5... | collective-permute-start | bytes 196616 | tf_op jit(solution)/shard_map/ppermute | solution.py:42
  47.3 0.1 collective-permute-done.6.from_below
  47.4 4.1 %collective-permute-done.7.from_above = f32[16,8,128]{2,1,0:T(8,128)S(1)} collective-permute-done((f32[16,8,128]{2,1,0:T(8,128)S(1)}, f32[16,8,128]{2,1,0:T(8,128)S(1)}, u32[]{:S(2)}, u32[]{:S(2)}) %collective-permute-start.7) | collective-permute-done | bytes 65568 | tf_op jit(solution)/shard_map/ppermute | solution.py:42
  51.6 5.2 %shard_map.108 = (f32[3,8,16,128]{3,2,1,0:T(8,128)}, f32[6,16,128]{2,1,0:T(8,128)S(1)}, f32[4,16,128]{2,1,0:T(8,128)S(1)}, f32[5,16,128]{2,1,0:T(8,128)S(1)}, f32[5,16,128]{2,1,0:T(8,128)S(1)}) custom-call(f32[256,8,128]{2,1,0:T(8,128)S(1)} %get-tuple-element.25.main, f32[16,8,128]{2,1,0:T(8,128)S(1)} %collective-permute-done.6.from_below, ...), custom_call_target="tpu_custom_call" | custom-call | tf_op jit(solution)/shard_map/pallas_call | solution.py:53
  56.7 1.9 %collective-permute-start.8 = (f32[5,16,128]{2,1,0:T(8,128)S(1)}, f32[5,16,128]{2,1,0:T(8,128)S(1)}, u32[]{:S(2)}, u32[]{:S(2)}) collective-permute-start(f32[5,16,128]{2,1,0:T(8,128)S(1)} %get-tuple-element.32), channel_id=1, source_target_pairs={{0,1},{1,0},{2,3},{3,2},{4,5},{5,4},{6,7},{7,6},{8,9},{9,8},{10,11... | collective-permute-start | bytes 122888 | tf_op jit(solution)/shard_map/ppermute | solution.py:32
  58.6 2.1 %collective-permute-start.9 = (f32[5,16,128]{2,1,0:T(8,128)S(1)}, f32[5,16,128]{2,1,0:T(8,128)S(1)}, u32[]{:S(2)}, u32[]{:S(2)}) collective-permute-start(f32[5,16,128]{2,1,0:T(8,128)S(1)} %get-tuple-element.33), channel_id=1, source_target_pairs={{1,2},{2,1},{3,4},{4,3},{5,6},{6,5},{7,8},{8,7},{9,10},{10,9},{11,... | collective-permute-start | bytes 122888 | tf_op jit(solution)/shard_map/ppermute | solution.py:33
  60.8 9.2 %collective-permute-done.9.got_odd = f32[5,16,128]{2,1,0:T(8,128)S(1)} collective-permute-done((f32[5,16,128]{2,1,0:T(8,128)S(1)}, f32[5,16,128]{2,1,0:T(8,128)S(1)}, u32[]{:S(2)}, u32[]{:S(2)}) %collective-permute-start.9) | collective-permute-done | bytes 40992 | tf_op jit(solution)/shard_map/ppermute | solution.py:33
  70.0 0.9 %shard_map.109 = f32[4,8,64]{2,1,0:T(8,128)} custom-call(f32[6,16,128]{2,1,0:T(8,128)S(1)} %get-tuple-element.30.coupled, f32[4,16,128]{2,1,0:T(8,128)S(1)} %get-tuple-element.31.pscale, f32[5,16,128]{2,1,0:T(8,128)S(1)} %collective-permute-done.8.got_even, f32[5,16,128]{2,1,0:T(8,128)S(1)} %collective-permute-done.9.got_odd, ...), custom_call_target="tpu_custom_call" | custom-call | tf_op jit(solution)/shard_map/pallas_call | solution.py:53
  (18 shorter events, 0.1 us)
Async XLA Ops:
  0.6 0.9 %copy-start = (f32[3,8,16,128]{3,2,1,0:T(8,128)S(1)}, f32[3,8,16,128]{3,2,1,0:T(8,128)}, u32[]{:S(2)}) copy-start(f32[3,8,16,128]{3,2,1,0:T(8,128)} %rhs.5) | copy-start | bytes 589828
  1.6 0.8 %copy-start.2 = (f32[8,16,128]{2,1,0:T(8,128)S(1)}, f32[8,16,128]{2,1,0:T(8,128)}, u32[]{:S(2)}) copy-start(f32[8,16,128]{2,1,0:T(8,128)} %visc.5) | copy-start | bytes 196612
  2.4 0.8 %copy-start.4 = (f32[8,16,128]{2,1,0:T(8,128)S(1)}, f32[8,16,128]{2,1,0:T(8,128)}, u32[]{:S(2)}) copy-start(f32[8,16,128]{2,1,0:T(8,128)} %mass.5) | copy-start | bytes 196612
  3.2 0.7 %copy-start.8 = (f32[4,8,64]{2,1,0:T(8,128)S(1)}, f32[4,8,64]{2,1,0:T(8,128)}, u32[]{:S(2)}) copy-start(f32[4,8,64]{2,1,0:T(8,128)} %pscale.1) | copy-start | bytes 24580
  4.0 0.7 %copy-start.9 = (f32[4,8,64]{2,1,0:T(8,128)S(1)}, f32[4,8,64]{2,1,0:T(8,128)}, u32[]{:S(2)}) copy-start(f32[4,8,64]{2,1,0:T(8,128)} %prhs.1) | copy-start | bytes 24580
  4.7 0.7 copy-start.10
  5.3 0.7 copy-start.11
  6.6 34.2 %collective-permute-start.2 = (f32[44,8,128]{2,1,0:T(8,128)S(1)}, f32[44,8,128]{2,1,0:T(8,128)S(1)}, u32[]{:S(2)}, u32[]{:S(2)}) collective-permute-start(f32[44,8,128]{2,1,0:T(8,128)S(1)} %get-tuple-element.20), channel_id=1, source_target_pairs={{0,32},{32,64},{64,96},{96,128},{128,160},{160,192},{192,224},{1,3... | collective-permute-start | bytes 540680 | tf_op jit(solution)/shard_map/ppermute | solution.py:41
  11.4 29.4 %copy-start.1 = (f32[3,8,16,128]{3,2,1,0:T(8,128)S(1)}, f32[3,8,16,128]{3,2,1,0:T(8,128)}, u32[]{:S(2)}) copy-start(f32[3,8,16,128]{3,2,1,0:T(8,128)} %rhs.5) | copy-start | bytes 589828
  11.4 29.4 %collective-permute-start.3 = (f32[44,8,128]{2,1,0:T(8,128)S(1)}, f32[44,8,128]{2,1,0:T(8,128)S(1)}, u32[]{:S(2)}, u32[]{:S(2)}) collective-permute-start(f32[44,8,128]{2,1,0:T(8,128)S(1)} %get-tuple-element.21), channel_id=1, source_target_pairs={{32,0},{64,32},{96,64},{128,96},{160,128},{192,160},{224,192},{33,... | collective-permute-start | bytes 540680 | tf_op jit(solution)/shard_map/ppermute | solution.py:42
  14.4 6.9 %collective-permute-start = (f32[9,16,128]{2,1,0:T(8,128)S(1)}, f32[9,16,128]{2,1,0:T(8,128)S(1)}, u32[]{:S(2)}, u32[]{:S(2)}) collective-permute-start(f32[9,16,128]{2,1,0:T(8,128)S(1)} %get-tuple-element.18), channel_id=1, source_target_pairs={{0,1},{1,0},{2,3},{3,2},{4,5},{5,4},{6,7},{7,6},{8,9},{9,8},{10,11... | collective-permute-start | bytes 221192 | tf_op jit(solution)/shard_map/ppermute | solution.py:32
  16.4 24.5 %copy-start.3 = (f32[8,16,128]{2,1,0:T(8,128)S(1)}, f32[8,16,128]{2,1,0:T(8,128)}, u32[]{:S(2)}) copy-start(f32[8,16,128]{2,1,0:T(8,128)} %visc.5) | copy-start | bytes 196612
  16.4 24.5 %copy-start.5 = (f32[8,16,128]{2,1,0:T(8,128)S(1)}, f32[8,16,128]{2,1,0:T(8,128)}, u32[]{:S(2)}) copy-start(f32[8,16,128]{2,1,0:T(8,128)} %mass.5) | copy-start | bytes 196612
  16.4 11.8 %collective-permute-start.1 = (f32[9,16,128]{2,1,0:T(8,128)S(1)}, f32[9,16,128]{2,1,0:T(8,128)S(1)}, u32[]{:S(2)}, u32[]{:S(2)}) collective-permute-start(f32[9,16,128]{2,1,0:T(8,128)S(1)} %get-tuple-element.19), channel_id=1, source_target_pairs={{1,2},{2,1},{3,4},{4,3},{5,6},{6,5},{7,8},{8,7},{9,10},{10,9},{11,... | collective-permute-start | bytes 221192 | tf_op jit(solution)/shard_map/ppermute | solution.py:33
  28.2 7.1 %collective-permute-start.4 = (f32[18,8,128]{2,1,0:T(8,128)S(1)}, f32[18,8,128]{2,1,0:T(8,128)S(1)}, u32[]{:S(2)}, u32[]{:S(2)}) collective-permute-start(f32[18,8,128]{2,1,0:T(8,128)S(1)} %get-tuple-element.22), channel_id=1, source_target_pairs={{0,32},{32,64},{64,96},{96,128},{128,160},{160,192},{192,224},{1,3... | collective-permute-start | bytes 221192 | tf_op jit(solution)/shard_map/ppermute | solution.py:41
  33.4 7.5 %collective-permute-start.5 = (f32[18,8,128]{2,1,0:T(8,128)S(1)}, f32[18,8,128]{2,1,0:T(8,128)S(1)}, u32[]{:S(2)}, u32[]{:S(2)}) collective-permute-start(f32[18,8,128]{2,1,0:T(8,128)S(1)} %get-tuple-element.23), channel_id=1, source_target_pairs={{32,0},{64,32},{96,64},{128,96},{160,128},{192,160},{224,192},{33,... | collective-permute-start | bytes 221192 | tf_op jit(solution)/shard_map/ppermute | solution.py:42
  40.9 10.7 %copy-start.6 = (bf16[512,256]{1,0:T(8,128)(2,1)S(1)}, bf16[512,256]{1,0:T(8,128)(2,1)}, u32[]{:S(2)}) copy-start(bf16[512,256]{1,0:T(8,128)(2,1)} %constant.5.clone.ring) | copy-start | bytes 786436
  40.9 10.7 %copy-start.7 = (bf16[512,128]{1,0:T(8,128)(2,1)S(1)}, bf16[512,128]{1,0:T(8,128)(2,1)}, u32[]{:S(2)}) copy-start(bf16[512,128]{1,0:T(8,128)(2,1)} %constant.4.clone.table) | copy-start | bytes 393220
  41.3 6.2 %collective-permute-start.6 = (f32[16,8,128]{2,1,0:T(8,128)S(1)}, f32[16,8,128]{2,1,0:T(8,128)S(1)}, u32[]{:S(2)}, u32[]{:S(2)}) collective-permute-start(f32[16,8,128]{2,1,0:T(8,128)S(1)} %get-tuple-element.26), channel_id=1, source_target_pairs={{0,256},{256,512},{512,768},{1,257},{257,513},{513,769},{2,258},{2... | collective-permute-start | bytes 196616 | tf_op jit(solution)/shard_map/ppermute | solution.py:41
  45.4 6.2 %collective-permute-start.7 = (f32[16,8,128]{2,1,0:T(8,128)S(1)}, f32[16,8,128]{2,1,0:T(8,128)S(1)}, u32[]{:S(2)}, u32[]{:S(2)}) collective-permute-start(f32[16,8,128]{2,1,0:T(8,128)S(1)} %get-tuple-element.27), channel_id=1, source_target_pairs={{256,0},{512,256},{768,512},{257,1},{513,257},{769,513},{258,2},{5... | collective-permute-start | bytes 196616 | tf_op jit(solution)/shard_map/ppermute | solution.py:42
  56.7 4.0 %collective-permute-start.8 = (f32[5,16,128]{2,1,0:T(8,128)S(1)}, f32[5,16,128]{2,1,0:T(8,128)S(1)}, u32[]{:S(2)}, u32[]{:S(2)}) collective-permute-start(f32[5,16,128]{2,1,0:T(8,128)S(1)} %get-tuple-element.32), channel_id=1, source_target_pairs={{0,1},{1,0},{2,3},{3,2},{4,5},{5,4},{6,7},{7,6},{8,9},{9,8},{10,11... | collective-permute-start | bytes 122888 | tf_op jit(solution)/shard_map/ppermute | solution.py:32
  58.6 11.3 %collective-permute-start.9 = (f32[5,16,128]{2,1,0:T(8,128)S(1)}, f32[5,16,128]{2,1,0:T(8,128)S(1)}, u32[]{:S(2)}, u32[]{:S(2)}) collective-permute-start(f32[5,16,128]{2,1,0:T(8,128)S(1)} %get-tuple-element.33), channel_id=1, source_target_pairs={{1,2},{2,1},{3,4},{4,3},{5,6},{6,5},{7,8},{8,7},{9,10},{10,9},{11,... | collective-permute-start | bytes 122888 | tf_op jit(solution)/shard_map/ppermute | solution.py:33

commit v4 on v3

--- a/solution.py
+++ b/solution.py
@@ -80,21 +80,7 @@
         c.wait()
 
 
-def pack_y_own(rhs, visc, mass, pscale, prhs, vbounds, pbounds, up, down, pt, coefs):
-    def put(plane, value):
-        down[plane] = value[:8]
-        up[plane] = value[8:]
-
-    for z in range(Z):
-        for c in range(3):
-            put(c * Z + z, rhs[c, z])
-        put(3 * Z + z, visc[z])
-        put(4 * Z + z, mass[z])
-    for k in range(PZ):
-        tile = jnp.concatenate([pscale[k], prhs[k]], axis=1)
-        pt[k] = tile
-        up[5 * Z + k] = tile
-        down[5 * Z + k] = tile
+def scalars(vbounds, pbounds, coefs):
     for i, bounds in enumerate((vbounds, pbounds)):
         for j, value in enumerate(coefficients(bounds)):
             coefs[5 * i + j] = value
@@ -106,41 +92,38 @@
     return jnp.where(even, b, a), jnp.where(even, a, b)
 
 
-def pack_y_halo(got_even, got_odd, up, down):
-    for i in range(9):
-        for side, value in enumerate(z_halo(got_even, got_odd, i)):
-            down[9 * side + i] = value[:8]
-            up[9 * side + i] = value[8:]
-
-
-def pack_x(
-    rhs, visc, mass, got_even, got_odd, below_own, above_own, below_halo, above_halo, pt,
-    main, up, down,
-):
-    def put(p, value, below, above):
-        main[4 * p] = below
-        main[4 * p + 1] = value[:8]
-        main[4 * p + 2] = value[8:]
-        main[4 * p + 3] = above
+def pack_y(rhs, visc, mass, got_even, got_odd, pscale, prhs, up, down):
+    def put(plane, value):
+        down[plane] = value[:8]
+        up[plane] = value[8:]
 
     for z in range(Z):
         for c in range(3):
-            i = c * Z + z
-            put(c * ZW + 2 + z, rhs[c, z], below_own[i], above_own[i])
-        put(S0 + 2 + z, visc[z], below_own[3 * Z + z], above_own[3 * Z + z])
-        put(M0 + 1 + z, mass[z], below_own[4 * Z + z], above_own[4 * Z + z])
+            put(c * ZW + 2 + z, rhs[c, z])
+        put(S0 + 2 + z, visc[z])
+        put(M0 + 1 + z, mass[z])
     for i in range(9):
         field, j = divmod(i, 2)
         places = (field * ZW + j, field * ZW + ZW - 2 + j) if i < 8 else (M0, M0 + Z + 1)
-        for side, value in enumerate(z_halo(got_even, got_odd, i)):
-            put(places[side], value, below_halo[9 * side + i], above_halo[9 * side + i])
+        for place, value in zip(places, z_halo(got_even, got_odd, i)):
+            put(place, value)
+    for k in range(PZ):
+        tile = jnp.concatenate([pscale[k], prhs[k]], axis=1)
+        up[PLANES + k] = tile
+        down[PLANES + k] = tile
+
+
+def pack_x(low_rows, high_rows, below, above, main, up, down):
+    for p in range(PLANES):
+        for i, src in enumerate((below, low_rows, high_rows, above)):
+            main[4 * p + i] = src[p]
     lane = lanes()
     for k in range(PZ):
-        tiles = (below_own[5 * Z + k], pt[k], above_own[5 * Z + k])
-        for t, src in enumerate(tiles):
-            turned = pltpu.roll(src, 64, axis=1)
-            main[VT + 3 * k + t] = jnp.where(lane < 64, src, turned)
-            main[VT + 12 + 3 * k + t] = jnp.where(lane < 64, turned, src)
+        for t, src in enumerate((below, low_rows, above)):
+            tile = src[PLANES + k]
+            turned = pltpu.roll(tile, 64, axis=1)
+            main[VT + 3 * k + t] = jnp.where(lane < 64, tile, turned)
+            main[VT + 12 + 3 * k + t] = jnp.where(lane < 64, turned, tile)
     for i in range(PACKED):
         turned = main[16 * i : 16 * i + 16].reshape(X, X).T
         down[i] = turned[:8]
@@ -376,14 +359,11 @@
         pack_z, [(9, *plane)] * 2, scratch=[pltpu.SemaphoreType.DMA((10,))], hbm=(0, 1, 2)
     )(rhs, visc, mass)
     z_halos = swap_neighbours("gz", msg_even, msg_odd)
-    up, down, pt, coefs = call(
-        pack_y_own, [(5 * Z + PZ, *tile)] * 2 + [(PZ, *tile), (10, *tile)], smem=(5, 6)
-    )(rhs, visc, mass, pscale, prhs, vbounds, pbounds)
-    y_own = both_neighbours("gy", up, down)
-    up, down = call(pack_y_halo, [(18, *tile)] * 2)(*z_halos)
-    y_halos = both_neighbours("gy", up, down)
+    (coefs,) = call(scalars, [(10, *tile)], smem=(0, 1))(vbounds, pbounds)
+    up, down = call(pack_y, [(PLANES + PZ, *tile)] * 2)(rhs, visc, mass, *z_halos, pscale, prhs)
+    below, above = both_neighbours("gy", up, down)
     main, up, down = call(pack_x, [(TILES, *tile), (PACKED, *tile), (PACKED, *tile)])(
-        rhs, visc, mass, *z_halos, *y_own, *y_halos, pt
+        down, up, below, above
     )
     below, above = both_neighbours("gx", up, down)
     vel, coupled, scale, msg_even, msg_odd = call(

time: 71.6 us -> 62.7 us (0.88)
  starting transfers between devices: 30.8 us -> 25.6 us
  local copies, waits for them, and re-layouts: 5.38 us -> 1.47 us
    ppermute x3 -> x2, starting transfers between devices: 14.1 us -> 9.98 us  [both_neighbours(): from_below = lax.ppermute(to_above, axis, up)]
    unnamed x24 -> x18, local copies, waits for them, and re-layouts: 5.38 us -> 1.47 us
    ppermute x3 -> x2, starting transfers between devices: 5.89 us -> 3.97 us  [both_neighbours(): from_above = lax.ppermute(to_below, axis, down)]
    ppermute x3 -> x2, waiting for transfers between devices: 0.13 us -> 1.85 us  [both_neighbours(): from_below = lax.ppermute(to_above, axis, up)]
    ppermute x2, waiting for transfers between devices: 16.1 us -> 15.2 us  [swap_neighbours(): outer = lax.ppermute(second, axis, odd)]
    ppermute x2, starting transfers between devices: 7 us -> 7.84 us  [swap_neighbours(): outer = lax.ppermute(second, axis, odd)]
    ppermute x3 -> x2, waiting for transfers between devices: 9.64 us -> 9.24 us  [both_neighbours(): from_above = lax.ppermute(to_below, axis, down)]
  transfers between devices with their start and end apart: 10 -> 8, of which waited for: 5 -> 5; matrix products, arithmetic and copies ran while one was open for 0% -> 0% of each run, Pallas kernels for 1% -> 1%
where the time goes in v4:
time: 62.7 us; the launch traced here: 62.2 us
  waiting for transfers between devices  26.2 us (42%)
  starting transfers between devices  25.6 us (41%)
  Pallas kernels  8.01 us (13%)
  local copies, waits for them, and re-layouts  1.47 us (2%)
  between operations  0.82 us (1%)
    ppermute x2, waiting for transfers between devices, swap_neighbours(): outer = lax.ppermute(second, axis, odd)  15.2 us
    ppermute x2, starting transfers between devices, both_neighbours(): from_below = lax.ppermute(to_above, axis, up)  9.98 us
    ppermute x2, waiting for transfers between devices, both_neighbours(): from_above = lax.ppermute(to_below, axis, down)  9.24 us
    pallas_call x6, Pallas kernels, run(): pl.pallas_call(body, in_specs=[pl.BlockSpec(memory_space=space.get(i, plt...  8.01 us
    ppermute x2, starting transfers between devices, swap_neighbours(): outer = lax.ppermute(second, axis, odd)  7.84 us
    ppermute x2, starting transfers between devices, both_neighbours(): from_above = lax.ppermute(to_below, axis, down)  3.97 us
    ppermute x2, starting transfers between devices, swap_neighbours(): inner = lax.ppermute(first, axis, even)  3.83 us
    ppermute x2, waiting for transfers between devices, both_neighbours(): from_below = lax.ppermute(to_above, axis, up)  1.85 us
  transfers between devices with their start and end apart: 8, of which 5 were waited for; matrix products, arithmetic and copies ran while one was open for 0% of the time, Pallas kernels for 1%

profile of v4, /device:TPU:562, one launch (start us, length us, event | category | flops | bytes accessed | tf_op | source)
XLA Modules:
  0.0 62.2 jit_solution(6336968815152738512)
XLA Ops:
  0.6 0.0 copy-start.2
  0.7 1.0 %shard_map.104 = (f32[9,16,128]{2,1,0:T(8,128)S(1)}, f32[9,16,128]{2,1,0:T(8,128)S(1)}) custom-call(f32[3,8,16,128]{3,2,1,0:T(8,128)} %rhs.3, f32[8,16,128]{2,1,0:T(8,128)} %visc.3, f32[8,16,128]{2,1,0:T(8,128)} %mass.3), custom_call_target="tpu_custom_call" | custom-call | tf_op jit(solution)/shard_map/pallas_call | solution.py:53
  1.7 1.9 %collective-permute-start = (f32[9,16,128]{2,1,0:T(8,128)S(1)}, f32[9,16,128]{2,1,0:T(8,128)S(1)}, u32[]{:S(2)}, u32[]{:S(2)}) collective-permute-start(f32[9,16,128]{2,1,0:T(8,128)S(1)} %get-tuple-element.14), channel_id=1, source_target_pairs={{0,1},{1,0},{2,3},{3,2},{4,5},{5,4},{6,7},{7,6},{8,9},{9,8},{10,11... | collective-permute-start | bytes 221192 | tf_op jit(solution)/shard_map/ppermute | solution.py:32
  3.6 4.8 %collective-permute-start.1 = (f32[9,16,128]{2,1,0:T(8,128)S(1)}, f32[9,16,128]{2,1,0:T(8,128)S(1)}, u32[]{:S(2)}, u32[]{:S(2)}) collective-permute-start(f32[9,16,128]{2,1,0:T(8,128)S(1)} %get-tuple-element.15), channel_id=1, source_target_pairs={{1,2},{2,1},{3,4},{4,3},{5,6},{6,5},{7,8},{8,7},{9,10},{10,9},{11,... | collective-permute-start | bytes 221192 | tf_op jit(solution)/shard_map/ppermute | solution.py:33
  8.4 0.0 collective-permute-done.got_even
  8.4 6.9 %collective-permute-done.1.got_odd = f32[9,16,128]{2,1,0:T(8,128)S(1)} collective-permute-done((f32[9,16,128]{2,1,0:T(8,128)S(1)}, f32[9,16,128]{2,1,0:T(8,128)S(1)}, u32[]{:S(2)}, u32[]{:S(2)}) %collective-permute-start.1) | collective-permute-done | bytes 73760 | tf_op jit(solution)/shard_map/ppermute | solution.py:33
  15.3 0.0 copy-start.5
  15.3 0.7 %copy-done.5 = f32[4,8,64]{2,1,0:T(8,128)S(1)} copy-done((f32[4,8,64]{2,1,0:T(8,128)S(1)}, f32[4,8,64]{2,1,0:T(8,128)}, u32[]{:S(2)}) %copy-start.5) | copy-done | bytes 8216
  16.0 0.7 %copy-done.6 = f32[4,8,64]{2,1,0:T(8,128)S(1)} copy-done((f32[4,8,64]{2,1,0:T(8,128)S(1)}, f32[4,8,64]{2,1,0:T(8,128)}, u32[]{:S(2)}) %copy-start.6) | copy-done | bytes 8216
  16.7 0.1 shard_map.105
  16.8 4.8 %collective-permute-start.2 = (f32[62,8,128]{2,1,0:T(8,128)S(1)}, f32[62,8,128]{2,1,0:T(8,128)S(1)}, u32[]{:S(2)}, u32[]{:S(2)}) collective-permute-start(f32[62,8,128]{2,1,0:T(8,128)S(1)} %get-tuple-element.17.high_rows), channel_id=1, source_target_pairs={{0,32},{32,64},{64,96},{96,128},{128,160},{160,192},{192,224},{1,3... | collective-permute-start | bytes 761864 | tf_op jit(solution)/shard_map/ppermute | solution.py:41
  21.6 0.0 copy-start.1
  21.6 2.1 %collective-permute-start.3 = (f32[62,8,128]{2,1,0:T(8,128)S(1)}, f32[62,8,128]{2,1,0:T(8,128)S(1)}, u32[]{:S(2)}, u32[]{:S(2)}) collective-permute-start(f32[62,8,128]{2,1,0:T(8,128)S(1)} %get-tuple-element.16.low_rows), channel_id=1, source_target_pairs={{32,0},{64,32},{96,64},{128,96},{160,128},{192,160},{224,192},{33,... | collective-permute-start | bytes 761864 | tf_op jit(solution)/shard_map/ppermute | solution.py:42
  23.7 1.8 %collective-permute-done.2.below = f32[62,8,128]{2,1,0:T(8,128)S(1)} collective-permute-done((f32[62,8,128]{2,1,0:T(8,128)S(1)}, f32[62,8,128]{2,1,0:T(8,128)S(1)}, u32[]{:S(2)}, u32[]{:S(2)}) %collective-permute-start.2) | collective-permute-done | bytes 253984 | tf_op jit(solution)/shard_map/ppermute | solution.py:41
  25.5 5.6 %collective-permute-done.3.above = f32[62,8,128]{2,1,0:T(8,128)S(1)} collective-permute-done((f32[62,8,128]{2,1,0:T(8,128)S(1)}, f32[62,8,128]{2,1,0:T(8,128)S(1)}, u32[]{:S(2)}, u32[]{:S(2)}) %collective-permute-start.3) | collective-permute-done | bytes 253984 | tf_op jit(solution)/shard_map/ppermute | solution.py:42
  31.1 0.4 shard_map.106
  31.5 0.0 copy-start.7
  31.5 0.0 copy-start.8
  31.5 5.2 %collective-permute-start.4 = (f32[16,8,128]{2,1,0:T(8,128)S(1)}, f32[16,8,128]{2,1,0:T(8,128)S(1)}, u32[]{:S(2)}, u32[]{:S(2)}) collective-permute-start(f32[16,8,128]{2,1,0:T(8,128)S(1)} %get-tuple-element.19), channel_id=1, source_target_pairs={{0,256},{256,512},{512,768},{1,257},{257,513},{513,769},{2,258},{2... | collective-permute-start | bytes 196616 | tf_op jit(solution)/shard_map/ppermute | solution.py:41
  36.7 1.9 %collective-permute-start.5 = (f32[16,8,128]{2,1,0:T(8,128)S(1)}, f32[16,8,128]{2,1,0:T(8,128)S(1)}, u32[]{:S(2)}, u32[]{:S(2)}) collective-permute-start(f32[16,8,128]{2,1,0:T(8,128)S(1)} %get-tuple-element.20), channel_id=1, source_target_pairs={{256,0},{512,256},{768,512},{257,1},{513,257},{769,513},{258,2},{5... | collective-permute-start | bytes 196616 | tf_op jit(solution)/shard_map/ppermute | solution.py:42
  38.6 0.0 copy-done.7
  38.7 0.0 copy-done.8
  38.7 0.6 shard_map.107.coefs
  39.2 0.0 collective-permute-done.4.from_below
  39.2 3.6 %collective-permute-done.5.from_above = f32[16,8,128]{2,1,0:T(8,128)S(1)} collective-permute-done((f32[16,8,128]{2,1,0:T(8,128)S(1)}, f32[16,8,128]{2,1,0:T(8,128)S(1)}, u32[]{:S(2)}, u32[]{:S(2)}) %collective-permute-start.5) | collective-permute-done | bytes 65568 | tf_op jit(solution)/shard_map/ppermute | solution.py:42
  42.9 0.0 copy-done.1
  42.9 5.1 %shard_map.108 = (f32[3,8,16,128]{3,2,1,0:T(8,128)}, f32[6,16,128]{2,1,0:T(8,128)S(1)}, f32[4,16,128]{2,1,0:T(8,128)S(1)}, f32[5,16,128]{2,1,0:T(8,128)S(1)}, f32[5,16,128]{2,1,0:T(8,128)S(1)}) custom-call(f32[256,8,128]{2,1,0:T(8,128)S(1)} %get-tuple-element.18.main, f32[16,8,128]{2,1,0:T(8,128)S(1)} %collective-permute-done.4.from_below, ...), custom_call_target="tpu_custom_call" | custom-call | tf_op jit(solution)/shard_map/pallas_call | solution.py:53
  48.0 1.9 %collective-permute-start.6 = (f32[5,16,128]{2,1,0:T(8,128)S(1)}, f32[5,16,128]{2,1,0:T(8,128)S(1)}, u32[]{:S(2)}, u32[]{:S(2)}) collective-permute-start(f32[5,16,128]{2,1,0:T(8,128)S(1)} %get-tuple-element.24), channel_id=1, source_target_pairs={{0,1},{1,0},{2,3},{3,2},{4,5},{5,4},{6,7},{7,6},{8,9},{9,8},{10,11... | collective-permute-start | bytes 122888 | tf_op jit(solution)/shard_map/ppermute | solution.py:32
  49.9 3.1 %collective-permute-start.7 = (f32[5,16,128]{2,1,0:T(8,128)S(1)}, f32[5,16,128]{2,1,0:T(8,128)S(1)}, u32[]{:S(2)}, u32[]{:S(2)}) collective-permute-start(f32[5,16,128]{2,1,0:T(8,128)S(1)} %get-tuple-element.25), channel_id=1, source_target_pairs={{1,2},{2,1},{3,4},{4,3},{5,6},{6,5},{7,8},{8,7},{9,10},{10,9},{11,... | collective-permute-start | bytes 122888 | tf_op jit(solution)/shard_map/ppermute | solution.py:33
  53.0 0.0 collective-permute-done.6.got_even
  53.0 8.3 %collective-permute-done.7.got_odd = f32[5,16,128]{2,1,0:T(8,128)S(1)} collective-permute-done((f32[5,16,128]{2,1,0:T(8,128)S(1)}, f32[5,16,128]{2,1,0:T(8,128)S(1)}, u32[]{:S(2)}, u32[]{:S(2)}) %collective-permute-start.7) | collective-permute-done | bytes 40992 | tf_op jit(solution)/shard_map/ppermute | solution.py:33
  61.3 0.9 %shard_map.109 = f32[4,8,64]{2,1,0:T(8,128)} custom-call(f32[6,16,128]{2,1,0:T(8,128)S(1)} %get-tuple-element.22.coupled, f32[4,16,128]{2,1,0:T(8,128)S(1)} %get-tuple-element.23.pscale, f32[5,16,128]{2,1,0:T(8,128)S(1)} %collective-permute-done.6.got_even, f32[5,16,128]{2,1,0:T(8,128)S(1)} %collective-permute-done.7.got_odd, f32[10,8,128]{2,1,0:T(8,128)S(1)} %shard_map.107.coefs), custom_call_target="tpu_custom_call" | custom-call | tf_op jit(solution)/shard_map/pallas_call | solution.py:53
  (8 shorter events, 0.0 us)
Async XLA Ops:
  0.6 14.6 %copy-start.2 = (f32[8,16,128]{2,1,0:T(8,128)S(1)}, f32[8,16,128]{2,1,0:T(8,128)}, u32[]{:S(2)}) copy-start(f32[8,16,128]{2,1,0:T(8,128)} %visc.3) | copy-start | bytes 196612
  0.6 14.6 %copy-start.3 = (f32[8,16,128]{2,1,0:T(8,128)S(1)}, f32[8,16,128]{2,1,0:T(8,128)}, u32[]{:S(2)}) copy-start(f32[8,16,128]{2,1,0:T(8,128)} %mass.3) | copy-start | bytes 196612
  0.6 14.6 %copy-start = (f32[3,8,16,128]{3,2,1,0:T(8,128)S(1)}, f32[3,8,16,128]{3,2,1,0:T(8,128)}, u32[]{:S(2)}) copy-start(f32[3,8,16,128]{3,2,1,0:T(8,128)} %rhs.3) | copy-start | bytes 589828
  1.7 6.7 %collective-permute-start = (f32[9,16,128]{2,1,0:T(8,128)S(1)}, f32[9,16,128]{2,1,0:T(8,128)S(1)}, u32[]{:S(2)}, u32[]{:S(2)}) collective-permute-start(f32[9,16,128]{2,1,0:T(8,128)S(1)} %get-tuple-element.14), channel_id=1, source_target_pairs={{0,1},{1,0},{2,3},{3,2},{4,5},{5,4},{6,7},{7,6},{8,9},{9,8},{10,11... | collective-permute-start | bytes 221192 | tf_op jit(solution)/shard_map/ppermute | solution.py:32
  3.6 11.7 %collective-permute-start.1 = (f32[9,16,128]{2,1,0:T(8,128)S(1)}, f32[9,16,128]{2,1,0:T(8,128)S(1)}, u32[]{:S(2)}, u32[]{:S(2)}) collective-permute-start(f32[9,16,128]{2,1,0:T(8,128)S(1)} %get-tuple-element.15), channel_id=1, source_target_pairs={{1,2},{2,1},{3,4},{4,3},{5,6},{6,5},{7,8},{8,7},{9,10},{10,9},{11,... | collective-permute-start | bytes 221192 | tf_op jit(solution)/shard_map/ppermute | solution.py:33
  15.3 0.7 %copy-start.5 = (f32[4,8,64]{2,1,0:T(8,128)S(1)}, f32[4,8,64]{2,1,0:T(8,128)}, u32[]{:S(2)}) copy-start(f32[4,8,64]{2,1,0:T(8,128)} %pscale.1) | copy-start | bytes 24580
  16.0 0.7 %copy-start.6 = (f32[4,8,64]{2,1,0:T(8,128)S(1)}, f32[4,8,64]{2,1,0:T(8,128)}, u32[]{:S(2)}) copy-start(f32[4,8,64]{2,1,0:T(8,128)} %prhs.1) | copy-start | bytes 24580
  16.8 8.7 %collective-permute-start.2 = (f32[62,8,128]{2,1,0:T(8,128)S(1)}, f32[62,8,128]{2,1,0:T(8,128)S(1)}, u32[]{:S(2)}, u32[]{:S(2)}) collective-permute-start(f32[62,8,128]{2,1,0:T(8,128)S(1)} %get-tuple-element.17.high_rows), channel_id=1, source_target_pairs={{0,32},{32,64},{64,96},{96,128},{128,160},{160,192},{192,224},{1,3... | collective-permute-start | bytes 761864 | tf_op jit(solution)/shard_map/ppermute | solution.py:41
  21.6 21.3 %copy-start.1 = (bf16[512,256]{1,0:T(8,128)(2,1)S(1)}, bf16[512,256]{1,0:T(8,128)(2,1)}, u32[]{:S(2)}) copy-start(bf16[512,256]{1,0:T(8,128)(2,1)} %constant.5.clone.ring) | copy-start | bytes 786436
  21.6 9.5 %collective-permute-start.3 = (f32[62,8,128]{2,1,0:T(8,128)S(1)}, f32[62,8,128]{2,1,0:T(8,128)S(1)}, u32[]{:S(2)}, u32[]{:S(2)}) collective-permute-start(f32[62,8,128]{2,1,0:T(8,128)S(1)} %get-tuple-element.16.low_rows), channel_id=1, source_target_pairs={{32,0},{64,32},{96,64},{128,96},{160,128},{192,160},{224,192},{33,... | collective-permute-start | bytes 761864 | tf_op jit(solution)/shard_map/ppermute | solution.py:42
  31.1 11.7 %copy-start.4 = (bf16[512,128]{1,0:T(8,128)(2,1)S(1)}, bf16[512,128]{1,0:T(8,128)(2,1)}, u32[]{:S(2)}) copy-start(bf16[512,128]{1,0:T(8,128)(2,1)} %constant.4.clone.table) | copy-start | bytes 393220
  31.5 7.1 %copy-start.7 = (f32[2]{0:T(128)S(1)}, f32[2]{0:T(128)}, u32[]{:S(2)}) copy-start(f32[2]{0:T(128)} %vbounds.1) | copy-start | bytes 28
  31.5 7.1 %copy-start.8 = (f32[2]{0:T(128)S(1)}, f32[2]{0:T(128)}, u32[]{:S(2)}) copy-start(f32[2]{0:T(128)} %pbounds.1) | copy-start | bytes 28
  31.5 7.7 %collective-permute-start.4 = (f32[16,8,128]{2,1,0:T(8,128)S(1)}, f32[16,8,128]{2,1,0:T(8,128)S(1)}, u32[]{:S(2)}, u32[]{:S(2)}) collective-permute-start(f32[16,8,128]{2,1,0:T(8,128)S(1)} %get-tuple-element.19), channel_id=1, source_target_pairs={{0,256},{256,512},{512,768},{1,257},{257,513},{513,769},{2,258},{2... | collective-permute-start | bytes 196616 | tf_op jit(solution)/shard_map/ppermute | solution.py:41
  36.7 6.2 %collective-permute-start.5 = (f32[16,8,128]{2,1,0:T(8,128)S(1)}, f32[16,8,128]{2,1,0:T(8,128)S(1)}, u32[]{:S(2)}, u32[]{:S(2)}) collective-permute-start(f32[16,8,128]{2,1,0:T(8,128)S(1)} %get-tuple-element.20), channel_id=1, source_target_pairs={{256,0},{512,256},{768,512},{257,1},{513,257},{769,513},{258,2},{5... | collective-permute-start | bytes 196616 | tf_op jit(solution)/shard_map/ppermute | solution.py:42
  48.0 5.0 %collective-permute-start.6 = (f32[5,16,128]{2,1,0:T(8,128)S(1)}, f32[5,16,128]{2,1,0:T(8,128)S(1)}, u32[]{:S(2)}, u32[]{:S(2)}) collective-permute-start(f32[5,16,128]{2,1,0:T(8,128)S(1)} %get-tuple-element.24), channel_id=1, source_target_pairs={{0,1},{1,0},{2,3},{3,2},{4,5},{5,4},{6,7},{7,6},{8,9},{9,8},{10,11... | collective-permute-start | bytes 122888 | tf_op jit(solution)/shard_map/ppermute | solution.py:32
  49.9 11.3 %collective-permute-start.7 = (f32[5,16,128]{2,1,0:T(8,128)S(1)}, f32[5,16,128]{2,1,0:T(8,128)S(1)}, u32[]{:S(2)}, u32[]{:S(2)}) collective-permute-start(f32[5,16,128]{2,1,0:T(8,128)S(1)} %get-tuple-element.25), channel_id=1, source_target_pairs={{1,2},{2,1},{3,4},{4,3},{5,6},{6,5},{7,8},{8,7},{9,10},{10,9},{11,... | collective-permute-start | bytes 122888 | tf_op jit(solution)/shard_map/ppermute | solution.py:33

commit v5 on v4

--- a/solution.py
+++ b/solution.py
@@ -43,7 +43,7 @@
     return from_below, from_above
 
 
-def call(body, outs, scratch=(), smem=(), hbm=()):
+def call(body, outs, scratch=(), smem=(), hbm=(), vmem=()):
     def run(*args):
         space = {i: pltpu.SMEM for i in smem} | {i: pltpu.HBM for i in hbm}
         args = [
@@ -56,7 +56,10 @@
                 pl.BlockSpec(memory_space=space.get(i, pltpu.VMEM)) for i in range(len(args))
             ],
             out_specs=[pl.BlockSpec(memory_space=pltpu.VMEM) for _ in outs],
-            out_shape=[jax.ShapeDtypeStruct(o, F32) for o in outs],
+            out_shape=[
+                pltpu.VMEM(o, F32) if i in vmem else jax.ShapeDtypeStruct(o, F32)
+                for i, o in enumerate(outs)
+            ],
             scratch_shapes=list(scratch),
             compiler_params=pltpu.CompilerParams(vmem_limit_bytes=VMEM_LIMIT),
         )(*args)
@@ -64,20 +67,26 @@
     return run
 
 
-def pack_z(rhs, visc, mass, msg_even, msg_odd, sems):
+def pack_z(rhs, visc, mass, msg_even, msg_odd, far, sems):
     par = parity("gz")
     copies = []
-    for out, up in ((msg_even, 1 - par), (msg_odd, par)):
-        z = pl.ds(6 * up, 2)
-        for c in range(3):
-            copies.append((rhs.at[c, z], out.at[pl.ds(2 * c, 2)]))
-        copies.append((visc.at[z], out.at[pl.ds(6, 2)]))
-        copies.append((mass.at[pl.ds(7 * up, 1)], out.at[pl.ds(8, 1)]))
+    for i, (out, up) in enumerate(((msg_even, 1 - par), (msg_odd, par))):
+        near, deep = 7 * up, 1 + 5 * up
+        copies += [
+            (rhs.at[:, near], out.at[3:6]),
+            (visc.at[near], out.at[6]),
+            (mass.at[near], out.at[7]),
+            (rhs.at[:, deep], far.at[i, :3]),
+            (visc.at[deep], far.at[i, 3]),
+        ]
     copies = [pltpu.make_async_copy(*c, sems.at[i]) for i, c in enumerate(copies)]
     for c in copies:
         c.start()
     for c in copies:
         c.wait()
+    for i, out in enumerate((msg_even, msg_odd)):
+        for c in range(3):
+            out[c] = far[i, c] * far[i, 3]
 
 
 def scalars(vbounds, pbounds, coefs):
@@ -92,35 +101,81 @@
     return jnp.where(even, b, a), jnp.where(even, a, b)
 
 
-def pack_y(rhs, visc, mass, got_even, got_odd, pscale, prhs, up, down):
-    def put(plane, value):
-        down[plane] = value[:8]
-        up[plane] = value[8:]
-
+def y_rows():
+    out = []
+    for p in range(PLANES):
+        if p not in (S0, S0 + ZW - 1):
+            out.append((p, 8, 7) if p // ZW == 1 else (p, 7, 6))
+    return out
+
+
+UP_ROWS = sum(r[1] for r in y_rows())
+DOWN_ROWS = sum(r[2] for r in y_rows())
+
+
+def padded(rows):
+    return -(-rows // 8) * 8
+
+
+def pack_nodes(pscale, prhs, pt):
+    for k in range(PZ):
+        pt[k] = jnp.concatenate([pscale[k], prhs[k]], axis=1)
+
+
+def pack_y(rhs, visc, mass, got_even, got_odd, pt, own, up, down):
     for z in range(Z):
         for c in range(3):
-            put(c * ZW + 2 + z, rhs[c, z])
-        put(S0 + 2 + z, visc[z])
-        put(M0 + 1 + z, mass[z])
-    for i in range(9):
-        field, j = divmod(i, 2)
-        places = (field * ZW + j, field * ZW + ZW - 2 + j) if i < 8 else (M0, M0 + Z + 1)
-        for place, value in zip(places, z_halo(got_even, got_odd, i)):
-            put(place, value)
+            own[c * ZW + 2 + z] = rhs[c, z]
+        own[S0 + 2 + z] = visc[z]
+        own[M0 + 1 + z] = mass[z]
+    for side, (deep, near) in enumerate(((0, 1), (ZW - 1, ZW - 2))):
+        for c in range(3):
+            own[c * ZW + deep] = z_halo(got_even, got_odd, c)[side]
+            own[c * ZW + near] = z_halo(got_even, got_odd, 3 + c)[side]
+        own[S0 + deep] = jnp.ones((Y, X), F32)
+        own[S0 + near] = z_halo(got_even, got_odd, 6)[side]
+        own[M0 + near - 1] = z_halo(got_even, got_odd, 7)[side]
+    row = lax.broadcasted_iota(jnp.int32, (8, X), 0)
+    at_up = at_down = 0
+    for p, n_up, n_down in y_rows():
+        if p // ZW == 1:
+            z = p - ZW
+            up[at_up : at_up + 8] = own[p, 8:] * jnp.where(row == 0, own[S0 + z, 8:], 1.0)
+            part = own[p, :8] * jnp.where(row == 6, own[S0 + z, :8], 1.0)
+            down[at_down : at_down + 7] = part[:7]
+        else:
+            up[at_up : at_up + n_up] = own[p, Y - n_up :]
+            down[at_down : at_down + n_down] = own[p, :n_down]
+        at_up, at_down = at_up + n_up, at_down + n_down
     for k in range(PZ):
-        tile = jnp.concatenate([pscale[k], prhs[k]], axis=1)
-        up[PLANES + k] = tile
-        down[PLANES + k] = tile
-
-
-def pack_x(low_rows, high_rows, below, above, main, up, down):
+        up[at_up + 2 * k : at_up + 2 * k + 2] = pt[k, 6:]
+        down[at_down + 2 * k : at_down + 2 * k + 2] = pt[k, :2]
+
+
+def pack_x(own, pt, below, above, main, up, down):
+    at_up = at_down = 0
+    rows = {r[0]: r[1:] for r in y_rows()}
     for p in range(PLANES):
-        for i, src in enumerate((below, low_rows, high_rows, above)):
-            main[4 * p + i] = src[p]
+        rest = jnp.full((8, X), 1.0 if S0 <= p < M0 else 0.0, F32)
+        main[4 * p] = rest
+        main[4 * p + 1] = own[p, :8]
+        main[4 * p + 2] = own[p, 8:]
+        main[4 * p + 3] = rest
+        n_up, n_down = rows.get(p, (0, 0))
+        if n_up:
+            main[4 * p, 8 - n_up :] = below[at_up : at_up + n_up]
+            main[4 * p + 3, :n_down] = above[at_down : at_down + n_down]
+        at_up, at_down = at_up + n_up, at_down + n_down
+    for k in range(PZ):
+        for t in (0, 2):
+            main[VT + 3 * k + t] = jnp.zeros((8, X), F32)
+        main[VT + 3 * k, 6:] = below[at_up + 2 * k : at_up + 2 * k + 2]
+        main[VT + 3 * k + 1] = pt[k]
+        main[VT + 3 * k + 2, :2] = above[at_down + 2 * k : at_down + 2 * k + 2]
     lane = lanes()
     for k in range(PZ):
-        for t, src in enumerate((below, low_rows, above)):
-            tile = src[PLANES + k]
+        for t in range(3):
+            tile = main[VT + 3 * k + t]
             turned = pltpu.roll(tile, 64, axis=1)
             main[VT + 3 * k + t] = jnp.where(lane < 64, tile, turned)
             main[VT + 12 + 3 * k + t] = jnp.where(lane < 64, turned, tile)
@@ -314,23 +369,27 @@
         coupled[k + 1, :12] = nodes(VT + 12, k) - div[16 * (k + 1) : 16 * (k + 1) + 12]
     par = parity("gz")
     for out, up in ((msg_even, 1 - par), (msg_odd, par)):
-        for j in range(3):
-            out[j] = coupled[3 * up + j]
-        for j in range(2):
-            out[3 + j] = pscale[2 * up + j]
-
-
-def pressure_step(coupled, pscale, got_even, got_odd, coefs, out):
-    below, above = [], []
-    for i in range(5):
-        low, high = z_halo(got_even, got_odd, i)
-        below.append(low)
-        above.append(high)
+        parts = (
+            coupled[2 + up] * pscale[1 + up], coupled[1 + 3 * up], coupled[5 * up], pscale[3 * up],
+        )
+        for j, part in enumerate(parts):
+            out[12 * j : 12 * j + 12] = part[:12]
+
+
+def pressure_step(coupled, pscale, got_even, got_odd, coefs, out, halo):
+    even = parity("gz") == 0
+    halo[...] = jnp.zeros_like(halo)
+    for i in range(4):
+        rows = slice(12 * i, 12 * i + 12)
+        a, b = got_even[rows], got_odd[rows]
+        halo[0, i, :12] = jnp.where(even, b, a)
+        halo[1, i, :12] = jnp.where(even, a, b)
     b = [
-        below[0], below[1] + coupled[0], below[2] + coupled[1], coupled[2], coupled[3],
-        coupled[4] + above[0], coupled[5] + above[1], above[2],
+        halo[0, 0], halo[0, 1] + coupled[0], halo[0, 2] + coupled[1], coupled[2],
+        coupled[3], coupled[4] + halo[1, 2], coupled[5] + halo[1, 1], halo[1, 0],
     ]
-    s = [below[3], below[4], pscale[0], pscale[1], pscale[2], pscale[3], above[3], above[4]]
+    one = jnp.ones((16, X), F32)
+    s = [one, halo[0, 3], pscale[0], pscale[1], pscale[2], pscale[3], halo[1, 3], one]
     inv, a1, g1, a2, g2 = (tall(coefs[5 + i], 16) for i in range(5))
 
     def operator(w, z):
@@ -356,19 +415,26 @@
 def per_device(rhs, prhs, visc, mass, pscale, vbounds, pbounds):
     plane, tile = (Y, X), (8, X)
     msg_even, msg_odd = call(
-        pack_z, [(9, *plane)] * 2, scratch=[pltpu.SemaphoreType.DMA((10,))], hbm=(0, 1, 2)
+        pack_z,
+        [(8, *plane)] * 2,
+        scratch=[pltpu.VMEM((2, 4, *plane), F32), pltpu.SemaphoreType.DMA((10,))],
+        hbm=(0, 1, 2),
     )(rhs, visc, mass)
     z_halos = swap_neighbours("gz", msg_even, msg_odd)
     (coefs,) = call(scalars, [(10, *tile)], smem=(0, 1))(vbounds, pbounds)
-    up, down = call(pack_y, [(PLANES + PZ, *tile)] * 2)(rhs, visc, mass, *z_halos, pscale, prhs)
+    (pt,) = call(pack_nodes, [(PZ, *tile)])(pscale, prhs)
+    own, up, down = call(
+        pack_y, [(PLANES, *plane), (padded(UP_ROWS + 8), X), (padded(DOWN_ROWS + 8), X)]
+    )(rhs, visc, mass, *z_halos, pt)
     below, above = both_neighbours("gy", up, down)
     main, up, down = call(pack_x, [(TILES, *tile), (PACKED, *tile), (PACKED, *tile)])(
-        down, up, below, above
+        own, pt, below, above
     )
     below, above = both_neighbours("gx", up, down)
     vel, coupled, scale, msg_even, msg_odd = call(
         velocity_step,
-        [(3, Z, Y, X), (6, *plane), (PZ, *plane), (5, *plane), (5, *plane)],
+        [(3, Z, Y, X), (6, *plane), (PZ, *plane), (48, X), (48, X)],
+        vmem=(0,),
         scratch=[
             pltpu.VMEM((TILES, 8, X), F32),
             pltpu.VMEM((2, 3, 2, ZW, 32, X), F32),
@@ -384,7 +450,9 @@
         ],
     )(main, below, above, jnp.asarray(restriction()), jnp.asarray(smoothing()), coefs)
     z_halos = swap_neighbours("gz", msg_even, msg_odd)
-    (pressure,) = call(pressure_step, [(PZ, PY, PX)])(coupled, scale, *z_halos, coefs)
+    (pressure,) = call(
+        pressure_step, [(PZ, PY, PX)], scratch=[pltpu.VMEM((2, 4, *plane), F32)]
+    )(coupled, scale, *z_halos, coefs)
     return vel, pressure
 
 

time: 62.7 us -> 59 us (0.941)
  the two profiles are of different devices: /device:TPU:562 before, /device:TPU:1 now
where the time goes in v5:
time: 59 us; the launch traced here: 58.6 us
  starting transfers between devices  29.1 us (49%)
  waiting for transfers between devices  20.3 us (34%)
  Pallas kernels  7.65 us (13%)
  between operations  0.83 us (1%)
  local copies, waits for them, and re-layouts  0.72 us (1%)
    ppermute x2, starting transfers between devices, swap_neighbours(): inner = lax.ppermute(first, axis, even)  17.9 us
    ppermute x2, waiting for transfers between devices, swap_neighbours(): outer = lax.ppermute(second, axis, odd)  11.9 us
    ppermute x2, waiting for transfers between devices, both_neighbours(): from_above = lax.ppermute(to_below, axis, down)  8.38 us
    pallas_call x7, Pallas kernels, run(): pl.pallas_call(body, in_specs=[pl.BlockSpec(memory_space=space.get(i, plt...  7.65 us
    ppermute x2, starting transfers between devices, swap_neighbours(): outer = lax.ppermute(second, axis, odd)  5.85 us
    ppermute x2, starting transfers between devices, both_neighbours(): from_below = lax.ppermute(to_above, axis, up)  2.73 us
    ppermute x2, starting transfers between devices, both_neighbours(): from_above = lax.ppermute(to_below, axis, down)  2.58 us
  transfers between devices with their start and end apart: 8, of which 4 were waited for; matrix products, arithmetic and copies ran while one was open for 1% of the time, Pallas kernels for 1%

profile of v5, /device:TPU:1, one launch (start us, length us, event | category | flops | bytes accessed | tf_op | source)
XLA Modules:
  0.0 58.6 jit_solution(16555673656163657141)
XLA Ops:
  0.6 0.0 copy-start
  0.6 0.0 copy-start.6
  0.7 0.0 copy-start.5
  0.7 0.0 copy-start.2
  0.7 0.0 copy-start.3
  0.7 1.0 %shard_map.104 = (f32[8,16,128]{2,1,0:T(8,128)S(1)}, f32[8,16,128]{2,1,0:T(8,128)S(1)}) custom-call(f32[3,8,16,128]{3,2,1,0:T(8,128)} %rhs.3, f32[8,16,128]{2,1,0:T(8,128)} %visc.3, f32[8,16,128]{2,1,0:T(8,128)} %mass.3), custom_call_target="tpu_custom_call" | custom-call | tf_op jit(solution)/shard_map/pallas_call | solution.py:53
  1.7 16.0 %collective-permute-start = (f32[8,16,128]{2,1,0:T(8,128)S(1)}, f32[8,16,128]{2,1,0:T(8,128)S(1)}, u32[]{:S(2)}, u32[]{:S(2)}) collective-permute-start(f32[8,16,128]{2,1,0:T(8,128)S(1)} %get-tuple-element.15), channel_id=1, source_target_pairs={{0,1},{1,0},{2,3},{3,2},{4,5},{5,4},{6,7},{7,6},{8,9},{9,8},{10,11... | collective-permute-start | bytes 196616 | tf_op jit(solution)/shard_map/ppermute | solution.py:32
  17.7 1.9 %collective-permute-start.1 = (f32[8,16,128]{2,1,0:T(8,128)S(1)}, f32[8,16,128]{2,1,0:T(8,128)S(1)}, u32[]{:S(2)}, u32[]{:S(2)}) collective-permute-start(f32[8,16,128]{2,1,0:T(8,128)S(1)} %get-tuple-element.16), channel_id=1, source_target_pairs={{1,2},{2,1},{3,4},{4,3},{5,6},{6,5},{7,8},{8,7},{9,10},{10,9},{11,... | collective-permute-start | bytes 196616 | tf_op jit(solution)/shard_map/ppermute | solution.py:33
  19.7 0.0 copy-done.6
  19.7 0.1 shard_map.105.pt
  19.8 0.0 collective-permute-done.got_even
  19.8 7.5 %collective-permute-done.1.got_odd = f32[8,16,128]{2,1,0:T(8,128)S(1)} collective-permute-done((f32[8,16,128]{2,1,0:T(8,128)S(1)}, f32[8,16,128]{2,1,0:T(8,128)S(1)}, u32[]{:S(2)}, u32[]{:S(2)}) %collective-permute-start.1) | collective-permute-done | bytes 65568 | tf_op jit(solution)/shard_map/ppermute | solution.py:33
  27.2 0.1 shard_map.106
  27.3 1.3 %collective-permute-start.2 = (f32[416,128]{1,0:T(8,128)S(1)}, f32[416,128]{1,0:T(8,128)S(1)}, u32[]{:S(2)}, u32[]{:S(2)}) collective-permute-start(f32[416,128]{1,0:T(8,128)S(1)} %get-tuple-element.18), channel_id=1, source_target_pairs={{0,32},{32,64},{64,96},{96,128},{128,160},{160,192},{192,224},{1,3... | collective-permute-start | bytes 638984 | tf_op jit(solution)/shard_map/ppermute | solution.py:41
  28.6 1.3 %collective-permute-start.3 = (f32[360,128]{1,0:T(8,128)S(1)}, f32[360,128]{1,0:T(8,128)S(1)}, u32[]{:S(2)}, u32[]{:S(2)}) collective-permute-start(f32[360,128]{1,0:T(8,128)S(1)} %get-tuple-element.19), channel_id=1, source_target_pairs={{32,0},{64,32},{96,64},{128,96},{160,128},{192,160},{224,192},{33,... | collective-permute-start | bytes 552968 | tf_op jit(solution)/shard_map/ppermute | solution.py:42
  29.9 5.3 %collective-permute-done.3.above = f32[360,128]{1,0:T(8,128)S(1)} collective-permute-done((f32[360,128]{1,0:T(8,128)S(1)}, f32[360,128]{1,0:T(8,128)S(1)}, u32[]{:S(2)}, u32[]{:S(2)}) %collective-permute-start.3) | collective-permute-done | bytes 184352 | tf_op jit(solution)/shard_map/ppermute | solution.py:42
  35.2 0.0 collective-permute-done.2.below
  35.2 0.4 shard_map.107
  35.6 0.0 copy-start.7
  35.6 0.0 copy-start.8
  35.6 1.4 %collective-permute-start.4 = (f32[16,8,128]{2,1,0:T(8,128)S(1)}, f32[16,8,128]{2,1,0:T(8,128)S(1)}, u32[]{:S(2)}, u32[]{:S(2)}) collective-permute-start(f32[16,8,128]{2,1,0:T(8,128)S(1)} %get-tuple-element.21), channel_id=1, source_target_pairs={{0,256},{256,512},{512,768},{1,257},{257,513},{513,769},{2,258},{2... | collective-permute-start | bytes 196616 | tf_op jit(solution)/shard_map/ppermute | solution.py:41
  37.1 1.3 %collective-permute-start.5 = (f32[16,8,128]{2,1,0:T(8,128)S(1)}, f32[16,8,128]{2,1,0:T(8,128)S(1)}, u32[]{:S(2)}, u32[]{:S(2)}) collective-permute-start(f32[16,8,128]{2,1,0:T(8,128)S(1)} %get-tuple-element.22), channel_id=1, source_target_pairs={{256,0},{512,256},{768,512},{257,1},{513,257},{769,513},{258,2},{5... | collective-permute-start | bytes 196616 | tf_op jit(solution)/shard_map/ppermute | solution.py:42
  38.4 0.6 shard_map.108.coefs
  39.0 0.0 collective-permute-done.4.from_below
  39.0 3.1 %collective-permute-done.5.from_above = f32[16,8,128]{2,1,0:T(8,128)S(1)} collective-permute-done((f32[16,8,128]{2,1,0:T(8,128)S(1)}, f32[16,8,128]{2,1,0:T(8,128)S(1)}, u32[]{:S(2)}, u32[]{:S(2)}) %collective-permute-start.5) | collective-permute-done | bytes 65568 | tf_op jit(solution)/shard_map/ppermute | solution.py:42
  42.1 4.6 %shard_map.109 = (f32[3,8,16,128]{3,2,1,0:T(8,128)S(1)}, f32[6,16,128]{2,1,0:T(8,128)S(1)}, f32[4,16,128]{2,1,0:T(8,128)S(1)}, f32[48,128]{1,0:T(8,128)S(1)}, f32[48,128]{1,0:T(8,128)S(1)}) custom-call(f32[256,8,128]{2,1,0:T(8,128)S(1)} %get-tuple-element.20.main, f32[16,8,128]{2,1,0:T(8,128)S(1)} %collective-permute-done.4.from_below, ...), custom_call_target="tpu_custom_call" | custom-call | tf_op jit(solution)/shard_map/pallas_call | solution.py:53
  46.7 1.9 %collective-permute-start.6 = (f32[48,128]{1,0:T(8,128)S(1)}, f32[48,128]{1,0:T(8,128)S(1)}, u32[]{:S(2)}, u32[]{:S(2)}) collective-permute-start(f32[48,128]{1,0:T(8,128)S(1)} %get-tuple-element.26), channel_id=1, source_target_pairs={{0,1},{1,0},{2,3},{3,2},{4,5},{5,4},{6,7},{7,6},{8,9},{9,8},{10,11... | collective-permute-start | bytes 73736 | tf_op jit(solution)/shard_map/ppermute | solution.py:32
  48.7 3.9 %collective-permute-start.7 = (f32[48,128]{1,0:T(8,128)S(1)}, f32[48,128]{1,0:T(8,128)S(1)}, u32[]{:S(2)}, u32[]{:S(2)}) collective-permute-start(f32[48,128]{1,0:T(8,128)S(1)} %get-tuple-element.27), channel_id=1, source_target_pairs={{1,2},{2,1},{3,4},{4,3},{5,6},{6,5},{7,8},{8,7},{9,10},{10,9},{11,... | collective-permute-start | bytes 73736 | tf_op jit(solution)/shard_map/ppermute | solution.py:33
  52.6 0.7 %copy.11 = f32[3,8,16,128]{3,2,1,0:T(8,128)} copy(f32[3,8,16,128]{3,2,1,0:T(8,128)S(1)} %get-tuple-element.28) | data formatting | bytes 393216
  53.3 0.0 collective-permute-done.6.got_even
  53.3 4.4 %collective-permute-done.7.got_odd = f32[48,128]{1,0:T(8,128)S(1)} collective-permute-done((f32[48,128]{1,0:T(8,128)S(1)}, f32[48,128]{1,0:T(8,128)S(1)}, u32[]{:S(2)}, u32[]{:S(2)}) %collective-permute-start.7) | collective-permute-done | bytes 24608 | tf_op jit(solution)/shard_map/ppermute | solution.py:33
  57.7 0.9 %shard_map.110 = f32[4,8,64]{2,1,0:T(8,128)} custom-call(f32[6,16,128]{2,1,0:T(8,128)S(1)} %get-tuple-element.24.coupled, f32[4,16,128]{2,1,0:T(8,128)S(1)} %get-tuple-element.25.pscale, f32[48,128]{1,0:T(8,128)S(1)} %collective-permute-done.6.got_even, f32[48,128]{1,0:T(8,128)S(1)} %collective-permute-done.7.got_odd, f32[10,8,128]{2,1,0:T(8,128)S(1)} %shard_map.108.coefs), custom_call_target="tpu_custom_call" | custom-call | tf_op jit(solution)/shard_map/pallas_call | solution.py:53
  (10 shorter events, 0.0 us)
Async XLA Ops:
  0.6 26.6 %copy-start = (f32[3,8,16,128]{3,2,1,0:T(8,128)S(1)}, f32[3,8,16,128]{3,2,1,0:T(8,128)}, u32[]{:S(2)}) copy-start(f32[3,8,16,128]{3,2,1,0:T(8,128)} %rhs.3) | copy-start | bytes 589828
  0.6 19.0 %copy-start.6 = (f32[4,8,64]{2,1,0:T(8,128)S(1)}, f32[4,8,64]{2,1,0:T(8,128)}, u32[]{:S(2)}) copy-start(f32[4,8,64]{2,1,0:T(8,128)} %prhs.1) | copy-start | bytes 24580
  0.7 19.0 %copy-start.5 = (f32[4,8,64]{2,1,0:T(8,128)S(1)}, f32[4,8,64]{2,1,0:T(8,128)}, u32[]{:S(2)}) copy-start(f32[4,8,64]{2,1,0:T(8,128)} %pscale.1) | copy-start | bytes 24580
  0.7 26.6 %copy-start.2 = (f32[8,16,128]{2,1,0:T(8,128)S(1)}, f32[8,16,128]{2,1,0:T(8,128)}, u32[]{:S(2)}) copy-start(f32[8,16,128]{2,1,0:T(8,128)} %visc.3) | copy-start | bytes 196612
  0.7 26.6 %copy-start.3 = (f32[8,16,128]{2,1,0:T(8,128)S(1)}, f32[8,16,128]{2,1,0:T(8,128)}, u32[]{:S(2)}) copy-start(f32[8,16,128]{2,1,0:T(8,128)} %mass.3) | copy-start | bytes 196612
  1.7 18.1 %collective-permute-start = (f32[8,16,128]{2,1,0:T(8,128)S(1)}, f32[8,16,128]{2,1,0:T(8,128)S(1)}, u32[]{:S(2)}, u32[]{:S(2)}) collective-permute-start(f32[8,16,128]{2,1,0:T(8,128)S(1)} %get-tuple-element.15), channel_id=1, source_target_pairs={{0,1},{1,0},{2,3},{3,2},{4,5},{5,4},{6,7},{7,6},{8,9},{9,8},{10,11... | collective-permute-start | bytes 196616 | tf_op jit(solution)/shard_map/ppermute | solution.py:32
  17.7 9.5 %collective-permute-start.1 = (f32[8,16,128]{2,1,0:T(8,128)S(1)}, f32[8,16,128]{2,1,0:T(8,128)S(1)}, u32[]{:S(2)}, u32[]{:S(2)}) collective-permute-start(f32[8,16,128]{2,1,0:T(8,128)S(1)} %get-tuple-element.16), channel_id=1, source_target_pairs={{1,2},{2,1},{3,4},{4,3},{5,6},{6,5},{7,8},{8,7},{9,10},{10,9},{11,... | collective-permute-start | bytes 196616 | tf_op jit(solution)/shard_map/ppermute | solution.py:33
  27.3 7.9 %collective-permute-start.2 = (f32[416,128]{1,0:T(8,128)S(1)}, f32[416,128]{1,0:T(8,128)S(1)}, u32[]{:S(2)}, u32[]{:S(2)}) collective-permute-start(f32[416,128]{1,0:T(8,128)S(1)} %get-tuple-element.18), channel_id=1, source_target_pairs={{0,32},{32,64},{64,96},{96,128},{128,160},{160,192},{192,224},{1,3... | collective-permute-start | bytes 638984 | tf_op jit(solution)/shard_map/ppermute | solution.py:41
  28.6 6.6 %collective-permute-start.3 = (f32[360,128]{1,0:T(8,128)S(1)}, f32[360,128]{1,0:T(8,128)S(1)}, u32[]{:S(2)}, u32[]{:S(2)}) collective-permute-start(f32[360,128]{1,0:T(8,128)S(1)} %get-tuple-element.19), channel_id=1, source_target_pairs={{32,0},{64,32},{96,64},{128,96},{160,128},{192,160},{224,192},{33,... | collective-permute-start | bytes 552968 | tf_op jit(solution)/shard_map/ppermute | solution.py:42
  35.2 6.9 %copy-start.1 = (bf16[512,256]{1,0:T(8,128)(2,1)S(1)}, bf16[512,256]{1,0:T(8,128)(2,1)}, u32[]{:S(2)}) copy-start(bf16[512,256]{1,0:T(8,128)(2,1)} %constant.5.clone.ring) | copy-start | bytes 786436
  35.2 6.9 %copy-start.4 = (bf16[512,128]{1,0:T(8,128)(2,1)S(1)}, bf16[512,128]{1,0:T(8,128)(2,1)}, u32[]{:S(2)}) copy-start(bf16[512,128]{1,0:T(8,128)(2,1)} %constant.4.clone.table) | copy-start | bytes 393220
  35.6 2.8 %copy-start.7 = (f32[2]{0:T(128)S(1)}, f32[2]{0:T(128)}, u32[]{:S(2)}) copy-start(f32[2]{0:T(128)} %vbounds.1) | copy-start | bytes 28
  35.6 2.8 %copy-start.8 = (f32[2]{0:T(128)S(1)}, f32[2]{0:T(128)}, u32[]{:S(2)}) copy-start(f32[2]{0:T(128)} %pbounds.1) | copy-start | bytes 28
  35.6 3.3 %collective-permute-start.4 = (f32[16,8,128]{2,1,0:T(8,128)S(1)}, f32[16,8,128]{2,1,0:T(8,128)S(1)}, u32[]{:S(2)}, u32[]{:S(2)}) collective-permute-start(f32[16,8,128]{2,1,0:T(8,128)S(1)} %get-tuple-element.21), channel_id=1, source_target_pairs={{0,256},{256,512},{512,768},{1,257},{257,513},{513,769},{2,258},{2... | collective-permute-start | bytes 196616 | tf_op jit(solution)/shard_map/ppermute | solution.py:41
  37.1 5.0 %collective-permute-start.5 = (f32[16,8,128]{2,1,0:T(8,128)S(1)}, f32[16,8,128]{2,1,0:T(8,128)S(1)}, u32[]{:S(2)}, u32[]{:S(2)}) collective-permute-start(f32[16,8,128]{2,1,0:T(8,128)S(1)} %get-tuple-element.22), channel_id=1, source_target_pairs={{256,0},{512,256},{768,512},{257,1},{513,257},{769,513},{258,2},{5... | collective-permute-start | bytes 196616 | tf_op jit(solution)/shard_map/ppermute | solution.py:42
  46.7 6.5 %collective-permute-start.6 = (f32[48,128]{1,0:T(8,128)S(1)}, f32[48,128]{1,0:T(8,128)S(1)}, u32[]{:S(2)}, u32[]{:S(2)}) collective-permute-start(f32[48,128]{1,0:T(8,128)S(1)} %get-tuple-element.26), channel_id=1, source_target_pairs={{0,1},{1,0},{2,3},{3,2},{4,5},{5,4},{6,7},{7,6},{8,9},{9,8},{10,11... | collective-permute-start | bytes 73736 | tf_op jit(solution)/shard_map/ppermute | solution.py:32
  48.7 9.1 %collective-permute-start.7 = (f32[48,128]{1,0:T(8,128)S(1)}, f32[48,128]{1,0:T(8,128)S(1)}, u32[]{:S(2)}, u32[]{:S(2)}) collective-permute-start(f32[48,128]{1,0:T(8,128)S(1)} %get-tuple-element.27), channel_id=1, source_target_pairs={{1,2},{2,1},{3,4},{4,3},{5,6},{6,5},{7,8},{8,7},{9,10},{10,9},{11,... | collective-permute-start | bytes 73736 | tf_op jit(solution)/shard_map/ppermute | solution.py:33

commit v6 on v5

--- a/solution.py
+++ b/solution.py
@@ -43,7 +43,7 @@
     return from_below, from_above
 
 
-def call(body, outs, scratch=(), smem=(), hbm=(), vmem=()):
+def call(body, outs, scratch=(), smem=(), hbm=(), vmem=(), hbm_out=()):
     def run(*args):
         space = {i: pltpu.SMEM for i in smem} | {i: pltpu.HBM for i in hbm}
         args = [
@@ -55,7 +55,10 @@
             in_specs=[
                 pl.BlockSpec(memory_space=space.get(i, pltpu.VMEM)) for i in range(len(args))
             ],
-            out_specs=[pl.BlockSpec(memory_space=pltpu.VMEM) for _ in outs],
+            out_specs=[
+                pl.BlockSpec(memory_space=pltpu.HBM if i in hbm_out else pltpu.VMEM)
+                for i in range(len(outs))
+            ],
             out_shape=[
                 pltpu.VMEM(o, F32) if i in vmem else jax.ShapeDtypeStruct(o, F32)
                 for i, o in enumerate(outs)
@@ -235,7 +238,7 @@
 def smoothing():
     ring = np.eye(2 * X, dtype=np.float32)
     ring += 0.5 * (np.roll(ring, 1, axis=0) + np.roll(ring, -1, axis=0))
-    return np.concatenate([ring, ring]).astype(ml_dtypes.bfloat16)
+    return np.concatenate([ring[:X], ring[:X], ring[X:], ring[X:]]).astype(ml_dtypes.bfloat16)
 
 
 def split(value, parts):
@@ -250,8 +253,47 @@
     return lax.dot_general(a, b, (((1,), (0,)), ((), ())), preferred_element_type=F32)
 
 
+def planes(ref, p):
+    return ref[pl.ds(4 * p, 4)].reshape(32, X)
+
+
+def loop(start, count, body):
+    def step(z, _):
+        body(z)
+        return 0
+
+    lax.fori_loop(start, start + count, step, 0)
+
+
+def weigh(src, w, c):
+    def body(z):
+        w[z] = planes(src, S0 + z) * planes(src, c * ZW + z)
+
+    loop(0, ZW, body)
+
+
+def sum_rows(w, t, lhs, first_row, col, z0, count):
+    def body(z):
+        v = w[z] + 0.5 * (w[z - 1] + w[z + 1])
+        t[8:40] = v
+        v = v + 0.5 * (t[7:39] + t[9:41])
+        at = pl.ds(first_row + (z - z0) * 32, 32)
+        for part, value in enumerate(split(v, 2)):
+            lhs[at, col + part * X : col + (part + 1) * X] = value
+
+    loop(z0, count, body)
+
+
+def first_sums(main, ring, sums, w, t, lhs):
+    t[...] = jnp.zeros_like(t)
+    for c in range(3):
+        weigh(main, w, c)
+        sum_rows(w, t, lhs, c * (Z + 2) * 32, 0, 1, Z + 2)
+    sums[...] = dot(lhs[...], ring[: 2 * X])
+
+
 def velocity_step(
-    main, from_below, from_above, table, ring, coefs, vel, coupled, pscale, msg_even, msg_odd,
+    main, from_below, from_above, table, ring, sums, coefs, vel, coupled, pscale, msg_even, msg_odd,
     halo, w, d, r, u, t, lhs, s, g, q, ptmp,
 ):
     lane = lanes()
@@ -262,68 +304,49 @@
 
     inv, a1, g1, a2, g2 = (tall(coefs[i], 32) for i in range(5))
     t[...] = jnp.zeros_like(t)
-
-    def planes(ref, p):
-        return ref[pl.ds(4 * p, 4)].reshape(32, X)
-
-    def smooth(k, z0, count):
-        for c in range(3):
-            def rows(z, _):
-                for h in range(2):
-                    src = w.at[k, c, h]
-                    v = src[z] + 0.5 * (src[z - 1] + src[z + 1])
-                    t[h, 8:40] = v
-                    v = v + 0.5 * (t[h, 7:39] + t[h, 9:41])
-                    at = pl.ds((c * count + z - z0) * 32, 32)
-                    for part, value in enumerate(split(v, 2)):
-                        lhs[at, (2 * part + h) * X : (2 * part + h + 1) * X] = value
-                return 0
-
-            lax.fori_loop(z0, z0 + count, rows, 0)
-        total = 3 * count * 32
-        s[:total] = dot(lhs[:total], ring[...])
+    both = (main, halo)
 
     for c in range(3):
-        def weight(z, _):
-            for h, src in enumerate((main, halo)):
-                w[0, c, h, z] = planes(src, S0 + z) * (planes(src, c * ZW + z) * inv)
-            return 0
-
-        lax.fori_loop(0, ZW, weight, 0)
-
-    smooth(0, 1, Z + 2)
+        weigh(halo, w.at[c, 1], c)
+        sum_rows(w.at[c, 1], t.at[1], lhs, c * (Z + 2) * 32, 2 * X, 1, Z + 2)
+    s[...] = dot(lhs[:, 2 * X :], ring[2 * X :])
+
     for c in range(3):
-        def sweep1(z, _):
+        def sweep1(z):
             at = pl.ds((c * (Z + 2) + z - 1) * 32, 32)
-            for h, src in enumerate((main, halo)):
+            for h, src in enumerate(both):
+                cols = slice(h * X, (h + 1) * X)
                 b = planes(src, c * ZW + z)
                 visc = planes(src, S0 + z)
                 d0 = b * inv
-                lap = 16.0 * w[0, c, h, z] - 2.0 * s[at, h * X : (h + 1) * X]
+                lap = 16.0 * (visc * d0) - (2.0 * inv) * (sums[at, cols] + s[at, cols])
                 res = b - (visc * lap + planes(src, M0 + z - 1) * d0)
                 d1 = a1 * d0 + g1 * res
                 r[c, h, z] = res
                 d[c, h, z] = d1
-                w[1, c, h, z] = visc * d1
-            return 0
-
-        lax.fori_loop(1, ZW - 1, sweep1, 0)
-
-    smooth(1, 2, Z)
+                w[c, h, z] = visc * d1
+
+        loop(1, Z + 2, sweep1)
+
     for c in range(3):
-        def sweep2(z, _):
+        for h in range(2):
+            sum_rows(w.at[c, h], t.at[h], lhs, c * Z * 32, 2 * h * X, 2, Z)
+    total = 3 * Z * 32
+    s[:total] = dot(lhs[:total], ring[...])
+
+    for c in range(3):
+        def sweep2(z):
             at = pl.ds((c * Z + z - 2) * 32, 32)
-            for h, src in enumerate((main, halo)):
+            for h, src in enumerate(both):
                 d1 = d[c, h, z]
-                lap = 16.0 * w[1, c, h, z] - 2.0 * s[at, h * X : (h + 1) * X]
+                lap = 16.0 * w[c, h, z] - 2.0 * s[at, h * X : (h + 1) * X]
                 res = r[c, h, z] - (planes(src, S0 + z) * lap + planes(src, M0 + z - 1) * d1)
-                total = planes(src, c * ZW + z) * inv + d1 + (a2 * d1 + g2 * res)
-                u[c, h, z - 2] = total
+                value = planes(src, c * ZW + z) * inv + d1 + (a2 * d1 + g2 * res)
+                u[c, h, z - 2] = value
                 if h == 0:
-                    vel[c, z - 2] = total[8:24]
-            return 0
-
-        lax.fori_loop(2, ZW - 2, sweep2, 0)
+                    vel[c, z - 2] = value[8:24]
+
+        loop(2, Z, sweep2)
 
     q[...] = jnp.zeros_like(q)
     for node in range(-1, 5):
@@ -376,7 +399,9 @@
             out[12 * j : 12 * j + 12] = part[:12]
 
 
-def pressure_step(coupled, pscale, got_even, got_odd, coefs, out, halo):
+def pressure_step(coupled, pscale, got_even, got_odd, coefs, vel, vel_out, out, halo, sem):
+    write = pltpu.make_async_copy(vel, vel_out, sem)
+    write.start()
     even = parity("gz") == 0
     halo[...] = jnp.zeros_like(halo)
     for i in range(4):
@@ -410,6 +435,7 @@
         total = d0[z] + d1[z] + (a2 * d1[z] + g2 * res)
         total = pltpu.roll(pltpu.roll(total, 14, axis=0), X - 2, axis=1)
         out[z - 2] = total[:PY, :PX]
+    write.wait()
 
 
 def per_device(rhs, prhs, visc, mass, pscale, vbounds, pbounds):
@@ -431,29 +457,42 @@
         own, pt, below, above
     )
     below, above = both_neighbours("gx", up, down)
+    ring = jnp.asarray(smoothing())
+    rows = 3 * (Z + 2) * 32
+    (sums,) = call(
+        first_sums,
+        [(rows, 2 * X)],
+        scratch=[
+            pltpu.VMEM((ZW, 32, X), F32),
+            pltpu.VMEM((48, X), F32),
+            pltpu.VMEM((rows, 2 * X), jnp.bfloat16),
+        ],
+    )(main, ring)
     vel, coupled, scale, msg_even, msg_odd = call(
         velocity_step,
         [(3, Z, Y, X), (6, *plane), (PZ, *plane), (48, X), (48, X)],
         vmem=(0,),
         scratch=[
             pltpu.VMEM((TILES, 8, X), F32),
-            pltpu.VMEM((2, 3, 2, ZW, 32, X), F32),
+            pltpu.VMEM((3, 2, ZW, 32, X), F32),
             pltpu.VMEM((3, 2, ZW, 32, X), F32),
             pltpu.VMEM((3, 2, ZW, 32, X), F32),
             pltpu.VMEM((3, 2, Z, 32, X), F32),
             pltpu.VMEM((2, 48, X), F32),
-            pltpu.VMEM((3 * (Z + 2) * 32, 4 * X), jnp.bfloat16),
-            pltpu.VMEM((3 * (Z + 2) * 32, 2 * X), F32),
+            pltpu.VMEM((rows, 4 * X), jnp.bfloat16),
+            pltpu.VMEM((rows, 2 * X), F32),
             pltpu.VMEM((3, 32, X), F32),
             pltpu.VMEM((96, 4 * X), F32),
             pltpu.VMEM((24, X), F32),
         ],
-    )(main, below, above, jnp.asarray(restriction()), jnp.asarray(smoothing()), coefs)
+    )(main, below, above, jnp.asarray(restriction()), ring, sums, coefs)
     z_halos = swap_neighbours("gz", msg_even, msg_odd)
-    (pressure,) = call(
-        pressure_step, [(PZ, PY, PX)], scratch=[pltpu.VMEM((2, 4, *plane), F32)]
-    )(coupled, scale, *z_halos, coefs)
-    return vel, pressure
+    return call(
+        pressure_step,
+        [(3, Z, Y, X), (PZ, PY, PX)],
+        scratch=[pltpu.VMEM((2, 4, *plane), F32), pltpu.SemaphoreType.DMA],
+        hbm_out=(0,),
+    )(coupled, scale, *z_halos, coefs, vel)
 
 
 def solution(mesh):

time: 59 us -> 59.4 us (level)
  Pallas kernels: 7.65 us -> 9.16 us
  local copies, waits for them, and re-layouts: 0.72 us -> 0.04 us
    pallas_call x7 -> x8, Pallas kernels: 7.65 us -> 9.16 us  [run(): pl.pallas_call(body, in_specs=[pl.BlockSpec(memory_space=space.get(i, plt...]
    ppermute x2, waiting for transfers between devices: 8.38 us -> 7.28 us  [both_neighbours(): from_above = lax.ppermute(to_below, axis, down)]
    unnamed x19 -> x18, local copies, waits for them, and re-layouts: 0.72 us -> 0.04 us
    ppermute x2, waiting for transfers between devices: 11.9 us -> 12.6 us  [swap_neighbours(): outer = lax.ppermute(second, axis, odd)]
  transfers between devices with their start and end apart: 8 -> 8, of which waited for: 4 -> 4; matrix products, arithmetic and copies ran while one was open for 1% -> 0% of each run, Pallas kernels for 1% -> 3%
where the time goes in v6:
time: 59.4 us; the launch traced here: 59 us
  starting transfers between devices  29.1 us (49%)
  waiting for transfers between devices  19.9 us (34%)
  Pallas kernels  9.16 us (15%)
  between operations  0.86 us (1%)
    ppermute x2, starting transfers between devices, swap_neighbours(): inner = lax.ppermute(first, axis, even)  17.9 us
    ppermute x2, waiting for transfers between devices, swap_neighbours(): outer = lax.ppermute(second, axis, odd)  12.6 us
    pallas_call x8, Pallas kernels, run(): pl.pallas_call(body, in_specs=[pl.BlockSpec(memory_space=space.get(i, plt...  9.16 us
    ppermute x2, waiting for transfers between devices, both_neighbours(): from_above = lax.ppermute(to_below, axis, down)  7.28 us
    ppermute x2, starting transfers between devices, swap_neighbours(): outer = lax.ppermute(second, axis, odd)  5.85 us
    ppermute x2, starting transfers between devices, both_neighbours(): from_below = lax.ppermute(to_above, axis, up)  2.73 us
    ppermute x2, starting transfers between devices, both_neighbours(): from_above = lax.ppermute(to_below, axis, down)  2.58 us
  transfers between devices with their start and end apart: 8, of which 4 were waited for; matrix products, arithmetic and copies ran while one was open for 0% of the time, Pallas kernels for 3%

profile of v6, /device:TPU:1, one launch (start us, length us, event | category | flops | bytes accessed | tf_op | source)
XLA Modules:
  0.0 59.0 jit_solution(1808739723471847555)
XLA Ops:
  0.6 0.0 copy-start.1
  0.6 0.0 copy-start.5
  0.7 0.0 copy-start.6
  0.7 1.0 %shard_map.104 = (f32[8,16,128]{2,1,0:T(8,128)S(1)}, f32[8,16,128]{2,1,0:T(8,128)S(1)}) custom-call(f32[3,8,16,128]{3,2,1,0:T(8,128)} %rhs.3, f32[8,16,128]{2,1,0:T(8,128)} %visc.3, f32[8,16,128]{2,1,0:T(8,128)} %mass.3), custom_call_target="tpu_custom_call" | custom-call | tf_op jit(solution)/shard_map/pallas_call | solution.py:53
  1.7 16.0 %collective-permute-start = (f32[8,16,128]{2,1,0:T(8,128)S(1)}, f32[8,16,128]{2,1,0:T(8,128)S(1)}, u32[]{:S(2)}, u32[]{:S(2)}) collective-permute-start(f32[8,16,128]{2,1,0:T(8,128)S(1)} %get-tuple-element.15), channel_id=1, source_target_pairs={{0,1},{1,0},{2,3},{3,2},{4,5},{5,4},{6,7},{7,6},{8,9},{9,8},{10,11... | collective-permute-start | bytes 196616 | tf_op jit(solution)/shard_map/ppermute | solution.py:32
  17.7 1.9 %collective-permute-start.1 = (f32[8,16,128]{2,1,0:T(8,128)S(1)}, f32[8,16,128]{2,1,0:T(8,128)S(1)}, u32[]{:S(2)}, u32[]{:S(2)}) collective-permute-start(f32[8,16,128]{2,1,0:T(8,128)S(1)} %get-tuple-element.16), channel_id=1, source_target_pairs={{1,2},{2,1},{3,4},{4,3},{5,6},{6,5},{7,8},{8,7},{9,10},{10,9},{11,... | collective-permute-start | bytes 196616 | tf_op jit(solution)/shard_map/ppermute | solution.py:33
  19.7 0.1 shard_map.105.pt
  19.8 0.0 collective-permute-done.got_even
  19.8 7.5 %collective-permute-done.1.got_odd = f32[8,16,128]{2,1,0:T(8,128)S(1)} collective-permute-done((f32[8,16,128]{2,1,0:T(8,128)S(1)}, f32[8,16,128]{2,1,0:T(8,128)S(1)}, u32[]{:S(2)}, u32[]{:S(2)}) %collective-permute-start.1) | collective-permute-done | bytes 65568 | tf_op jit(solution)/shard_map/ppermute | solution.py:33
  27.2 0.1 shard_map.106
  27.3 1.3 %collective-permute-start.2 = (f32[416,128]{1,0:T(8,128)S(1)}, f32[416,128]{1,0:T(8,128)S(1)}, u32[]{:S(2)}, u32[]{:S(2)}) collective-permute-start(f32[416,128]{1,0:T(8,128)S(1)} %get-tuple-element.18), channel_id=1, source_target_pairs={{0,32},{32,64},{64,96},{96,128},{128,160},{160,192},{192,224},{1,3... | collective-permute-start | bytes 638984 | tf_op jit(solution)/shard_map/ppermute | solution.py:41
  28.6 1.3 %collective-permute-start.3 = (f32[360,128]{1,0:T(8,128)S(1)}, f32[360,128]{1,0:T(8,128)S(1)}, u32[]{:S(2)}, u32[]{:S(2)}) collective-permute-start(f32[360,128]{1,0:T(8,128)S(1)} %get-tuple-element.19), channel_id=1, source_target_pairs={{32,0},{64,32},{96,64},{128,96},{160,128},{192,160},{224,192},{33,... | collective-permute-start | bytes 552968 | tf_op jit(solution)/shard_map/ppermute | solution.py:42
  29.9 5.3 %collective-permute-done.3.above = f32[360,128]{1,0:T(8,128)S(1)} collective-permute-done((f32[360,128]{1,0:T(8,128)S(1)}, f32[360,128]{1,0:T(8,128)S(1)}, u32[]{:S(2)}, u32[]{:S(2)}) %collective-permute-start.3) | collective-permute-done | bytes 184352 | tf_op jit(solution)/shard_map/ppermute | solution.py:42
  35.2 0.0 collective-permute-done.2.below
  35.2 0.4 shard_map.107
  35.6 0.0 copy-start.7
  35.6 0.0 copy-start.8
  35.6 1.4 %collective-permute-start.4 = (f32[16,8,128]{2,1,0:T(8,128)S(1)}, f32[16,8,128]{2,1,0:T(8,128)S(1)}, u32[]{:S(2)}, u32[]{:S(2)}) collective-permute-start(f32[16,8,128]{2,1,0:T(8,128)S(1)} %get-tuple-element.21), channel_id=1, source_target_pairs={{0,256},{256,512},{512,768},{1,257},{257,513},{513,769},{2,258},{2... | collective-permute-start | bytes 196616 | tf_op jit(solution)/shard_map/ppermute | solution.py:41
  37.1 1.3 %collective-permute-start.5 = (f32[16,8,128]{2,1,0:T(8,128)S(1)}, f32[16,8,128]{2,1,0:T(8,128)S(1)}, u32[]{:S(2)}, u32[]{:S(2)}) collective-permute-start(f32[16,8,128]{2,1,0:T(8,128)S(1)} %get-tuple-element.22), channel_id=1, source_target_pairs={{256,0},{512,256},{768,512},{257,1},{513,257},{769,513},{258,2},{5... | collective-permute-start | bytes 196616 | tf_op jit(solution)/shard_map/ppermute | solution.py:42
  38.4 0.0 copy-done.7
  38.4 0.0 copy-done.8
  38.4 0.6 shard_map.109.coefs
  39.0 0.0 copy-start.4
  39.0 1.1 %shard_map.108.sums = f32[960,256]{1,0:T(8,128)S(1)} custom-call(f32[256,8,128]{2,1,0:T(8,128)S(1)} %get-tuple-element.20.main, bf16[512,256]{1,0:T(8,128)(2,1)S(1)} %copy-done), custom_call_target="tpu_custom_call" | custom-call | tf_op jit(solution)/shard_map/pallas_call | solution.py:53
  40.1 0.0 collective-permute-done.4.from_below
  40.1 2.0 %collective-permute-done.5.from_above = f32[16,8,128]{2,1,0:T(8,128)S(1)} collective-permute-done((f32[16,8,128]{2,1,0:T(8,128)S(1)}, f32[16,8,128]{2,1,0:T(8,128)S(1)}, u32[]{:S(2)}, u32[]{:S(2)}) %collective-permute-start.5) | collective-permute-done | bytes 65568 | tf_op jit(solution)/shard_map/ppermute | solution.py:42
  42.1 4.7 %shard_map.110 = (f32[3,8,16,128]{3,2,1,0:T(8,128)S(1)}, f32[6,16,128]{2,1,0:T(8,128)S(1)}, f32[4,16,128]{2,1,0:T(8,128)S(1)}, f32[48,128]{1,0:T(8,128)S(1)}, f32[48,128]{1,0:T(8,128)S(1)}) custom-call(f32[256,8,128]{2,1,0:T(8,128)S(1)} %get-tuple-element.20.main, f32[16,8,128]{2,1,0:T(8,128)S(1)} %collective-permute-done.4.from_below, ...), custom_call_target="tpu_custom_call" | custom-call | tf_op jit(solution)/shard_map/pallas_call | solution.py:53
  46.8 1.9 %collective-permute-start.6 = (f32[48,128]{1,0:T(8,128)S(1)}, f32[48,128]{1,0:T(8,128)S(1)}, u32[]{:S(2)}, u32[]{:S(2)}) collective-permute-start(f32[48,128]{1,0:T(8,128)S(1)} %get-tuple-element.25), channel_id=1, source_target_pairs={{0,1},{1,0},{2,3},{3,2},{4,5},{5,4},{6,7},{7,6},{8,9},{9,8},{10,11... | collective-permute-start | bytes 73736 | tf_op jit(solution)/shard_map/ppermute | solution.py:32
  48.7 3.9 %collective-permute-start.7 = (f32[48,128]{1,0:T(8,128)S(1)}, f32[48,128]{1,0:T(8,128)S(1)}, u32[]{:S(2)}, u32[]{:S(2)}) collective-permute-start(f32[48,128]{1,0:T(8,128)S(1)} %get-tuple-element.26), channel_id=1, source_target_pairs={{1,2},{2,1},{3,4},{4,3},{5,6},{6,5},{7,8},{8,7},{9,10},{10,9},{11,... | collective-permute-start | bytes 73736 | tf_op jit(solution)/shard_map/ppermute | solution.py:33
  52.6 0.0 collective-permute-done.6.got_even
  52.6 5.1 %collective-permute-done.7.got_odd = f32[48,128]{1,0:T(8,128)S(1)} collective-permute-done((f32[48,128]{1,0:T(8,128)S(1)}, f32[48,128]{1,0:T(8,128)S(1)}, u32[]{:S(2)}, u32[]{:S(2)}) %collective-permute-start.7) | collective-permute-done | bytes 24608 | tf_op jit(solution)/shard_map/ppermute | solution.py:33
  57.7 1.3 %shard_map.111 = (f32[3,8,16,128]{3,2,1,0:T(8,128)}, f32[4,8,64]{2,1,0:T(8,128)}) custom-call(f32[6,16,128]{2,1,0:T(8,128)S(1)} %get-tuple-element.23.coupled, f32[4,16,128]{2,1,0:T(8,128)S(1)} %get-tuple-element.24.pscale, f32[48,128]{1,0:T(8,128)S(1)} %collective-permute-done.6.got_even, f32[48,128]{1,0:T(8,128)S(1)} %collective-permute-done.7.got_odd, ...), custom_call_target="tpu_custom_call" | custom-call | tf_op jit(solution)/shard_map/pallas_call | solution.py:53
  (10 shorter events, 0.0 us)
Async XLA Ops:
  0.6 26.6 %copy-start.1 = (f32[3,8,16,128]{3,2,1,0:T(8,128)S(1)}, f32[3,8,16,128]{3,2,1,0:T(8,128)}, u32[]{:S(2)}) copy-start(f32[3,8,16,128]{3,2,1,0:T(8,128)} %rhs.3) | copy-start | bytes 589828
  0.6 19.0 %copy-start.5 = (f32[4,8,64]{2,1,0:T(8,128)S(1)}, f32[4,8,64]{2,1,0:T(8,128)}, u32[]{:S(2)}) copy-start(f32[4,8,64]{2,1,0:T(8,128)} %pscale.1) | copy-start | bytes 24580
  0.7 19.0 %copy-start.6 = (f32[4,8,64]{2,1,0:T(8,128)S(1)}, f32[4,8,64]{2,1,0:T(8,128)}, u32[]{:S(2)}) copy-start(f32[4,8,64]{2,1,0:T(8,128)} %prhs.1) | copy-start | bytes 24580
  0.7 26.6 %copy-start.2 = (f32[8,16,128]{2,1,0:T(8,128)S(1)}, f32[8,16,128]{2,1,0:T(8,128)}, u32[]{:S(2)}) copy-start(f32[8,16,128]{2,1,0:T(8,128)} %visc.3) | copy-start | bytes 196612
  0.7 26.6 %copy-start.3 = (f32[8,16,128]{2,1,0:T(8,128)S(1)}, f32[8,16,128]{2,1,0:T(8,128)}, u32[]{:S(2)}) copy-start(f32[8,16,128]{2,1,0:T(8,128)} %mass.3) | copy-start | bytes 196612
  1.7 18.1 %collective-permute-start = (f32[8,16,128]{2,1,0:T(8,128)S(1)}, f32[8,16,128]{2,1,0:T(8,128)S(1)}, u32[]{:S(2)}, u32[]{:S(2)}) collective-permute-start(f32[8,16,128]{2,1,0:T(8,128)S(1)} %get-tuple-element.15), channel_id=1, source_target_pairs={{0,1},{1,0},{2,3},{3,2},{4,5},{5,4},{6,7},{7,6},{8,9},{9,8},{10,11... | collective-permute-start | bytes 196616 | tf_op jit(solution)/shard_map/ppermute | solution.py:32
  17.7 9.5 %collective-permute-start.1 = (f32[8,16,128]{2,1,0:T(8,128)S(1)}, f32[8,16,128]{2,1,0:T(8,128)S(1)}, u32[]{:S(2)}, u32[]{:S(2)}) collective-permute-start(f32[8,16,128]{2,1,0:T(8,128)S(1)} %get-tuple-element.16), channel_id=1, source_target_pairs={{1,2},{2,1},{3,4},{4,3},{5,6},{6,5},{7,8},{8,7},{9,10},{10,9},{11,... | collective-permute-start | bytes 196616 | tf_op jit(solution)/shard_map/ppermute | solution.py:33
  27.3 7.9 %collective-permute-start.2 = (f32[416,128]{1,0:T(8,128)S(1)}, f32[416,128]{1,0:T(8,128)S(1)}, u32[]{:S(2)}, u32[]{:S(2)}) collective-permute-start(f32[416,128]{1,0:T(8,128)S(1)} %get-tuple-element.18), channel_id=1, source_target_pairs={{0,32},{32,64},{64,96},{96,128},{128,160},{160,192},{192,224},{1,3... | collective-permute-start | bytes 638984 | tf_op jit(solution)/shard_map/ppermute | solution.py:41
  28.6 6.6 %collective-permute-start.3 = (f32[360,128]{1,0:T(8,128)S(1)}, f32[360,128]{1,0:T(8,128)S(1)}, u32[]{:S(2)}, u32[]{:S(2)}) collective-permute-start(f32[360,128]{1,0:T(8,128)S(1)} %get-tuple-element.19), channel_id=1, source_target_pairs={{32,0},{64,32},{96,64},{128,96},{160,128},{192,160},{224,192},{33,... | collective-permute-start | bytes 552968 | tf_op jit(solution)/shard_map/ppermute | solution.py:42
  35.2 3.8 %copy-start = (bf16[512,256]{1,0:T(8,128)(2,1)S(1)}, bf16[512,256]{1,0:T(8,128)(2,1)}, u32[]{:S(2)}) copy-start(bf16[512,256]{1,0:T(8,128)(2,1)} %constant.4.clone.ring) | copy-start | bytes 786436
  35.6 2.8 %copy-start.7 = (f32[2]{0:T(128)S(1)}, f32[2]{0:T(128)}, u32[]{:S(2)}) copy-start(f32[2]{0:T(128)} %vbounds.1) | copy-start | bytes 28
  35.6 2.8 %copy-start.8 = (f32[2]{0:T(128)S(1)}, f32[2]{0:T(128)}, u32[]{:S(2)}) copy-start(f32[2]{0:T(128)} %pbounds.1) | copy-start | bytes 28
  35.6 4.4 %collective-permute-start.4 = (f32[16,8,128]{2,1,0:T(8,128)S(1)}, f32[16,8,128]{2,1,0:T(8,128)S(1)}, u32[]{:S(2)}, u32[]{:S(2)}) collective-permute-start(f32[16,8,128]{2,1,0:T(8,128)S(1)} %get-tuple-element.21), channel_id=1, source_target_pairs={{0,256},{256,512},{512,768},{1,257},{257,513},{513,769},{2,258},{2... | collective-permute-start | bytes 196616 | tf_op jit(solution)/shard_map/ppermute | solution.py:41
  37.1 5.0 %collective-permute-start.5 = (f32[16,8,128]{2,1,0:T(8,128)S(1)}, f32[16,8,128]{2,1,0:T(8,128)S(1)}, u32[]{:S(2)}, u32[]{:S(2)}) collective-permute-start(f32[16,8,128]{2,1,0:T(8,128)S(1)} %get-tuple-element.22), channel_id=1, source_target_pairs={{256,0},{512,256},{768,512},{257,1},{513,257},{769,513},{258,2},{5... | collective-permute-start | bytes 196616 | tf_op jit(solution)/shard_map/ppermute | solution.py:42
  39.0 3.1 %copy-start.4 = (bf16[512,128]{1,0:T(8,128)(2,1)S(1)}, bf16[512,128]{1,0:T(8,128)(2,1)}, u32[]{:S(2)}) copy-start(bf16[512,128]{1,0:T(8,128)(2,1)} %constant.5.clone.table) | copy-start | bytes 393220
  46.8 5.9 %collective-permute-start.6 = (f32[48,128]{1,0:T(8,128)S(1)}, f32[48,128]{1,0:T(8,128)S(1)}, u32[]{:S(2)}, u32[]{:S(2)}) collective-permute-start(f32[48,128]{1,0:T(8,128)S(1)} %get-tuple-element.25), channel_id=1, source_target_pairs={{0,1},{1,0},{2,3},{3,2},{4,5},{5,4},{6,7},{7,6},{8,9},{9,8},{10,11... | collective-permute-start | bytes 73736 | tf_op jit(solution)/shard_map/ppermute | solution.py:32
  48.7 9.1 %collective-permute-start.7 = (f32[48,128]{1,0:T(8,128)S(1)}, f32[48,128]{1,0:T(8,128)S(1)}, u32[]{:S(2)}, u32[]{:S(2)}) collective-permute-start(f32[48,128]{1,0:T(8,128)S(1)} %get-tuple-element.26), channel_id=1, source_target_pairs={{1,2},{2,1},{3,4},{4,3},{5,6},{6,5},{7,8},{8,7},{9,10},{10,9},{11,... | collective-permute-start | bytes 73736 | tf_op jit(solution)/shard_map/ppermute | solution.py:33

commit v7 on v6

--- a/solution.py
+++ b/solution.py
@@ -43,7 +43,7 @@
     return from_below, from_above
 
 
-def call(body, outs, scratch=(), smem=(), hbm=(), vmem=(), hbm_out=()):
+def call(body, outs, scratch=(), smem=(), hbm=(), vmem=()):
     def run(*args):
         space = {i: pltpu.SMEM for i in smem} | {i: pltpu.HBM for i in hbm}
         args = [
@@ -55,10 +55,7 @@
             in_specs=[
                 pl.BlockSpec(memory_space=space.get(i, pltpu.VMEM)) for i in range(len(args))
             ],
-            out_specs=[
-                pl.BlockSpec(memory_space=pltpu.HBM if i in hbm_out else pltpu.VMEM)
-                for i in range(len(outs))
-            ],
+            out_specs=[pl.BlockSpec(memory_space=pltpu.VMEM) for _ in outs],
             out_shape=[
                 pltpu.VMEM(o, F32) if i in vmem else jax.ShapeDtypeStruct(o, F32)
                 for i, o in enumerate(outs)
@@ -257,38 +254,45 @@
     return ref[pl.ds(4 * p, 4)].reshape(32, X)
 
 
-def loop(start, count, body):
-    def step(z, _):
-        body(z)
+def loop(start, count, body, each=1):
+    def step(i, _):
+        body([start + each * i + j for j in range(each)])
         return 0
 
-    lax.fori_loop(start, start + count, step, 0)
-
-
-def weigh(src, w, c):
-    def body(z):
-        w[z] = planes(src, S0 + z) * planes(src, c * ZW + z)
-
-    loop(0, ZW, body)
-
-
-def sum_rows(w, t, lhs, first_row, col, z0, count):
-    def body(z):
-        v = w[z] + 0.5 * (w[z - 1] + w[z + 1])
-        t[8:40] = v
-        v = v + 0.5 * (t[7:39] + t[9:41])
-        at = pl.ds(first_row + (z - z0) * 32, 32)
-        for part, value in enumerate(split(v, 2)):
-            lhs[at, col + part * X : col + (part + 1) * X] = value
-
-    loop(z0, count, body)
+    lax.fori_loop(0, count // each, step, 0)
+
+
+def weigh(src, w):
+    def body(zs):
+        for z in zs:
+            visc = planes(src, S0 + z)
+            for c in range(3):
+                w[c, z] = visc * planes(src, c * ZW + z)
+
+    loop(0, ZW, body, 3)
+
+
+def sum_rows(chains, t, lhs, z0, count):
+    def body(zs):
+        work = [(z, *chain) for z in zs for chain in chains]
+        first = []
+        for i, (z, c, w, col) in enumerate(work):
+            v = w[z] + 0.5 * (w[z - 1] + w[z + 1])
+            t[i, 8:40] = v
+            first.append(v)
+        for i, (z, c, w, col) in enumerate(work):
+            v = first[i] + 0.5 * (t[i, 7:39] + t[i, 9:41])
+            at = pl.ds((c * count + z - z0) * 32, 32)
+            for part, value in enumerate(split(v, 2)):
+                lhs[at, col + part * X : col + (part + 1) * X] = value
+
+    loop(z0, count, body, 6 // len(chains))
 
 
 def first_sums(main, ring, sums, w, t, lhs):
     t[...] = jnp.zeros_like(t)
-    for c in range(3):
-        weigh(main, w, c)
-        sum_rows(w, t, lhs, c * (Z + 2) * 32, 0, 1, Z + 2)
+    weigh(main, w)
+    sum_rows([(c, w.at[c], 0) for c in range(3)], t, lhs, 1, Z + 2)
     sums[...] = dot(lhs[...], ring[: 2 * X])
 
 
@@ -306,47 +310,47 @@
     t[...] = jnp.zeros_like(t)
     both = (main, halo)
 
-    for c in range(3):
-        weigh(halo, w.at[c, 1], c)
-        sum_rows(w.at[c, 1], t.at[1], lhs, c * (Z + 2) * 32, 2 * X, 1, Z + 2)
+    weigh(halo, w.at[1])
+    sum_rows([(c, w.at[1, c], 2 * X) for c in range(3)], t, lhs, 1, Z + 2)
     s[...] = dot(lhs[:, 2 * X :], ring[2 * X :])
 
-    for c in range(3):
-        def sweep1(z):
-            at = pl.ds((c * (Z + 2) + z - 1) * 32, 32)
-            for h, src in enumerate(both):
-                cols = slice(h * X, (h + 1) * X)
+    def sweep1(zs):
+        (z,) = zs
+        for h, src in enumerate(both):
+            visc, mass = planes(src, S0 + z), planes(src, M0 + z - 1)
+            cols = slice(h * X, (h + 1) * X)
+            for c in range(3):
+                at = pl.ds((c * (Z + 2) + z - 1) * 32, 32)
                 b = planes(src, c * ZW + z)
-                visc = planes(src, S0 + z)
                 d0 = b * inv
                 lap = 16.0 * (visc * d0) - (2.0 * inv) * (sums[at, cols] + s[at, cols])
-                res = b - (visc * lap + planes(src, M0 + z - 1) * d0)
+                res = b - (visc * lap + mass * d0)
                 d1 = a1 * d0 + g1 * res
-                r[c, h, z] = res
-                d[c, h, z] = d1
-                w[c, h, z] = visc * d1
-
-        loop(1, Z + 2, sweep1)
-
-    for c in range(3):
-        for h in range(2):
-            sum_rows(w.at[c, h], t.at[h], lhs, c * Z * 32, 2 * h * X, 2, Z)
+                r[h, c, z] = res
+                d[h, c, z] = d1
+                w[h, c, z] = visc * d1
+
+    loop(1, Z + 2, sweep1)
+
+    sum_rows([(c, w.at[h, c], 2 * h * X) for h in range(2) for c in range(3)], t, lhs, 2, Z)
     total = 3 * Z * 32
     s[:total] = dot(lhs[:total], ring[...])
 
-    for c in range(3):
-        def sweep2(z):
-            at = pl.ds((c * Z + z - 2) * 32, 32)
-            for h, src in enumerate(both):
-                d1 = d[c, h, z]
-                lap = 16.0 * w[c, h, z] - 2.0 * s[at, h * X : (h + 1) * X]
-                res = r[c, h, z] - (planes(src, S0 + z) * lap + planes(src, M0 + z - 1) * d1)
+    def sweep2(zs):
+        (z,) = zs
+        for h, src in enumerate(both):
+            visc, mass = planes(src, S0 + z), planes(src, M0 + z - 1)
+            for c in range(3):
+                at = pl.ds((c * Z + z - 2) * 32, 32)
+                d1 = d[h, c, z]
+                lap = 16.0 * w[h, c, z] - 2.0 * s[at, h * X : (h + 1) * X]
+                res = r[h, c, z] - (visc * lap + mass * d1)
                 value = planes(src, c * ZW + z) * inv + d1 + (a2 * d1 + g2 * res)
                 u[c, h, z - 2] = value
                 if h == 0:
                     vel[c, z - 2] = value[8:24]
 
-        loop(2, Z, sweep2)
+    loop(2, Z, sweep2)
 
     q[...] = jnp.zeros_like(q)
     for node in range(-1, 5):
@@ -399,9 +403,7 @@
             out[12 * j : 12 * j + 12] = part[:12]
 
 
-def pressure_step(coupled, pscale, got_even, got_odd, coefs, vel, vel_out, out, halo, sem):
-    write = pltpu.make_async_copy(vel, vel_out, sem)
-    write.start()
+def pressure_step(coupled, pscale, got_even, got_odd, coefs, out, halo):
     even = parity("gz") == 0
     halo[...] = jnp.zeros_like(halo)
     for i in range(4):
@@ -435,7 +437,6 @@
         total = d0[z] + d1[z] + (a2 * d1[z] + g2 * res)
         total = pltpu.roll(pltpu.roll(total, 14, axis=0), X - 2, axis=1)
         out[z - 2] = total[:PY, :PX]
-    write.wait()
 
 
 def per_device(rhs, prhs, visc, mass, pscale, vbounds, pbounds):
@@ -463,8 +464,8 @@
         first_sums,
         [(rows, 2 * X)],
         scratch=[
-            pltpu.VMEM((ZW, 32, X), F32),
-            pltpu.VMEM((48, X), F32),
+            pltpu.VMEM((3, ZW, 32, X), F32),
+            pltpu.VMEM((6, 48, X), F32),
             pltpu.VMEM((rows, 2 * X), jnp.bfloat16),
         ],
     )(main, ring)
@@ -474,11 +475,11 @@
         vmem=(0,),
         scratch=[
             pltpu.VMEM((TILES, 8, X), F32),
-            pltpu.VMEM((3, 2, ZW, 32, X), F32),
-            pltpu.VMEM((3, 2, ZW, 32, X), F32),
-            pltpu.VMEM((3, 2, ZW, 32, X), F32),
+            pltpu.VMEM((2, 3, ZW, 32, X), F32),
+            pltpu.VMEM((2, 3, ZW, 32, X), F32),
+            pltpu.VMEM((2, 3, ZW, 32, X), F32),
             pltpu.VMEM((3, 2, Z, 32, X), F32),
-            pltpu.VMEM((2, 48, X), F32),
+            pltpu.VMEM((6, 48, X), F32),
             pltpu.VMEM((rows, 4 * X), jnp.bfloat16),
             pltpu.VMEM((rows, 2 * X), F32),
             pltpu.VMEM((3, 32, X), F32),
@@ -487,12 +488,10 @@
         ],
     )(main, below, above, jnp.asarray(restriction()), ring, sums, coefs)
     z_halos = swap_neighbours("gz", msg_even, msg_odd)
-    return call(
-        pressure_step,
-        [(3, Z, Y, X), (PZ, PY, PX)],
-        scratch=[pltpu.VMEM((2, 4, *plane), F32), pltpu.SemaphoreType.DMA],
-        hbm_out=(0,),
-    )(coupled, scale, *z_halos, coefs, vel)
+    (pressure,) = call(
+        pressure_step, [(PZ, PY, PX)], scratch=[pltpu.VMEM((2, 4, *plane), F32)]
+    )(coupled, scale, *z_halos, coefs)
+    return vel, pressure
 
 
 def solution(mesh):

time: 59.4 us -> 57.6 us (0.970)
  Pallas kernels: 9.16 us -> 6.92 us
  local copies, waits for them, and re-layouts: 0.04 us -> 0.72 us
    pallas_call x8, Pallas kernels: 9.16 us -> 6.92 us  [run(): pl.pallas_call(body, in_specs=[pl.BlockSpec(memory_space=space.get(i, plt...]
    unnamed x18 -> x19, local copies, waits for them, and re-layouts: 0.04 us -> 0.72 us
    ppermute x2, waiting for transfers between devices: 12.6 us -> 11.9 us  [swap_neighbours(): outer = lax.ppermute(second, axis, odd)]
  transfers between devices with their start and end apart: 8 -> 8, of which waited for: 4 -> 4; matrix products, arithmetic and copies ran while one was open for 0% -> 1% of each run, Pallas kernels for 3% -> 2%
where the time goes in v7:
time: 57.6 us; the launch traced here: 57.3 us
  starting transfers between devices  29.1 us (51%)
  waiting for transfers between devices  19.7 us (34%)
  Pallas kernels  6.92 us (12%)
  between operations  0.85 us (1%)
  local copies, waits for them, and re-layouts  0.72 us (1%)
    ppermute x2, starting transfers between devices, swap_neighbours(): inner = lax.ppermute(first, axis, even)  17.9 us
    ppermute x2, waiting for transfers between devices, swap_neighbours(): outer = lax.ppermute(second, axis, odd)  11.9 us
    ppermute x2, waiting for transfers between devices, both_neighbours(): from_above = lax.ppermute(to_below, axis, down)  7.79 us
    pallas_call x8, Pallas kernels, run(): pl.pallas_call(body, in_specs=[pl.BlockSpec(memory_space=space.get(i, plt...  6.92 us
    ppermute x2, starting transfers between devices, swap_neighbours(): outer = lax.ppermute(second, axis, odd)  5.85 us
    ppermute x2, starting transfers between devices, both_neighbours(): from_below = lax.ppermute(to_above, axis, up)  2.73 us
    ppermute x2, starting transfers between devices, both_neighbours(): from_above = lax.ppermute(to_below, axis, down)  2.58 us
  transfers between devices with their start and end apart: 8, of which 4 were waited for; matrix products, arithmetic and copies ran while one was open for 1% of the time, Pallas kernels for 2%

profile of v7, /device:TPU:1, one launch (start us, length us, event | category | flops | bytes accessed | tf_op | source)
XLA Modules:
  0.0 57.3 jit_solution(10987878231363272149)
XLA Ops:
  0.6 0.0 copy-start.1
  0.6 0.0 copy-start.5
  0.7 1.0 %shard_map.104 = (f32[8,16,128]{2,1,0:T(8,128)S(1)}, f32[8,16,128]{2,1,0:T(8,128)S(1)}) custom-call(f32[3,8,16,128]{3,2,1,0:T(8,128)} %rhs.3, f32[8,16,128]{2,1,0:T(8,128)} %visc.3, f32[8,16,128]{2,1,0:T(8,128)} %mass.3), custom_call_target="tpu_custom_call" | custom-call | tf_op jit(solution)/shard_map/pallas_call | solution.py:53
  1.7 16.0 %collective-permute-start = (f32[8,16,128]{2,1,0:T(8,128)S(1)}, f32[8,16,128]{2,1,0:T(8,128)S(1)}, u32[]{:S(2)}, u32[]{:S(2)}) collective-permute-start(f32[8,16,128]{2,1,0:T(8,128)S(1)} %get-tuple-element.15), channel_id=1, source_target_pairs={{0,1},{1,0},{2,3},{3,2},{4,5},{5,4},{6,7},{7,6},{8,9},{9,8},{10,11... | collective-permute-start | bytes 196616 | tf_op jit(solution)/shard_map/ppermute | solution.py:32
  17.7 1.9 %collective-permute-start.1 = (f32[8,16,128]{2,1,0:T(8,128)S(1)}, f32[8,16,128]{2,1,0:T(8,128)S(1)}, u32[]{:S(2)}, u32[]{:S(2)}) collective-permute-start(f32[8,16,128]{2,1,0:T(8,128)S(1)} %get-tuple-element.16), channel_id=1, source_target_pairs={{1,2},{2,1},{3,4},{4,3},{5,6},{6,5},{7,8},{8,7},{9,10},{10,9},{11,... | collective-permute-start | bytes 196616 | tf_op jit(solution)/shard_map/ppermute | solution.py:33
  19.7 0.1 shard_map.105.pt
  19.8 0.0 collective-permute-done.got_even
  19.8 7.5 %collective-permute-done.1.got_odd = f32[8,16,128]{2,1,0:T(8,128)S(1)} collective-permute-done((f32[8,16,128]{2,1,0:T(8,128)S(1)}, f32[8,16,128]{2,1,0:T(8,128)S(1)}, u32[]{:S(2)}, u32[]{:S(2)}) %collective-permute-start.1) | collective-permute-done | bytes 65568 | tf_op jit(solution)/shard_map/ppermute | solution.py:33
  27.2 0.1 shard_map.106
  27.3 1.3 %collective-permute-start.2 = (f32[416,128]{1,0:T(8,128)S(1)}, f32[416,128]{1,0:T(8,128)S(1)}, u32[]{:S(2)}, u32[]{:S(2)}) collective-permute-start(f32[416,128]{1,0:T(8,128)S(1)} %get-tuple-element.18), channel_id=1, source_target_pairs={{0,32},{32,64},{64,96},{96,128},{128,160},{160,192},{192,224},{1,3... | collective-permute-start | bytes 638984 | tf_op jit(solution)/shard_map/ppermute | solution.py:41
  28.6 1.3 %collective-permute-start.3 = (f32[360,128]{1,0:T(8,128)S(1)}, f32[360,128]{1,0:T(8,128)S(1)}, u32[]{:S(2)}, u32[]{:S(2)}) collective-permute-start(f32[360,128]{1,0:T(8,128)S(1)} %get-tuple-element.19), channel_id=1, source_target_pairs={{32,0},{64,32},{96,64},{128,96},{160,128},{192,160},{224,192},{33,... | collective-permute-start | bytes 552968 | tf_op jit(solution)/shard_map/ppermute | solution.py:42
  29.9 5.3 %collective-permute-done.3.above = f32[360,128]{1,0:T(8,128)S(1)} collective-permute-done((f32[360,128]{1,0:T(8,128)S(1)}, f32[360,128]{1,0:T(8,128)S(1)}, u32[]{:S(2)}, u32[]{:S(2)}) %collective-permute-start.3) | collective-permute-done | bytes 184352 | tf_op jit(solution)/shard_map/ppermute | solution.py:42
  35.2 0.0 collective-permute-done.2.below
  35.2 0.4 shard_map.107
  35.6 0.0 copy-start.7
  35.6 0.0 copy-start.8
  35.6 1.4 %collective-permute-start.4 = (f32[16,8,128]{2,1,0:T(8,128)S(1)}, f32[16,8,128]{2,1,0:T(8,128)S(1)}, u32[]{:S(2)}, u32[]{:S(2)}) collective-permute-start(f32[16,8,128]{2,1,0:T(8,128)S(1)} %get-tuple-element.21), channel_id=1, source_target_pairs={{0,256},{256,512},{512,768},{1,257},{257,513},{513,769},{2,258},{2... | collective-permute-start | bytes 196616 | tf_op jit(solution)/shard_map/ppermute | solution.py:41
  37.1 1.3 %collective-permute-start.5 = (f32[16,8,128]{2,1,0:T(8,128)S(1)}, f32[16,8,128]{2,1,0:T(8,128)S(1)}, u32[]{:S(2)}, u32[]{:S(2)}) collective-permute-start(f32[16,8,128]{2,1,0:T(8,128)S(1)} %get-tuple-element.22), channel_id=1, source_target_pairs={{256,0},{512,256},{768,512},{257,1},{513,257},{769,513},{258,2},{5... | collective-permute-start | bytes 196616 | tf_op jit(solution)/shard_map/ppermute | solution.py:42
  38.4 0.0 copy-done.7
  38.4 0.0 copy-done.8
  38.4 0.6 shard_map.109.coefs
  39.0 0.0 copy-start.4
  39.0 0.6 shard_map.108.sums
  39.6 0.0 collective-permute-done.4.from_below
  39.6 2.5 %collective-permute-done.5.from_above = f32[16,8,128]{2,1,0:T(8,128)S(1)} collective-permute-done((f32[16,8,128]{2,1,0:T(8,128)S(1)}, f32[16,8,128]{2,1,0:T(8,128)S(1)}, u32[]{:S(2)}, u32[]{:S(2)}) %collective-permute-start.5) | collective-permute-done | bytes 65568 | tf_op jit(solution)/shard_map/ppermute | solution.py:42
  42.1 3.3 %shard_map.110 = (f32[3,8,16,128]{3,2,1,0:T(8,128)S(1)}, f32[6,16,128]{2,1,0:T(8,128)S(1)}, f32[4,16,128]{2,1,0:T(8,128)S(1)}, f32[48,128]{1,0:T(8,128)S(1)}, f32[48,128]{1,0:T(8,128)S(1)}) custom-call(f32[256,8,128]{2,1,0:T(8,128)S(1)} %get-tuple-element.20.main, f32[16,8,128]{2,1,0:T(8,128)S(1)} %collective-permute-done.4.from_below, ...), custom_call_target="tpu_custom_call" | custom-call | tf_op jit(solution)/shard_map/pallas_call | solution.py:53
  45.4 1.9 %collective-permute-start.6 = (f32[48,128]{1,0:T(8,128)S(1)}, f32[48,128]{1,0:T(8,128)S(1)}, u32[]{:S(2)}, u32[]{:S(2)}) collective-permute-start(f32[48,128]{1,0:T(8,128)S(1)} %get-tuple-element.26), channel_id=1, source_target_pairs={{0,1},{1,0},{2,3},{3,2},{4,5},{5,4},{6,7},{7,6},{8,9},{9,8},{10,11... | collective-permute-start | bytes 73736 | tf_op jit(solution)/shard_map/ppermute | solution.py:32
  47.4 3.9 %collective-permute-start.7 = (f32[48,128]{1,0:T(8,128)S(1)}, f32[48,128]{1,0:T(8,128)S(1)}, u32[]{:S(2)}, u32[]{:S(2)}) collective-permute-start(f32[48,128]{1,0:T(8,128)S(1)} %get-tuple-element.27), channel_id=1, source_target_pairs={{1,2},{2,1},{3,4},{4,3},{5,6},{6,5},{7,8},{8,7},{9,10},{10,9},{11,... | collective-permute-start | bytes 73736 | tf_op jit(solution)/shard_map/ppermute | solution.py:33
  51.3 0.7 %copy.11 = f32[3,8,16,128]{3,2,1,0:T(8,128)} copy(f32[3,8,16,128]{3,2,1,0:T(8,128)S(1)} %get-tuple-element.28) | data formatting | bytes 393216
  52.0 0.0 collective-permute-done.6.got_even
  52.0 4.4 %collective-permute-done.7.got_odd = f32[48,128]{1,0:T(8,128)S(1)} collective-permute-done((f32[48,128]{1,0:T(8,128)S(1)}, f32[48,128]{1,0:T(8,128)S(1)}, u32[]{:S(2)}, u32[]{:S(2)}) %collective-permute-start.7) | collective-permute-done | bytes 24608 | tf_op jit(solution)/shard_map/ppermute | solution.py:33
  56.4 0.9 %shard_map.111 = f32[4,8,64]{2,1,0:T(8,128)} custom-call(f32[6,16,128]{2,1,0:T(8,128)S(1)} %get-tuple-element.24.coupled, f32[4,16,128]{2,1,0:T(8,128)S(1)} %get-tuple-element.25.pscale, f32[48,128]{1,0:T(8,128)S(1)} %collective-permute-done.6.got_even, f32[48,128]{1,0:T(8,128)S(1)} %collective-permute-done.7.got_odd, f32[10,8,128]{2,1,0:T(8,128)S(1)} %shard_map.109.coefs), custom_call_target="tpu_custom_call" | custom-call | tf_op jit(solution)/shard_map/pallas_call | solution.py:53
  (11 shorter events, 0.0 us)
Async XLA Ops:
  0.6 26.6 %copy-start.1 = (f32[3,8,16,128]{3,2,1,0:T(8,128)S(1)}, f32[3,8,16,128]{3,2,1,0:T(8,128)}, u32[]{:S(2)}) copy-start(f32[3,8,16,128]{3,2,1,0:T(8,128)} %rhs.3) | copy-start | bytes 589828
  0.6 19.0 %copy-start.5 = (f32[4,8,64]{2,1,0:T(8,128)S(1)}, f32[4,8,64]{2,1,0:T(8,128)}, u32[]{:S(2)}) copy-start(f32[4,8,64]{2,1,0:T(8,128)} %pscale.1) | copy-start | bytes 24580
  0.7 19.0 %copy-start.6 = (f32[4,8,64]{2,1,0:T(8,128)S(1)}, f32[4,8,64]{2,1,0:T(8,128)}, u32[]{:S(2)}) copy-start(f32[4,8,64]{2,1,0:T(8,128)} %prhs.1) | copy-start | bytes 24580
  0.7 26.6 %copy-start.2 = (f32[8,16,128]{2,1,0:T(8,128)S(1)}, f32[8,16,128]{2,1,0:T(8,128)}, u32[]{:S(2)}) copy-start(f32[8,16,128]{2,1,0:T(8,128)} %visc.3) | copy-start | bytes 196612
  0.7 26.6 %copy-start.3 = (f32[8,16,128]{2,1,0:T(8,128)S(1)}, f32[8,16,128]{2,1,0:T(8,128)}, u32[]{:S(2)}) copy-start(f32[8,16,128]{2,1,0:T(8,128)} %mass.3) | copy-start | bytes 196612
  1.7 18.1 %collective-permute-start = (f32[8,16,128]{2,1,0:T(8,128)S(1)}, f32[8,16,128]{2,1,0:T(8,128)S(1)}, u32[]{:S(2)}, u32[]{:S(2)}) collective-permute-start(f32[8,16,128]{2,1,0:T(8,128)S(1)} %get-tuple-element.15), channel_id=1, source_target_pairs={{0,1},{1,0},{2,3},{3,2},{4,5},{5,4},{6,7},{7,6},{8,9},{9,8},{10,11... | collective-permute-start | bytes 196616 | tf_op jit(solution)/shard_map/ppermute | solution.py:32
  17.7 9.5 %collective-permute-start.1 = (f32[8,16,128]{2,1,0:T(8,128)S(1)}, f32[8,16,128]{2,1,0:T(8,128)S(1)}, u32[]{:S(2)}, u32[]{:S(2)}) collective-permute-start(f32[8,16,128]{2,1,0:T(8,128)S(1)} %get-tuple-element.16), channel_id=1, source_target_pairs={{1,2},{2,1},{3,4},{4,3},{5,6},{6,5},{7,8},{8,7},{9,10},{10,9},{11,... | collective-permute-start | bytes 196616 | tf_op jit(solution)/shard_map/ppermute | solution.py:33
  27.3 7.9 %collective-permute-start.2 = (f32[416,128]{1,0:T(8,128)S(1)}, f32[416,128]{1,0:T(8,128)S(1)}, u32[]{:S(2)}, u32[]{:S(2)}) collective-permute-start(f32[416,128]{1,0:T(8,128)S(1)} %get-tuple-element.18), channel_id=1, source_target_pairs={{0,32},{32,64},{64,96},{96,128},{128,160},{160,192},{192,224},{1,3... | collective-permute-start | bytes 638984 | tf_op jit(solution)/shard_map/ppermute | solution.py:41
  28.6 6.6 %collective-permute-start.3 = (f32[360,128]{1,0:T(8,128)S(1)}, f32[360,128]{1,0:T(8,128)S(1)}, u32[]{:S(2)}, u32[]{:S(2)}) collective-permute-start(f32[360,128]{1,0:T(8,128)S(1)} %get-tuple-element.19), channel_id=1, source_target_pairs={{32,0},{64,32},{96,64},{128,96},{160,128},{192,160},{224,192},{33,... | collective-permute-start | bytes 552968 | tf_op jit(solution)/shard_map/ppermute | solution.py:42
  35.2 3.8 %copy-start = (bf16[512,256]{1,0:T(8,128)(2,1)S(1)}, bf16[512,256]{1,0:T(8,128)(2,1)}, u32[]{:S(2)}) copy-start(bf16[512,256]{1,0:T(8,128)(2,1)} %constant.4.clone.ring) | copy-start | bytes 786436
  35.6 2.8 %copy-start.7 = (f32[2]{0:T(128)S(1)}, f32[2]{0:T(128)}, u32[]{:S(2)}) copy-start(f32[2]{0:T(128)} %vbounds.1) | copy-start | bytes 28
  35.6 2.8 %copy-start.8 = (f32[2]{0:T(128)S(1)}, f32[2]{0:T(128)}, u32[]{:S(2)}) copy-start(f32[2]{0:T(128)} %pbounds.1) | copy-start | bytes 28
  35.6 3.9 %collective-permute-start.4 = (f32[16,8,128]{2,1,0:T(8,128)S(1)}, f32[16,8,128]{2,1,0:T(8,128)S(1)}, u32[]{:S(2)}, u32[]{:S(2)}) collective-permute-start(f32[16,8,128]{2,1,0:T(8,128)S(1)} %get-tuple-element.21), channel_id=1, source_target_pairs={{0,256},{256,512},{512,768},{1,257},{257,513},{513,769},{2,258},{2... | collective-permute-start | bytes 196616 | tf_op jit(solution)/shard_map/ppermute | solution.py:41
  37.1 5.0 %collective-permute-start.5 = (f32[16,8,128]{2,1,0:T(8,128)S(1)}, f32[16,8,128]{2,1,0:T(8,128)S(1)}, u32[]{:S(2)}, u32[]{:S(2)}) collective-permute-start(f32[16,8,128]{2,1,0:T(8,128)S(1)} %get-tuple-element.22), channel_id=1, source_target_pairs={{256,0},{512,256},{768,512},{257,1},{513,257},{769,513},{258,2},{5... | collective-permute-start | bytes 196616 | tf_op jit(solution)/shard_map/ppermute | solution.py:42
  39.0 3.1 %copy-start.4 = (bf16[512,128]{1,0:T(8,128)(2,1)S(1)}, bf16[512,128]{1,0:T(8,128)(2,1)}, u32[]{:S(2)}) copy-start(bf16[512,128]{1,0:T(8,128)(2,1)} %constant.5.clone.table) | copy-start | bytes 393220
  45.4 6.5 %collective-permute-start.6 = (f32[48,128]{1,0:T(8,128)S(1)}, f32[48,128]{1,0:T(8,128)S(1)}, u32[]{:S(2)}, u32[]{:S(2)}) collective-permute-start(f32[48,128]{1,0:T(8,128)S(1)} %get-tuple-element.26), channel_id=1, source_target_pairs={{0,1},{1,0},{2,3},{3,2},{4,5},{5,4},{6,7},{7,6},{8,9},{9,8},{10,11... | collective-permute-start | bytes 73736 | tf_op jit(solution)/shard_map/ppermute | solution.py:32
  47.4 9.1 %collective-permute-start.7 = (f32[48,128]{1,0:T(8,128)S(1)}, f32[48,128]{1,0:T(8,128)S(1)}, u32[]{:S(2)}, u32[]{:S(2)}) collective-permute-start(f32[48,128]{1,0:T(8,128)S(1)} %get-tuple-element.27), channel_id=1, source_target_pairs={{1,2},{2,1},{3,4},{4,3},{5,6},{6,5},{7,8},{8,7},{9,10},{10,9},{11,... | collective-permute-start | bytes 73736 | tf_op jit(solution)/shard_map/ppermute | solution.py:33

commit v8 on v7

--- a/solution.py
+++ b/solution.py
@@ -255,11 +255,8 @@
 
 
 def loop(start, count, body, each=1):
-    def step(i, _):
-        body([start + each * i + j for j in range(each)])
-        return 0
-
-    lax.fori_loop(0, count // each, step, 0)
+    for z in range(start, start + count, each):
+        body(list(range(z, min(z + each, start + count))))
 
 
 def weigh(src, w):
@@ -332,9 +329,10 @@
 
     loop(1, Z + 2, sweep1)
 
-    sum_rows([(c, w.at[h, c], 2 * h * X) for h in range(2) for c in range(3)], t, lhs, 2, Z)
-    total = 3 * Z * 32
-    s[:total] = dot(lhs[:total], ring[...])
+    for c in range(3):
+        sum_rows([(c, w.at[h, c], 2 * h * X) for h in range(2)], t, lhs, 2, Z)
+        at = slice(c * Z * 32, (c + 1) * Z * 32)
+        s[at] = dot(lhs[at], ring[...])
 
     def sweep2(zs):
         (z,) = zs

time: 57.6 us -> 56.6 us (0.983)
  Pallas kernels: 6.92 us -> 5.72 us
    pallas_call x8, Pallas kernels: 6.92 us -> 5.72 us  [run(): pl.pallas_call(body, in_specs=[pl.BlockSpec(memory_space=space.get(i, plt...]
where the time goes in v8:
time: 56.6 us; the launch traced here: 56.2 us
  starting transfers between devices  29.1 us (51%)
  waiting for transfers between devices  19.8 us (35%)
  Pallas kernels  5.72 us (10%)
  between operations  0.85 us (2%)
  local copies, waits for them, and re-layouts  0.72 us (1%)
    ppermute x2, starting transfers between devices, swap_neighbours(): inner = lax.ppermute(first, axis, even)  17.9 us
    ppermute x2, waiting for transfers between devices, swap_neighbours(): outer = lax.ppermute(second, axis, odd)  11.9 us
    ppermute x2, waiting for transfers between devices, both_neighbours(): from_above = lax.ppermute(to_below, axis, down)  7.92 us
    ppermute x2, starting transfers between devices, swap_neighbours(): outer = lax.ppermute(second, axis, odd)  5.84 us
    pallas_call x8, Pallas kernels, run(): pl.pallas_call(body, in_specs=[pl.BlockSpec(memory_space=space.get(i, plt...  5.72 us
    ppermute x2, starting transfers between devices, both_neighbours(): from_below = lax.ppermute(to_above, axis, up)  2.73 us
    ppermute x2, starting transfers between devices, both_neighbours(): from_above = lax.ppermute(to_below, axis, down)  2.58 us
  transfers between devices with their start and end apart: 8, of which 4 were waited for; matrix products, arithmetic and copies ran while one was open for 1% of the time, Pallas kernels for 2%

profile of v8, /device:TPU:1, one launch (start us, length us, event | category | flops | bytes accessed | tf_op | source)
XLA Modules:
  0.0 56.2 jit_solution(280600642024211464)
XLA Ops:
  0.6 0.0 copy-start.1
  0.6 0.0 copy-start.5
  0.7 1.0 %shard_map.104 = (f32[8,16,128]{2,1,0:T(8,128)S(1)}, f32[8,16,128]{2,1,0:T(8,128)S(1)}) custom-call(f32[3,8,16,128]{3,2,1,0:T(8,128)} %rhs.3, f32[8,16,128]{2,1,0:T(8,128)} %visc.3, f32[8,16,128]{2,1,0:T(8,128)} %mass.3), custom_call_target="tpu_custom_call" | custom-call | tf_op jit(solution)/shard_map/pallas_call | solution.py:53
  1.7 16.0 %collective-permute-start = (f32[8,16,128]{2,1,0:T(8,128)S(1)}, f32[8,16,128]{2,1,0:T(8,128)S(1)}, u32[]{:S(2)}, u32[]{:S(2)}) collective-permute-start(f32[8,16,128]{2,1,0:T(8,128)S(1)} %get-tuple-element.15), channel_id=1, source_target_pairs={{0,1},{1,0},{2,3},{3,2},{4,5},{5,4},{6,7},{7,6},{8,9},{9,8},{10,11... | collective-permute-start | bytes 196616 | tf_op jit(solution)/shard_map/ppermute | solution.py:32
  17.7 1.9 %collective-permute-start.1 = (f32[8,16,128]{2,1,0:T(8,128)S(1)}, f32[8,16,128]{2,1,0:T(8,128)S(1)}, u32[]{:S(2)}, u32[]{:S(2)}) collective-permute-start(f32[8,16,128]{2,1,0:T(8,128)S(1)} %get-tuple-element.16), channel_id=1, source_target_pairs={{1,2},{2,1},{3,4},{4,3},{5,6},{6,5},{7,8},{8,7},{9,10},{10,9},{11,... | collective-permute-start | bytes 196616 | tf_op jit(solution)/shard_map/ppermute | solution.py:33
  19.7 0.1 shard_map.105.pt
  19.8 0.0 collective-permute-done.got_even
  19.8 7.5 %collective-permute-done.1.got_odd = f32[8,16,128]{2,1,0:T(8,128)S(1)} collective-permute-done((f32[8,16,128]{2,1,0:T(8,128)S(1)}, f32[8,16,128]{2,1,0:T(8,128)S(1)}, u32[]{:S(2)}, u32[]{:S(2)}) %collective-permute-start.1) | collective-permute-done | bytes 65568 | tf_op jit(solution)/shard_map/ppermute | solution.py:33
  27.2 0.1 shard_map.106
  27.3 1.3 %collective-permute-start.2 = (f32[416,128]{1,0:T(8,128)S(1)}, f32[416,128]{1,0:T(8,128)S(1)}, u32[]{:S(2)}, u32[]{:S(2)}) collective-permute-start(f32[416,128]{1,0:T(8,128)S(1)} %get-tuple-element.18), channel_id=1, source_target_pairs={{0,32},{32,64},{64,96},{96,128},{128,160},{160,192},{192,224},{1,3... | collective-permute-start | bytes 638984 | tf_op jit(solution)/shard_map/ppermute | solution.py:41
  28.6 1.3 %collective-permute-start.3 = (f32[360,128]{1,0:T(8,128)S(1)}, f32[360,128]{1,0:T(8,128)S(1)}, u32[]{:S(2)}, u32[]{:S(2)}) collective-permute-start(f32[360,128]{1,0:T(8,128)S(1)} %get-tuple-element.19), channel_id=1, source_target_pairs={{32,0},{64,32},{96,64},{128,96},{160,128},{192,160},{224,192},{33,... | collective-permute-start | bytes 552968 | tf_op jit(solution)/shard_map/ppermute | solution.py:42
  29.9 5.3 %collective-permute-done.3.above = f32[360,128]{1,0:T(8,128)S(1)} collective-permute-done((f32[360,128]{1,0:T(8,128)S(1)}, f32[360,128]{1,0:T(8,128)S(1)}, u32[]{:S(2)}, u32[]{:S(2)}) %collective-permute-start.3) | collective-permute-done | bytes 184352 | tf_op jit(solution)/shard_map/ppermute | solution.py:42
  35.2 0.0 collective-permute-done.2.below
  35.2 0.4 shard_map.107
  35.6 0.0 copy-start.7
  35.6 0.0 copy-start.8
  35.6 1.4 %collective-permute-start.4 = (f32[16,8,128]{2,1,0:T(8,128)S(1)}, f32[16,8,128]{2,1,0:T(8,128)S(1)}, u32[]{:S(2)}, u32[]{:S(2)}) collective-permute-start(f32[16,8,128]{2,1,0:T(8,128)S(1)} %get-tuple-element.21), channel_id=1, source_target_pairs={{0,256},{256,512},{512,768},{1,257},{257,513},{513,769},{2,258},{2... | collective-permute-start | bytes 196616 | tf_op jit(solution)/shard_map/ppermute | solution.py:41
  37.1 1.3 %collective-permute-start.5 = (f32[16,8,128]{2,1,0:T(8,128)S(1)}, f32[16,8,128]{2,1,0:T(8,128)S(1)}, u32[]{:S(2)}, u32[]{:S(2)}) collective-permute-start(f32[16,8,128]{2,1,0:T(8,128)S(1)} %get-tuple-element.22), channel_id=1, source_target_pairs={{256,0},{512,256},{768,512},{257,1},{513,257},{769,513},{258,2},{5... | collective-permute-start | bytes 196616 | tf_op jit(solution)/shard_map/ppermute | solution.py:42
  38.4 0.0 copy-done.7
  38.4 0.0 copy-done.8
  38.4 0.6 %shard_map.109.coefs = f32[10,8,128]{2,1,0:T(8,128)S(1)} custom-call(f32[2]{0:T(128)S(1)} %copy-done.7, f32[2]{0:T(128)S(1)} %copy-done.8), custom_call_target="tpu_custom_call" | custom-call | tf_op jit(solution)/shard_map/pallas_call | solution.py:53
  39.0 0.0 copy-start.4
  39.0 0.4 shard_map.108.sums
  39.4 0.0 collective-permute-done.4.from_below
  39.4 2.6 %collective-permute-done.5.from_above = f32[16,8,128]{2,1,0:T(8,128)S(1)} collective-permute-done((f32[16,8,128]{2,1,0:T(8,128)S(1)}, f32[16,8,128]{2,1,0:T(8,128)S(1)}, u32[]{:S(2)}, u32[]{:S(2)}) %collective-permute-start.5) | collective-permute-done | bytes 65568 | tf_op jit(solution)/shard_map/ppermute | solution.py:42
  42.1 2.3 %shard_map.110 = (f32[3,8,16,128]{3,2,1,0:T(8,128)S(1)}, f32[6,16,128]{2,1,0:T(8,128)S(1)}, f32[4,16,128]{2,1,0:T(8,128)S(1)}, f32[48,128]{1,0:T(8,128)S(1)}, f32[48,128]{1,0:T(8,128)S(1)}) custom-call(f32[256,8,128]{2,1,0:T(8,128)S(1)} %get-tuple-element.20.main, f32[16,8,128]{2,1,0:T(8,128)S(1)} %collective-permute-done.4.from_below, ...), custom_call_target="tpu_custom_call" | custom-call | tf_op jit(solution)/shard_map/pallas_call | solution.py:53
  44.4 1.9 %collective-permute-start.6 = (f32[48,128]{1,0:T(8,128)S(1)}, f32[48,128]{1,0:T(8,128)S(1)}, u32[]{:S(2)}, u32[]{:S(2)}) collective-permute-start(f32[48,128]{1,0:T(8,128)S(1)} %get-tuple-element.26), channel_id=1, source_target_pairs={{0,1},{1,0},{2,3},{3,2},{4,5},{5,4},{6,7},{7,6},{8,9},{9,8},{10,11... | collective-permute-start | bytes 73736 | tf_op jit(solution)/shard_map/ppermute | solution.py:32
  46.3 3.9 %collective-permute-start.7 = (f32[48,128]{1,0:T(8,128)S(1)}, f32[48,128]{1,0:T(8,128)S(1)}, u32[]{:S(2)}, u32[]{:S(2)}) collective-permute-start(f32[48,128]{1,0:T(8,128)S(1)} %get-tuple-element.27), channel_id=1, source_target_pairs={{1,2},{2,1},{3,4},{4,3},{5,6},{6,5},{7,8},{8,7},{9,10},{10,9},{11,... | collective-permute-start | bytes 73736 | tf_op jit(solution)/shard_map/ppermute | solution.py:33
  50.2 0.7 %copy.11 = f32[3,8,16,128]{3,2,1,0:T(8,128)} copy(f32[3,8,16,128]{3,2,1,0:T(8,128)S(1)} %get-tuple-element.28) | data formatting | bytes 393216
  50.9 0.0 collective-permute-done.6.got_even
  50.9 4.4 %collective-permute-done.7.got_odd = f32[48,128]{1,0:T(8,128)S(1)} collective-permute-done((f32[48,128]{1,0:T(8,128)S(1)}, f32[48,128]{1,0:T(8,128)S(1)}, u32[]{:S(2)}, u32[]{:S(2)}) %collective-permute-start.7) | collective-permute-done | bytes 24608 | tf_op jit(solution)/shard_map/ppermute | solution.py:33
  55.3 0.9 %shard_map.111 = f32[4,8,64]{2,1,0:T(8,128)} custom-call(f32[6,16,128]{2,1,0:T(8,128)S(1)} %get-tuple-element.24.coupled, f32[4,16,128]{2,1,0:T(8,128)S(1)} %get-tuple-element.25.pscale, f32[48,128]{1,0:T(8,128)S(1)} %collective-permute-done.6.got_even, f32[48,128]{1,0:T(8,128)S(1)} %collective-permute-done.7.got_odd, f32[10,8,128]{2,1,0:T(8,128)S(1)} %shard_map.109.coefs), custom_call_target="tpu_custom_call" | custom-call | tf_op jit(solution)/shard_map/pallas_call | solution.py:53
  (11 shorter events, 0.0 us)
Async XLA Ops:
  0.6 26.6 %copy-start.1 = (f32[3,8,16,128]{3,2,1,0:T(8,128)S(1)}, f32[3,8,16,128]{3,2,1,0:T(8,128)}, u32[]{:S(2)}) copy-start(f32[3,8,16,128]{3,2,1,0:T(8,128)} %rhs.3) | copy-start | bytes 589828
  0.6 19.0 %copy-start.5 = (f32[4,8,64]{2,1,0:T(8,128)S(1)}, f32[4,8,64]{2,1,0:T(8,128)}, u32[]{:S(2)}) copy-start(f32[4,8,64]{2,1,0:T(8,128)} %pscale.1) | copy-start | bytes 24580
  0.7 19.0 %copy-start.6 = (f32[4,8,64]{2,1,0:T(8,128)S(1)}, f32[4,8,64]{2,1,0:T(8,128)}, u32[]{:S(2)}) copy-start(f32[4,8,64]{2,1,0:T(8,128)} %prhs.1) | copy-start | bytes 24580
  0.7 26.6 %copy-start.2 = (f32[8,16,128]{2,1,0:T(8,128)S(1)}, f32[8,16,128]{2,1,0:T(8,128)}, u32[]{:S(2)}) copy-start(f32[8,16,128]{2,1,0:T(8,128)} %visc.3) | copy-start | bytes 196612
  0.7 26.6 %copy-start.3 = (f32[8,16,128]{2,1,0:T(8,128)S(1)}, f32[8,16,128]{2,1,0:T(8,128)}, u32[]{:S(2)}) copy-start(f32[8,16,128]{2,1,0:T(8,128)} %mass.3) | copy-start | bytes 196612
  1.7 18.1 %collective-permute-start = (f32[8,16,128]{2,1,0:T(8,128)S(1)}, f32[8,16,128]{2,1,0:T(8,128)S(1)}, u32[]{:S(2)}, u32[]{:S(2)}) collective-permute-start(f32[8,16,128]{2,1,0:T(8,128)S(1)} %get-tuple-element.15), channel_id=1, source_target_pairs={{0,1},{1,0},{2,3},{3,2},{4,5},{5,4},{6,7},{7,6},{8,9},{9,8},{10,11... | collective-permute-start | bytes 196616 | tf_op jit(solution)/shard_map/ppermute | solution.py:32
  17.7 9.5 %collective-permute-start.1 = (f32[8,16,128]{2,1,0:T(8,128)S(1)}, f32[8,16,128]{2,1,0:T(8,128)S(1)}, u32[]{:S(2)}, u32[]{:S(2)}) collective-permute-start(f32[8,16,128]{2,1,0:T(8,128)S(1)} %get-tuple-element.16), channel_id=1, source_target_pairs={{1,2},{2,1},{3,4},{4,3},{5,6},{6,5},{7,8},{8,7},{9,10},{10,9},{11,... | collective-permute-start | bytes 196616 | tf_op jit(solution)/shard_map/ppermute | solution.py:33
  27.3 7.9 %collective-permute-start.2 = (f32[416,128]{1,0:T(8,128)S(1)}, f32[416,128]{1,0:T(8,128)S(1)}, u32[]{:S(2)}, u32[]{:S(2)}) collective-permute-start(f32[416,128]{1,0:T(8,128)S(1)} %get-tuple-element.18), channel_id=1, source_target_pairs={{0,32},{32,64},{64,96},{96,128},{128,160},{160,192},{192,224},{1,3... | collective-permute-start | bytes 638984 | tf_op jit(solution)/shard_map/ppermute | solution.py:41
  28.6 6.6 %collective-permute-start.3 = (f32[360,128]{1,0:T(8,128)S(1)}, f32[360,128]{1,0:T(8,128)S(1)}, u32[]{:S(2)}, u32[]{:S(2)}) collective-permute-start(f32[360,128]{1,0:T(8,128)S(1)} %get-tuple-element.19), channel_id=1, source_target_pairs={{32,0},{64,32},{96,64},{128,96},{160,128},{192,160},{224,192},{33,... | collective-permute-start | bytes 552968 | tf_op jit(solution)/shard_map/ppermute | solution.py:42
  35.2 3.8 %copy-start = (bf16[512,256]{1,0:T(8,128)(2,1)S(1)}, bf16[512,256]{1,0:T(8,128)(2,1)}, u32[]{:S(2)}) copy-start(bf16[512,256]{1,0:T(8,128)(2,1)} %constant.4.clone.ring) | copy-start | bytes 786436
  35.6 2.8 %copy-start.7 = (f32[2]{0:T(128)S(1)}, f32[2]{0:T(128)}, u32[]{:S(2)}) copy-start(f32[2]{0:T(128)} %vbounds.1) | copy-start | bytes 28
  35.6 2.8 %copy-start.8 = (f32[2]{0:T(128)S(1)}, f32[2]{0:T(128)}, u32[]{:S(2)}) copy-start(f32[2]{0:T(128)} %pbounds.1) | copy-start | bytes 28
  35.6 3.8 %collective-permute-start.4 = (f32[16,8,128]{2,1,0:T(8,128)S(1)}, f32[16,8,128]{2,1,0:T(8,128)S(1)}, u32[]{:S(2)}, u32[]{:S(2)}) collective-permute-start(f32[16,8,128]{2,1,0:T(8,128)S(1)} %get-tuple-element.21), channel_id=1, source_target_pairs={{0,256},{256,512},{512,768},{1,257},{257,513},{513,769},{2,258},{2... | collective-permute-start | bytes 196616 | tf_op jit(solution)/shard_map/ppermute | solution.py:41
  37.1 5.0 %collective-permute-start.5 = (f32[16,8,128]{2,1,0:T(8,128)S(1)}, f32[16,8,128]{2,1,0:T(8,128)S(1)}, u32[]{:S(2)}, u32[]{:S(2)}) collective-permute-start(f32[16,8,128]{2,1,0:T(8,128)S(1)} %get-tuple-element.22), channel_id=1, source_target_pairs={{256,0},{512,256},{768,512},{257,1},{513,257},{769,513},{258,2},{5... | collective-permute-start | bytes 196616 | tf_op jit(solution)/shard_map/ppermute | solution.py:42
  39.0 3.1 %copy-start.4 = (bf16[512,128]{1,0:T(8,128)(2,1)S(1)}, bf16[512,128]{1,0:T(8,128)(2,1)}, u32[]{:S(2)}) copy-start(bf16[512,128]{1,0:T(8,128)(2,1)} %constant.5.clone.table) | copy-start | bytes 393220
  44.4 6.5 %collective-permute-start.6 = (f32[48,128]{1,0:T(8,128)S(1)}, f32[48,128]{1,0:T(8,128)S(1)}, u32[]{:S(2)}, u32[]{:S(2)}) collective-permute-start(f32[48,128]{1,0:T(8,128)S(1)} %get-tuple-element.26), channel_id=1, source_target_pairs={{0,1},{1,0},{2,3},{3,2},{4,5},{5,4},{6,7},{7,6},{8,9},{9,8},{10,11... | collective-permute-start | bytes 73736 | tf_op jit(solution)/shard_map/ppermute | solution.py:32
  46.3 9.1 %collective-permute-start.7 = (f32[48,128]{1,0:T(8,128)S(1)}, f32[48,128]{1,0:T(8,128)S(1)}, u32[]{:S(2)}, u32[]{:S(2)}) collective-permute-start(f32[48,128]{1,0:T(8,128)S(1)} %get-tuple-element.27), channel_id=1, source_target_pairs={{1,2},{2,1},{3,4},{4,3},{5,6},{6,5},{7,8},{8,7},{9,10},{10,9},{11,... | collective-permute-start | bytes 73736 | tf_op jit(solution)/shard_map/ppermute | solution.py:33

commit v9 on v8

--- a/solution.py
+++ b/solution.py
@@ -152,7 +152,7 @@
         down[at_down + 2 * k : at_down + 2 * k + 2] = pt[k, :2]
 
 
-def pack_x(own, pt, below, above, main, up, down):
+def pack_x(own, pt, below, above, main, msg_even, msg_odd):
     at_up = at_down = 0
     rows = {r[0]: r[1:] for r in y_rows()}
     for p in range(PLANES):
@@ -179,10 +179,12 @@
             turned = pltpu.roll(tile, 64, axis=1)
             main[VT + 3 * k + t] = jnp.where(lane < 64, tile, turned)
             main[VT + 12 + 3 * k + t] = jnp.where(lane < 64, turned, tile)
+    even = parity("gx") == 0
     for i in range(PACKED):
         turned = main[16 * i : 16 * i + 16].reshape(X, X).T
-        down[i] = turned[:8]
-        up[i] = turned[X - 8 :]
+        low, high = turned[:8], turned[X - 8 :]
+        msg_even[i] = jnp.where(even, high, low)
+        msg_odd[i] = jnp.where(even, low, high)
 
 
 def lanes():
@@ -294,13 +296,15 @@
 
 
 def velocity_step(
-    main, from_below, from_above, table, ring, sums, coefs, vel, coupled, pscale, msg_even, msg_odd,
+    main, got_even, got_odd, table, ring, sums, coefs, vel, coupled, pscale, msg_even, msg_odd,
     halo, w, d, r, u, t, lhs, s, g, q, ptmp,
 ):
     lane = lanes()
     gap = jnp.zeros((X - 16, X), F32)
+    even = parity("gx") == 0
     for i in range(PACKED):
-        strips = jnp.concatenate([from_above[i], gap, from_below[i]], axis=0)
+        a, b = got_even[i], got_odd[i]
+        strips = jnp.concatenate([jnp.where(even, a, b), gap, jnp.where(even, b, a)], axis=0)
         halo[16 * i : 16 * i + 16] = strips.T.reshape(16, 8, X)
 
     inv, a1, g1, a2, g2 = (tall(coefs[i], 32) for i in range(5))
@@ -452,10 +456,10 @@
         pack_y, [(PLANES, *plane), (padded(UP_ROWS + 8), X), (padded(DOWN_ROWS + 8), X)]
     )(rhs, visc, mass, *z_halos, pt)
     below, above = both_neighbours("gy", up, down)
-    main, up, down = call(pack_x, [(TILES, *tile), (PACKED, *tile), (PACKED, *tile)])(
+    main, msg_even, msg_odd = call(pack_x, [(TILES, *tile), (PACKED, *tile), (PACKED, *tile)])(
         own, pt, below, above
     )
-    below, above = both_neighbours("gx", up, down)
+    below, above = swap_neighbours("gx", msg_even, msg_odd)
     ring = jnp.asarray(smoothing())
     rows = 3 * (Z + 2) * 32
     (sums,) = call(

time: 56.6 us -> 56.4 us (level)
  the two profiles are of different devices: /device:TPU:1 before, /device:TPU:3 now
where the time goes in v9:
time: 56.4 us; the launch traced here: 56 us
  starting transfers between devices  34.5 us (61%)
  waiting for transfers between devices  14.1 us (25%)
  Pallas kernels  5.74 us (10%)
  between operations  0.85 us (2%)
  local copies, waits for them, and re-layouts  0.72 us (1%)
    ppermute x3, starting transfers between devices, swap_neighbours(): inner = lax.ppermute(first, axis, even)  17.4 us
    ppermute x3, starting transfers between devices, swap_neighbours(): outer = lax.ppermute(second, axis, odd)  12.5 us
    ppermute x3, waiting for transfers between devices, swap_neighbours(): outer = lax.ppermute(second, axis, odd)  9.16 us
    pallas_call x8, Pallas kernels, run(): pl.pallas_call(body, in_specs=[pl.BlockSpec(memory_space=space.get(i, plt...  5.74 us
    ppermute x1, waiting for transfers between devices, both_neighbours(): from_above = lax.ppermute(to_below, axis, down)  4.98 us
    ppermute x1, starting transfers between devices, both_neighbours(): from_below = lax.ppermute(to_above, axis, up)  3.33 us
    ppermute x1, starting transfers between devices, both_neighbours(): from_above = lax.ppermute(to_below, axis, down)  1.29 us
  transfers between devices with their start and end apart: 8, of which 4 were waited for; matrix products, arithmetic and copies ran while one was open for 1% of the time, Pallas kernels for 2%

profile of v9, /device:TPU:3, one launch (start us, length us, event | category | flops | bytes accessed | tf_op | source)
XLA Modules:
  0.0 56.0 jit_solution(2659431276041212970)
XLA Ops:
  0.6 0.0 copy-start.1
  0.6 0.0 copy-start.5
  0.7 0.0 copy-start.6
  0.7 1.0 %shard_map.104 = (f32[8,16,128]{2,1,0:T(8,128)S(1)}, f32[8,16,128]{2,1,0:T(8,128)S(1)}) custom-call(f32[3,8,16,128]{3,2,1,0:T(8,128)} %rhs.3, f32[8,16,128]{2,1,0:T(8,128)} %visc.3, f32[8,16,128]{2,1,0:T(8,128)} %mass.3), custom_call_target="tpu_custom_call" | custom-call | tf_op jit(solution)/shard_map/pallas_call | solution.py:53
  1.7 2.6 %collective-permute-start = (f32[8,16,128]{2,1,0:T(8,128)S(1)}, f32[8,16,128]{2,1,0:T(8,128)S(1)}, u32[]{:S(2)}, u32[]{:S(2)}) collective-permute-start(f32[8,16,128]{2,1,0:T(8,128)S(1)} %get-tuple-element.15), channel_id=1, source_target_pairs={{0,1},{1,0},{2,3},{3,2},{4,5},{5,4},{6,7},{7,6},{8,9},{9,8},{10,11... | collective-permute-start | bytes 196616 | tf_op jit(solution)/shard_map/ppermute | solution.py:32
  4.3 6.1 %collective-permute-start.1 = (f32[8,16,128]{2,1,0:T(8,128)S(1)}, f32[8,16,128]{2,1,0:T(8,128)S(1)}, u32[]{:S(2)}, u32[]{:S(2)}) collective-permute-start(f32[8,16,128]{2,1,0:T(8,128)S(1)} %get-tuple-element.16), channel_id=1, source_target_pairs={{1,2},{2,1},{3,4},{4,3},{5,6},{6,5},{7,8},{8,7},{9,10},{10,9},{11,... | collective-permute-start | bytes 196616 | tf_op jit(solution)/shard_map/ppermute | solution.py:33
  10.4 0.1 shard_map.105.pt
  10.5 0.0 collective-permute-done.got_even
  10.5 3.3 %collective-permute-done.1.got_odd = f32[8,16,128]{2,1,0:T(8,128)S(1)} collective-permute-done((f32[8,16,128]{2,1,0:T(8,128)S(1)}, f32[8,16,128]{2,1,0:T(8,128)S(1)}, u32[]{:S(2)}, u32[]{:S(2)}) %collective-permute-start.1) | collective-permute-done | bytes 65568 | tf_op jit(solution)/shard_map/ppermute | solution.py:33
  13.8 0.0 copy-done.2
  13.8 0.1 shard_map.106
  13.9 3.3 %collective-permute-start.2 = (f32[416,128]{1,0:T(8,128)S(1)}, f32[416,128]{1,0:T(8,128)S(1)}, u32[]{:S(2)}, u32[]{:S(2)}) collective-permute-start(f32[416,128]{1,0:T(8,128)S(1)} %get-tuple-element.18), channel_id=1, source_target_pairs={{0,32},{32,64},{64,96},{96,128},{128,160},{160,192},{192,224},{1,3... | collective-permute-start | bytes 638984 | tf_op jit(solution)/shard_map/ppermute | solution.py:41
  17.2 1.3 %collective-permute-start.3 = (f32[360,128]{1,0:T(8,128)S(1)}, f32[360,128]{1,0:T(8,128)S(1)}, u32[]{:S(2)}, u32[]{:S(2)}) collective-permute-start(f32[360,128]{1,0:T(8,128)S(1)} %get-tuple-element.19), channel_id=1, source_target_pairs={{32,0},{64,32},{96,64},{128,96},{160,128},{192,160},{224,192},{33,... | collective-permute-start | bytes 552968 | tf_op jit(solution)/shard_map/ppermute | solution.py:42
  18.5 5.0 %collective-permute-done.3.above = f32[360,128]{1,0:T(8,128)S(1)} collective-permute-done((f32[360,128]{1,0:T(8,128)S(1)}, f32[360,128]{1,0:T(8,128)S(1)}, u32[]{:S(2)}, u32[]{:S(2)}) %collective-permute-start.3) | collective-permute-done | bytes 184352 | tf_op jit(solution)/shard_map/ppermute | solution.py:42
  23.5 0.0 collective-permute-done.2.below
  23.5 0.4 shard_map.107
  23.9 0.0 copy-start.7
  23.9 0.0 copy-start.8
  23.9 12.9 %collective-permute-start.4 = (f32[16,8,128]{2,1,0:T(8,128)S(1)}, f32[16,8,128]{2,1,0:T(8,128)S(1)}, u32[]{:S(2)}, u32[]{:S(2)}) collective-permute-start(f32[16,8,128]{2,1,0:T(8,128)S(1)} %get-tuple-element.21), channel_id=1, source_target_pairs={{0,256},{256,0},{512,768},{768,512},{1,257},{257,1},{513,769},{769... | collective-permute-start | bytes 196616 | tf_op jit(solution)/shard_map/ppermute | solution.py:32
  36.8 1.9 %collective-permute-start.5 = (f32[16,8,128]{2,1,0:T(8,128)S(1)}, f32[16,8,128]{2,1,0:T(8,128)S(1)}, u32[]{:S(2)}, u32[]{:S(2)}) collective-permute-start(f32[16,8,128]{2,1,0:T(8,128)S(1)} %get-tuple-element.22), channel_id=1, source_target_pairs={{256,512},{512,256},{257,513},{513,257},{258,514},{514,258},{259,5... | collective-permute-start | bytes 196616 | tf_op jit(solution)/shard_map/ppermute | solution.py:33
  38.8 0.6 %shard_map.109.coefs = f32[10,8,128]{2,1,0:T(8,128)S(1)} custom-call(f32[2]{0:T(128)S(1)} %copy-done.7, f32[2]{0:T(128)S(1)} %copy-done.8), custom_call_target="tpu_custom_call" | custom-call | tf_op jit(solution)/shard_map/pallas_call | solution.py:53
  39.4 0.0 copy-start.4
  39.4 0.4 shard_map.108.sums
  39.8 0.0 collective-permute-done.4.got_even
  39.8 2.0 %collective-permute-done.5.got_odd = f32[16,8,128]{2,1,0:T(8,128)S(1)} collective-permute-done((f32[16,8,128]{2,1,0:T(8,128)S(1)}, f32[16,8,128]{2,1,0:T(8,128)S(1)}, u32[]{:S(2)}, u32[]{:S(2)}) %collective-permute-start.5) | collective-permute-done | bytes 65568 | tf_op jit(solution)/shard_map/ppermute | solution.py:33
  41.8 2.3 %shard_map.110 = (f32[3,8,16,128]{3,2,1,0:T(8,128)S(1)}, f32[6,16,128]{2,1,0:T(8,128)S(1)}, f32[4,16,128]{2,1,0:T(8,128)S(1)}, f32[48,128]{1,0:T(8,128)S(1)}, f32[48,128]{1,0:T(8,128)S(1)}) custom-call(f32[256,8,128]{2,1,0:T(8,128)S(1)} %get-tuple-element.20.main, f32[16,8,128]{2,1,0:T(8,128)S(1)} %collective-permute-done.4.got_even, ...), custom_call_target="tpu_custom_call" | custom-call | tf_op jit(solution)/shard_map/pallas_call | solution.py:53
  44.1 1.9 %collective-permute-start.6 = (f32[48,128]{1,0:T(8,128)S(1)}, f32[48,128]{1,0:T(8,128)S(1)}, u32[]{:S(2)}, u32[]{:S(2)}) collective-permute-start(f32[48,128]{1,0:T(8,128)S(1)} %get-tuple-element.26), channel_id=1, source_target_pairs={{0,1},{1,0},{2,3},{3,2},{4,5},{5,4},{6,7},{7,6},{8,9},{9,8},{10,11... | collective-permute-start | bytes 73736 | tf_op jit(solution)/shard_map/ppermute | solution.py:32
  46.1 4.5 %collective-permute-start.7 = (f32[48,128]{1,0:T(8,128)S(1)}, f32[48,128]{1,0:T(8,128)S(1)}, u32[]{:S(2)}, u32[]{:S(2)}) collective-permute-start(f32[48,128]{1,0:T(8,128)S(1)} %get-tuple-element.27), channel_id=1, source_target_pairs={{1,2},{2,1},{3,4},{4,3},{5,6},{6,5},{7,8},{8,7},{9,10},{10,9},{11,... | collective-permute-start | bytes 73736 | tf_op jit(solution)/shard_map/ppermute | solution.py:33
  50.6 0.7 %copy.11 = f32[3,8,16,128]{3,2,1,0:T(8,128)} copy(f32[3,8,16,128]{3,2,1,0:T(8,128)S(1)} %get-tuple-element.28) | data formatting | bytes 393216
  51.2 0.0 collective-permute-done.6.got_even
  51.2 3.9 %collective-permute-done.7.got_odd = f32[48,128]{1,0:T(8,128)S(1)} collective-permute-done((f32[48,128]{1,0:T(8,128)S(1)}, f32[48,128]{1,0:T(8,128)S(1)}, u32[]{:S(2)}, u32[]{:S(2)}) %collective-permute-start.7) | collective-permute-done | bytes 24608 | tf_op jit(solution)/shard_map/ppermute | solution.py:33
  55.1 0.9 %shard_map.111 = f32[4,8,64]{2,1,0:T(8,128)} custom-call(f32[6,16,128]{2,1,0:T(8,128)S(1)} %get-tuple-element.24.coupled, f32[4,16,128]{2,1,0:T(8,128)S(1)} %get-tuple-element.25.pscale, f32[48,128]{1,0:T(8,128)S(1)} %collective-permute-done.6.got_even, f32[48,128]{1,0:T(8,128)S(1)} %collective-permute-done.7.got_odd, f32[10,8,128]{2,1,0:T(8,128)S(1)} %shard_map.109.coefs), custom_call_target="tpu_custom_call" | custom-call | tf_op jit(solution)/shard_map/pallas_call | solution.py:53
  (11 shorter events, 0.0 us)
Async XLA Ops:
  0.6 13.2 %copy-start.1 = (f32[3,8,16,128]{3,2,1,0:T(8,128)S(1)}, f32[3,8,16,128]{3,2,1,0:T(8,128)}, u32[]{:S(2)}) copy-start(f32[3,8,16,128]{3,2,1,0:T(8,128)} %rhs.3) | copy-start | bytes 589828
  0.6 9.8 %copy-start.5 = (f32[4,8,64]{2,1,0:T(8,128)S(1)}, f32[4,8,64]{2,1,0:T(8,128)}, u32[]{:S(2)}) copy-start(f32[4,8,64]{2,1,0:T(8,128)} %pscale.1) | copy-start | bytes 24580
  0.7 9.8 %copy-start.6 = (f32[4,8,64]{2,1,0:T(8,128)S(1)}, f32[4,8,64]{2,1,0:T(8,128)}, u32[]{:S(2)}) copy-start(f32[4,8,64]{2,1,0:T(8,128)} %prhs.1) | copy-start | bytes 24580
  0.7 13.1 %copy-start.2 = (f32[8,16,128]{2,1,0:T(8,128)S(1)}, f32[8,16,128]{2,1,0:T(8,128)}, u32[]{:S(2)}) copy-start(f32[8,16,128]{2,1,0:T(8,128)} %visc.3) | copy-start | bytes 196612
  0.7 13.1 %copy-start.3 = (f32[8,16,128]{2,1,0:T(8,128)S(1)}, f32[8,16,128]{2,1,0:T(8,128)}, u32[]{:S(2)}) copy-start(f32[8,16,128]{2,1,0:T(8,128)} %mass.3) | copy-start | bytes 196612
  1.7 8.8 %collective-permute-start = (f32[8,16,128]{2,1,0:T(8,128)S(1)}, f32[8,16,128]{2,1,0:T(8,128)S(1)}, u32[]{:S(2)}, u32[]{:S(2)}) collective-permute-start(f32[8,16,128]{2,1,0:T(8,128)S(1)} %get-tuple-element.15), channel_id=1, source_target_pairs={{0,1},{1,0},{2,3},{3,2},{4,5},{5,4},{6,7},{7,6},{8,9},{9,8},{10,11... | collective-permute-start | bytes 196616 | tf_op jit(solution)/shard_map/ppermute | solution.py:32
  4.3 9.5 %collective-permute-start.1 = (f32[8,16,128]{2,1,0:T(8,128)S(1)}, f32[8,16,128]{2,1,0:T(8,128)S(1)}, u32[]{:S(2)}, u32[]{:S(2)}) collective-permute-start(f32[8,16,128]{2,1,0:T(8,128)S(1)} %get-tuple-element.16), channel_id=1, source_target_pairs={{1,2},{2,1},{3,4},{4,3},{5,6},{6,5},{7,8},{8,7},{9,10},{10,9},{11,... | collective-permute-start | bytes 196616 | tf_op jit(solution)/shard_map/ppermute | solution.py:33
  13.9 9.6 %collective-permute-start.2 = (f32[416,128]{1,0:T(8,128)S(1)}, f32[416,128]{1,0:T(8,128)S(1)}, u32[]{:S(2)}, u32[]{:S(2)}) collective-permute-start(f32[416,128]{1,0:T(8,128)S(1)} %get-tuple-element.18), channel_id=1, source_target_pairs={{0,32},{32,64},{64,96},{96,128},{128,160},{160,192},{192,224},{1,3... | collective-permute-start | bytes 638984 | tf_op jit(solution)/shard_map/ppermute | solution.py:41
  17.2 6.3 %collective-permute-start.3 = (f32[360,128]{1,0:T(8,128)S(1)}, f32[360,128]{1,0:T(8,128)S(1)}, u32[]{:S(2)}, u32[]{:S(2)}) collective-permute-start(f32[360,128]{1,0:T(8,128)S(1)} %get-tuple-element.19), channel_id=1, source_target_pairs={{32,0},{64,32},{96,64},{128,96},{160,128},{192,160},{224,192},{33,... | collective-permute-start | bytes 552968 | tf_op jit(solution)/shard_map/ppermute | solution.py:42
  23.5 15.9 %copy-start = (bf16[512,256]{1,0:T(8,128)(2,1)S(1)}, bf16[512,256]{1,0:T(8,128)(2,1)}, u32[]{:S(2)}) copy-start(bf16[512,256]{1,0:T(8,128)(2,1)} %constant.4.clone.ring) | copy-start | bytes 786436
  23.9 14.9 %copy-start.7 = (f32[2]{0:T(128)S(1)}, f32[2]{0:T(128)}, u32[]{:S(2)}) copy-start(f32[2]{0:T(128)} %vbounds.1) | copy-start | bytes 28
  23.9 14.9 %copy-start.8 = (f32[2]{0:T(128)S(1)}, f32[2]{0:T(128)}, u32[]{:S(2)}) copy-start(f32[2]{0:T(128)} %pbounds.1) | copy-start | bytes 28
  23.9 15.9 %collective-permute-start.4 = (f32[16,8,128]{2,1,0:T(8,128)S(1)}, f32[16,8,128]{2,1,0:T(8,128)S(1)}, u32[]{:S(2)}, u32[]{:S(2)}) collective-permute-start(f32[16,8,128]{2,1,0:T(8,128)S(1)} %get-tuple-element.21), channel_id=1, source_target_pairs={{0,256},{256,0},{512,768},{768,512},{1,257},{257,1},{513,769},{769... | collective-permute-start | bytes 196616 | tf_op jit(solution)/shard_map/ppermute | solution.py:32
  36.8 5.0 %collective-permute-start.5 = (f32[16,8,128]{2,1,0:T(8,128)S(1)}, f32[16,8,128]{2,1,0:T(8,128)S(1)}, u32[]{:S(2)}, u32[]{:S(2)}) collective-permute-start(f32[16,8,128]{2,1,0:T(8,128)S(1)} %get-tuple-element.22), channel_id=1, source_target_pairs={{256,512},{512,256},{257,513},{513,257},{258,514},{514,258},{259,5... | collective-permute-start | bytes 196616 | tf_op jit(solution)/shard_map/ppermute | solution.py:33
  39.4 2.5 %copy-start.4 = (bf16[512,128]{1,0:T(8,128)(2,1)S(1)}, bf16[512,128]{1,0:T(8,128)(2,1)}, u32[]{:S(2)}) copy-start(bf16[512,128]{1,0:T(8,128)(2,1)} %constant.5.clone.table) | copy-start | bytes 393220
  44.1 7.1 %collective-permute-start.6 = (f32[48,128]{1,0:T(8,128)S(1)}, f32[48,128]{1,0:T(8,128)S(1)}, u32[]{:S(2)}, u32[]{:S(2)}) collective-permute-start(f32[48,128]{1,0:T(8,128)S(1)} %get-tuple-element.26), channel_id=1, source_target_pairs={{0,1},{1,0},{2,3},{3,2},{4,5},{5,4},{6,7},{7,6},{8,9},{9,8},{10,11... | collective-permute-start | bytes 73736 | tf_op jit(solution)/shard_map/ppermute | solution.py:32
  46.1 9.1 %collective-permute-start.7 = (f32[48,128]{1,0:T(8,128)S(1)}, f32[48,128]{1,0:T(8,128)S(1)}, u32[]{:S(2)}, u32[]{:S(2)}) collective-permute-start(f32[48,128]{1,0:T(8,128)S(1)} %get-tuple-element.27), channel_id=1, source_target_pairs={{1,2},{2,1},{3,4},{4,3},{5,6},{6,5},{7,8},{8,7},{9,10},{10,9},{11,... | collective-permute-start | bytes 73736 | tf_op jit(solution)/shard_map/ppermute | solution.py:33

commit v10 on v9

--- a/solution.py
+++ b/solution.py
@@ -32,15 +32,6 @@
     inner = lax.ppermute(first, axis, even)
     outer = lax.ppermute(second, axis, odd)
     return inner, outer
-
-
-def both_neighbours(axis, to_above, to_below):
-    size = lax.axis_size(axis)
-    up = [(i, i + 1) for i in range(size - 1)]
-    down = [(i + 1, i) for i in range(size - 1)]
-    from_below = lax.ppermute(to_above, axis, up)
-    from_above = lax.ppermute(to_below, axis, down)
-    return from_below, from_above
 
 
 def call(body, outs, scratch=(), smem=(), hbm=(), vmem=()):
@@ -113,8 +104,7 @@
 DOWN_ROWS = sum(r[2] for r in y_rows())
 
 
-def padded(rows):
-    return -(-rows // 8) * 8
+Y_ROWS = -(-(max(UP_ROWS, DOWN_ROWS) + 8) // 8) * 8
 
 
 def pack_nodes(pscale, prhs, pt):
@@ -122,7 +112,7 @@
         pt[k] = jnp.concatenate([pscale[k], prhs[k]], axis=1)
 
 
-def pack_y(rhs, visc, mass, got_even, got_odd, pt, own, up, down):
+def pack_y(rhs, visc, mass, got_even, got_odd, pt, own, msg_even, msg_odd, up, down):
     for z in range(Z):
         for c in range(3):
             own[c * ZW + 2 + z] = rhs[c, z]
@@ -135,6 +125,9 @@
         own[S0 + deep] = jnp.ones((Y, X), F32)
         own[S0 + near] = z_halo(got_even, got_odd, 6)[side]
         own[M0 + near - 1] = z_halo(got_even, got_odd, 7)[side]
+    up[Y_ROWS - 8 :] = jnp.zeros((8, X), F32)
+    unused = DOWN_ROWS // 8 * 8
+    down[unused:] = jnp.zeros((Y_ROWS - unused, X), F32)
     row = lax.broadcasted_iota(jnp.int32, (8, X), 0)
     at_up = at_down = 0
     for p, n_up, n_down in y_rows():
@@ -150,9 +143,21 @@
     for k in range(PZ):
         up[at_up + 2 * k : at_up + 2 * k + 2] = pt[k, 6:]
         down[at_down + 2 * k : at_down + 2 * k + 2] = pt[k, :2]
-
-
-def pack_x(own, pt, below, above, main, msg_even, msg_odd):
+    even = parity("gy") == 0
+    for i in range(0, Y_ROWS, 8):
+        tile = slice(i, i + 8)
+        a, b = up[tile], down[tile]
+        msg_even[tile] = jnp.where(even, a, b)
+        msg_odd[tile] = jnp.where(even, b, a)
+
+
+def pack_x(own, pt, got_even, got_odd, main, msg_even, msg_odd, below, above):
+    even = parity("gy") == 0
+    for i in range(0, Y_ROWS, 8):
+        tile = slice(i, i + 8)
+        a, b = got_even[tile], got_odd[tile]
+        below[tile] = jnp.where(even, b, a)
+        above[tile] = jnp.where(even, a, b)
     at_up = at_down = 0
     rows = {r[0]: r[1:] for r in y_rows()}
     for p in range(PLANES):
@@ -452,13 +457,15 @@
     z_halos = swap_neighbours("gz", msg_even, msg_odd)
     (coefs,) = call(scalars, [(10, *tile)], smem=(0, 1))(vbounds, pbounds)
     (pt,) = call(pack_nodes, [(PZ, *tile)])(pscale, prhs)
-    own, up, down = call(
-        pack_y, [(PLANES, *plane), (padded(UP_ROWS + 8), X), (padded(DOWN_ROWS + 8), X)]
+    y_message = (Y_ROWS, X)
+    two = [pltpu.VMEM(y_message, F32)] * 2
+    own, msg_even, msg_odd = call(
+        pack_y, [(PLANES, *plane), y_message, y_message], scratch=two
     )(rhs, visc, mass, *z_halos, pt)
-    below, above = both_neighbours("gy", up, down)
-    main, msg_even, msg_odd = call(pack_x, [(TILES, *tile), (PACKED, *tile), (PACKED, *tile)])(
-        own, pt, below, above
-    )
+    y_halos = swap_neighbours("gy", msg_even, msg_odd)
+    main, msg_even, msg_odd = call(
+        pack_x, [(TILES, *tile), (PACKED, *tile), (PACKED, *tile)], scratch=two
+    )(own, pt, *y_halos)
     below, above = swap_neighbours("gx", msg_even, msg_odd)
     ring = jnp.asarray(smoothing())
     rows = 3 * (Z + 2) * 32

time: 56.4 us -> 57.4 us (1.018)
  the two profiles are of different devices: /device:TPU:3 before, /device:TPU:19 now
where the time goes in v10:
time: 57.4 us; the launch traced here: 57 us
  starting transfers between devices  37.6 us (66%)
  waiting for transfers between devices  12.1 us (21%)
  Pallas kernels  5.81 us (10%)
  between operations  0.86 us (1%)
  local copies, waits for them, and re-layouts  0.72 us (1%)
    ppermute x4, starting transfers between devices, swap_neighbours(): inner = lax.ppermute(first, axis, even)  20.1 us
    ppermute x4, starting transfers between devices, swap_neighbours(): outer = lax.ppermute(second, axis, odd)  17.5 us
    ppermute x4, waiting for transfers between devices, swap_neighbours(): outer = lax.ppermute(second, axis, odd)  12.1 us
    pallas_call x8, Pallas kernels, run(): pl.pallas_call(body, in_specs=[pl.BlockSpec(memory_space=space.get(i, plt...  5.81 us
  transfers between devices with their start and end apart: 8, of which 4 were waited for; matrix products, arithmetic and copies ran while one was open for 1% of the time, Pallas kernels for 2%

profile of v10, /device:TPU:19, one launch (start us, length us, event | category | flops | bytes accessed | tf_op | source)
XLA Modules:
  0.0 57.0 jit_solution(12093434458690631748)
XLA Ops:
  0.6 0.0 copy-start.1
  0.6 0.0 copy-start.5
  0.7 0.0 copy-start.6
  0.7 0.0 copy-start.2
  0.7 1.0 %shard_map.104 = (f32[8,16,128]{2,1,0:T(8,128)S(1)}, f32[8,16,128]{2,1,0:T(8,128)S(1)}) custom-call(f32[3,8,16,128]{3,2,1,0:T(8,128)} %rhs.3, f32[8,16,128]{2,1,0:T(8,128)} %visc.3, f32[8,16,128]{2,1,0:T(8,128)} %mass.3), custom_call_target="tpu_custom_call" | custom-call | tf_op jit(solution)/shard_map/pallas_call | solution.py:44
  1.7 2.6 %collective-permute-start = (f32[8,16,128]{2,1,0:T(8,128)S(1)}, f32[8,16,128]{2,1,0:T(8,128)S(1)}, u32[]{:S(2)}, u32[]{:S(2)}) collective-permute-start(f32[8,16,128]{2,1,0:T(8,128)S(1)} %get-tuple-element.15), channel_id=1, source_target_pairs={{0,1},{1,0},{2,3},{3,2},{4,5},{5,4},{6,7},{7,6},{8,9},{9,8},{10,11... | collective-permute-start | bytes 196616 | tf_op jit(solution)/shard_map/ppermute | solution.py:32
  4.3 6.1 %collective-permute-start.1 = (f32[8,16,128]{2,1,0:T(8,128)S(1)}, f32[8,16,128]{2,1,0:T(8,128)S(1)}, u32[]{:S(2)}, u32[]{:S(2)}) collective-permute-start(f32[8,16,128]{2,1,0:T(8,128)S(1)} %get-tuple-element.16), channel_id=1, source_target_pairs={{1,2},{2,1},{3,4},{4,3},{5,6},{6,5},{7,8},{8,7},{9,10},{10,9},{11,... | collective-permute-start | bytes 196616 | tf_op jit(solution)/shard_map/ppermute | solution.py:33
  10.4 0.1 shard_map.105.pt
  10.5 0.0 collective-permute-done.got_even
  10.5 3.3 %collective-permute-done.1.got_odd = f32[8,16,128]{2,1,0:T(8,128)S(1)} collective-permute-done((f32[8,16,128]{2,1,0:T(8,128)S(1)}, f32[8,16,128]{2,1,0:T(8,128)S(1)}, u32[]{:S(2)}, u32[]{:S(2)}) %collective-permute-start.1) | collective-permute-done | bytes 65568 | tf_op jit(solution)/shard_map/ppermute | solution.py:33
  13.8 0.1 shard_map.106
  13.9 2.0 %collective-permute-start.2 = (f32[416,128]{1,0:T(8,128)S(1)}, f32[416,128]{1,0:T(8,128)S(1)}, u32[]{:S(2)}, u32[]{:S(2)}) collective-permute-start(f32[416,128]{1,0:T(8,128)S(1)} %get-tuple-element.18), channel_id=1, source_target_pairs={{0,32},{32,0},{64,96},{96,64},{128,160},{160,128},{192,224},{224,1... | collective-permute-start | bytes 638984 | tf_op jit(solution)/shard_map/ppermute | solution.py:32
  15.9 4.7 %collective-permute-start.3 = (f32[416,128]{1,0:T(8,128)S(1)}, f32[416,128]{1,0:T(8,128)S(1)}, u32[]{:S(2)}, u32[]{:S(2)}) collective-permute-start(f32[416,128]{1,0:T(8,128)S(1)} %get-tuple-element.19), channel_id=1, source_target_pairs={{32,64},{64,32},{96,128},{128,96},{160,192},{192,160},{33,65},{65,... | collective-permute-start | bytes 638984 | tf_op jit(solution)/shard_map/ppermute | solution.py:33
  20.6 0.0 collective-permute-done.2.got_even
  20.6 3.2 %collective-permute-done.3.got_odd = f32[416,128]{1,0:T(8,128)S(1)} collective-permute-done((f32[416,128]{1,0:T(8,128)S(1)}, f32[416,128]{1,0:T(8,128)S(1)}, u32[]{:S(2)}, u32[]{:S(2)}) %collective-permute-start.3) | collective-permute-done | bytes 213024 | tf_op jit(solution)/shard_map/ppermute | solution.py:33
  23.8 0.4 shard_map.107
  24.2 0.0 copy-start.7
  24.2 0.0 copy-start.8
  24.3 13.6 %collective-permute-start.4 = (f32[16,8,128]{2,1,0:T(8,128)S(1)}, f32[16,8,128]{2,1,0:T(8,128)S(1)}, u32[]{:S(2)}, u32[]{:S(2)}) collective-permute-start(f32[16,8,128]{2,1,0:T(8,128)S(1)} %get-tuple-element.21), channel_id=1, source_target_pairs={{0,256},{256,0},{512,768},{768,512},{1,257},{257,1},{513,769},{769... | collective-permute-start | bytes 196616 | tf_op jit(solution)/shard_map/ppermute | solution.py:32
  37.9 1.9 %collective-permute-start.5 = (f32[16,8,128]{2,1,0:T(8,128)S(1)}, f32[16,8,128]{2,1,0:T(8,128)S(1)}, u32[]{:S(2)}, u32[]{:S(2)}) collective-permute-start(f32[16,8,128]{2,1,0:T(8,128)S(1)} %get-tuple-element.22), channel_id=1, source_target_pairs={{256,512},{512,256},{257,513},{513,257},{258,514},{514,258},{259,5... | collective-permute-start | bytes 196616 | tf_op jit(solution)/shard_map/ppermute | solution.py:33
  39.8 0.6 shard_map.109.coefs
  40.4 0.0 copy-start.4
  40.4 0.4 shard_map.108.sums
  40.9 0.0 collective-permute-done.4.got_even
  40.9 2.0 %collective-permute-done.5.got_odd = f32[16,8,128]{2,1,0:T(8,128)S(1)} collective-permute-done((f32[16,8,128]{2,1,0:T(8,128)S(1)}, f32[16,8,128]{2,1,0:T(8,128)S(1)}, u32[]{:S(2)}, u32[]{:S(2)}) %collective-permute-start.5) | collective-permute-done | bytes 65568 | tf_op jit(solution)/shard_map/ppermute | solution.py:33
  42.9 2.3 %shard_map.110 = (f32[3,8,16,128]{3,2,1,0:T(8,128)S(1)}, f32[6,16,128]{2,1,0:T(8,128)S(1)}, f32[4,16,128]{2,1,0:T(8,128)S(1)}, f32[48,128]{1,0:T(8,128)S(1)}, f32[48,128]{1,0:T(8,128)S(1)}) custom-call(f32[256,8,128]{2,1,0:T(8,128)S(1)} %get-tuple-element.20.main, f32[16,8,128]{2,1,0:T(8,128)S(1)} %collective-permute-done.4.got_even, ...), custom_call_target="tpu_custom_call" | custom-call | tf_op jit(solution)/shard_map/pallas_call | solution.py:44
  45.2 1.9 %collective-permute-start.6 = (f32[48,128]{1,0:T(8,128)S(1)}, f32[48,128]{1,0:T(8,128)S(1)}, u32[]{:S(2)}, u32[]{:S(2)}) collective-permute-start(f32[48,128]{1,0:T(8,128)S(1)} %get-tuple-element.26), channel_id=1, source_target_pairs={{0,1},{1,0},{2,3},{3,2},{4,5},{5,4},{6,7},{7,6},{8,9},{9,8},{10,11... | collective-permute-start | bytes 73736 | tf_op jit(solution)/shard_map/ppermute | solution.py:32
  47.1 4.8 %collective-permute-start.7 = (f32[48,128]{1,0:T(8,128)S(1)}, f32[48,128]{1,0:T(8,128)S(1)}, u32[]{:S(2)}, u32[]{:S(2)}) collective-permute-start(f32[48,128]{1,0:T(8,128)S(1)} %get-tuple-element.27), channel_id=1, source_target_pairs={{1,2},{2,1},{3,4},{4,3},{5,6},{6,5},{7,8},{8,7},{9,10},{10,9},{11,... | collective-permute-start | bytes 73736 | tf_op jit(solution)/shard_map/ppermute | solution.py:33
  51.9 0.7 %copy.11 = f32[3,8,16,128]{3,2,1,0:T(8,128)} copy(f32[3,8,16,128]{3,2,1,0:T(8,128)S(1)} %get-tuple-element.28) | data formatting | bytes 393216
  52.6 0.0 collective-permute-done.6.got_even
  52.6 3.6 %collective-permute-done.7.got_odd = f32[48,128]{1,0:T(8,128)S(1)} collective-permute-done((f32[48,128]{1,0:T(8,128)S(1)}, f32[48,128]{1,0:T(8,128)S(1)}, u32[]{:S(2)}, u32[]{:S(2)}) %collective-permute-start.7) | collective-permute-done | bytes 24608 | tf_op jit(solution)/shard_map/ppermute | solution.py:33
  56.1 0.9 %shard_map.111 = f32[4,8,64]{2,1,0:T(8,128)} custom-call(f32[6,16,128]{2,1,0:T(8,128)S(1)} %get-tuple-element.24.coupled, f32[4,16,128]{2,1,0:T(8,128)S(1)} %get-tuple-element.25.pscale, f32[48,128]{1,0:T(8,128)S(1)} %collective-permute-done.6.got_even, f32[48,128]{1,0:T(8,128)S(1)} %collective-permute-done.7.got_odd, f32[10,8,128]{2,1,0:T(8,128)S(1)} %shard_map.109.coefs), custom_call_target="tpu_custom_call" | custom-call | tf_op jit(solution)/shard_map/pallas_call | solution.py:44
  (11 shorter events, 0.0 us)
Async XLA Ops:
  0.6 13.2 %copy-start.1 = (f32[3,8,16,128]{3,2,1,0:T(8,128)S(1)}, f32[3,8,16,128]{3,2,1,0:T(8,128)}, u32[]{:S(2)}) copy-start(f32[3,8,16,128]{3,2,1,0:T(8,128)} %rhs.3) | copy-start | bytes 589828
  0.6 9.8 %copy-start.5 = (f32[4,8,64]{2,1,0:T(8,128)S(1)}, f32[4,8,64]{2,1,0:T(8,128)}, u32[]{:S(2)}) copy-start(f32[4,8,64]{2,1,0:T(8,128)} %pscale.1) | copy-start | bytes 24580
  0.7 9.8 %copy-start.6 = (f32[4,8,64]{2,1,0:T(8,128)S(1)}, f32[4,8,64]{2,1,0:T(8,128)}, u32[]{:S(2)}) copy-start(f32[4,8,64]{2,1,0:T(8,128)} %prhs.1) | copy-start | bytes 24580
  0.7 13.1 %copy-start.2 = (f32[8,16,128]{2,1,0:T(8,128)S(1)}, f32[8,16,128]{2,1,0:T(8,128)}, u32[]{:S(2)}) copy-start(f32[8,16,128]{2,1,0:T(8,128)} %visc.3) | copy-start | bytes 196612
  0.7 13.1 %copy-start.3 = (f32[8,16,128]{2,1,0:T(8,128)S(1)}, f32[8,16,128]{2,1,0:T(8,128)}, u32[]{:S(2)}) copy-start(f32[8,16,128]{2,1,0:T(8,128)} %mass.3) | copy-start | bytes 196612
  1.7 8.8 %collective-permute-start = (f32[8,16,128]{2,1,0:T(8,128)S(1)}, f32[8,16,128]{2,1,0:T(8,128)S(1)}, u32[]{:S(2)}, u32[]{:S(2)}) collective-permute-start(f32[8,16,128]{2,1,0:T(8,128)S(1)} %get-tuple-element.15), channel_id=1, source_target_pairs={{0,1},{1,0},{2,3},{3,2},{4,5},{5,4},{6,7},{7,6},{8,9},{9,8},{10,11... | collective-permute-start | bytes 196616 | tf_op jit(solution)/shard_map/ppermute | solution.py:32
  4.3 9.5 %collective-permute-start.1 = (f32[8,16,128]{2,1,0:T(8,128)S(1)}, f32[8,16,128]{2,1,0:T(8,128)S(1)}, u32[]{:S(2)}, u32[]{:S(2)}) collective-permute-start(f32[8,16,128]{2,1,0:T(8,128)S(1)} %get-tuple-element.16), channel_id=1, source_target_pairs={{1,2},{2,1},{3,4},{4,3},{5,6},{6,5},{7,8},{8,7},{9,10},{10,9},{11,... | collective-permute-start | bytes 196616 | tf_op jit(solution)/shard_map/ppermute | solution.py:33
  13.9 6.7 %collective-permute-start.2 = (f32[416,128]{1,0:T(8,128)S(1)}, f32[416,128]{1,0:T(8,128)S(1)}, u32[]{:S(2)}, u32[]{:S(2)}) collective-permute-start(f32[416,128]{1,0:T(8,128)S(1)} %get-tuple-element.18), channel_id=1, source_target_pairs={{0,32},{32,0},{64,96},{96,64},{128,160},{160,128},{192,224},{224,1... | collective-permute-start | bytes 638984 | tf_op jit(solution)/shard_map/ppermute | solution.py:32
  15.9 7.9 %collective-permute-start.3 = (f32[416,128]{1,0:T(8,128)S(1)}, f32[416,128]{1,0:T(8,128)S(1)}, u32[]{:S(2)}, u32[]{:S(2)}) collective-permute-start(f32[416,128]{1,0:T(8,128)S(1)} %get-tuple-element.19), channel_id=1, source_target_pairs={{32,64},{64,32},{96,128},{128,96},{160,192},{192,160},{33,65},{65,... | collective-permute-start | bytes 638984 | tf_op jit(solution)/shard_map/ppermute | solution.py:33
  23.8 16.6 %copy-start = (bf16[512,256]{1,0:T(8,128)(2,1)S(1)}, bf16[512,256]{1,0:T(8,128)(2,1)}, u32[]{:S(2)}) copy-start(bf16[512,256]{1,0:T(8,128)(2,1)} %constant.4.clone.ring) | copy-start | bytes 786436
  24.2 15.6 %copy-start.7 = (f32[2]{0:T(128)S(1)}, f32[2]{0:T(128)}, u32[]{:S(2)}) copy-start(f32[2]{0:T(128)} %vbounds.1) | copy-start | bytes 28
  24.2 15.6 %copy-start.8 = (f32[2]{0:T(128)S(1)}, f32[2]{0:T(128)}, u32[]{:S(2)}) copy-start(f32[2]{0:T(128)} %pbounds.1) | copy-start | bytes 28
  24.3 16.6 %collective-permute-start.4 = (f32[16,8,128]{2,1,0:T(8,128)S(1)}, f32[16,8,128]{2,1,0:T(8,128)S(1)}, u32[]{:S(2)}, u32[]{:S(2)}) collective-permute-start(f32[16,8,128]{2,1,0:T(8,128)S(1)} %get-tuple-element.21), channel_id=1, source_target_pairs={{0,256},{256,0},{512,768},{768,512},{1,257},{257,1},{513,769},{769... | collective-permute-start | bytes 196616 | tf_op jit(solution)/shard_map/ppermute | solution.py:32
  37.9 5.0 %collective-permute-start.5 = (f32[16,8,128]{2,1,0:T(8,128)S(1)}, f32[16,8,128]{2,1,0:T(8,128)S(1)}, u32[]{:S(2)}, u32[]{:S(2)}) collective-permute-start(f32[16,8,128]{2,1,0:T(8,128)S(1)} %get-tuple-element.22), channel_id=1, source_target_pairs={{256,512},{512,256},{257,513},{513,257},{258,514},{514,258},{259,5... | collective-permute-start | bytes 196616 | tf_op jit(solution)/shard_map/ppermute | solution.py:33
  40.4 2.5 %copy-start.4 = (bf16[512,128]{1,0:T(8,128)(2,1)S(1)}, bf16[512,128]{1,0:T(8,128)(2,1)}, u32[]{:S(2)}) copy-start(bf16[512,128]{1,0:T(8,128)(2,1)} %constant.5.clone.table) | copy-start | bytes 393220
  45.2 7.4 %collective-permute-start.6 = (f32[48,128]{1,0:T(8,128)S(1)}, f32[48,128]{1,0:T(8,128)S(1)}, u32[]{:S(2)}, u32[]{:S(2)}) collective-permute-start(f32[48,128]{1,0:T(8,128)S(1)} %get-tuple-element.26), channel_id=1, source_target_pairs={{0,1},{1,0},{2,3},{3,2},{4,5},{5,4},{6,7},{7,6},{8,9},{9,8},{10,11... | collective-permute-start | bytes 73736 | tf_op jit(solution)/shard_map/ppermute | solution.py:32
  47.1 9.1 %collective-permute-start.7 = (f32[48,128]{1,0:T(8,128)S(1)}, f32[48,128]{1,0:T(8,128)S(1)}, u32[]{:S(2)}, u32[]{:S(2)}) collective-permute-start(f32[48,128]{1,0:T(8,128)S(1)} %get-tuple-element.27), channel_id=1, source_target_pairs={{1,2},{2,1},{3,4},{4,3},{5,6},{6,5},{7,8},{8,7},{9,10},{10,9},{11,... | collective-permute-start | bytes 73736 | tf_op jit(solution)/shard_map/ppermute | solution.py:33
